TPU v7x, 8 devices: a whole 2x2x1 slice. The times are simulated.
8 devices in a mesh: dp: 1 (over z), tp: 8 (over y, x, core).
Axes of the slice: x: 2, y: 2, z: 1, core: 2. Of those that a mesh axis runs over, the one named last changes fastest.
Arguments:
- x_in: bfloat16 [4096, 2048], P(('dp', 'tp'))
- dy_in: bfloat16 [4096, 2048], P(('dp', 'tp'))
- w_q: bfloat16 [2048, 8, 256], P(None, 'tp')
- w_k: bfloat16 [2048, 1, 256], replicated
- w_v: bfloat16 [2048, 1, 256], replicated
- w_o: bfloat16 [8, 256, 2048], P('tp')
Outputs:
- output 1: bfloat16 [4096, 2048], P(('dp', 'tp'))
- output 2: float32 [2048, 8, 256], P('dp', 'tp')
- output 3: float32 [8, 256, 2048], P(('dp', 'tp'))
- output 4: float32 [2048, 256], P(('dp', 'tp'))
- output 5: float32 [2048, 256], P(('dp', 'tp'))
All inputs are finite; a program needn't handle non-finite values.
Results may differ from a plain program's by a relative error of at most 0.0101447.
Values are sent between devices in bfloat16 or wider.
A program may use at most 1 GiB of HBM per device.

v0:
```python
import jax
import jax.numpy as jnp
from jax import lax
from jax.sharding import PartitionSpec as P


def solution(mesh):
    n_model = mesh.shape["tp"]

    def local_grads(x_blk, dy_blk, wq_loc, w_k, w_v, wo_loc):
        f32 = jnp.float32
        bf16 = jnp.bfloat16
        model_dim, kv_heads, head_dim = w_k.shape
        repl = n_model // kv_heads
        scale = head_dim ** -0.5
        dev_idx = lax.axis_index("tp")
        kv_index = dev_idx // repl
        wk_loc = lax.dynamic_index_in_dim(w_k, kv_index, axis=1, keepdims=False)
        wv_loc = lax.dynamic_index_in_dim(w_v, kv_index, axis=1, keepdims=False)
        x_full = lax.all_gather(x_blk, "tp", axis=0, tiled=True)
        dy_full = lax.all_gather(dy_blk, "tp", axis=0, tiled=True)
        tokens = x_full.shape[0]
        queries = jnp.einsum("tc,che->hte", x_full, wq_loc, preferred_element_type=f32).astype(bf16)
        key_rows = jnp.dot(x_full, wk_loc, preferred_element_type=f32).astype(bf16)
        val_rows = jnp.dot(x_full, wv_loc, preferred_element_type=f32).astype(bf16)
        causal = lax.broadcasted_iota(jnp.int32, (tokens, tokens), 0) >= lax.broadcasted_iota(jnp.int32, (tokens, tokens), 1)
        scores = jnp.einsum("hqe,ke->hqk", queries, key_rows, preferred_element_type=f32) * scale
        scores = jnp.where(causal, scores, -jnp.inf)
        attn_prob = jax.nn.softmax(scores, axis=-1)
        prob_bf = attn_prob.astype(bf16)
        attn_out = jnp.einsum("hqk,ke->hqe", prob_bf, val_rows, preferred_element_type=f32).astype(bf16)
        d_out = jnp.einsum("tc,hec->hte", dy_full, wo_loc, preferred_element_type=f32).astype(bf16)
        grad_wo = jnp.einsum("hte,tc->hec", attn_out, dy_full, preferred_element_type=f32)
        d_prob = jnp.einsum("hqe,ke->hqk", d_out, val_rows, preferred_element_type=f32)
        delta_row = jnp.einsum("hqe,hqe->hq", d_out, attn_out, preferred_element_type=f32)[..., None]
        d_score = (attn_prob * (d_prob - delta_row)).astype(bf16)
        d_query = (jnp.einsum("hqk,ke->hqe", d_score, key_rows, preferred_element_type=f32) * scale).astype(bf16)
        d_key = (jnp.einsum("hqk,hqe->ke", d_score, queries, preferred_element_type=f32) * scale).astype(bf16)
        d_val = jnp.einsum("hqk,hqe->ke", prob_bf, d_out, preferred_element_type=f32).astype(bf16)
        grad_wq = jnp.einsum("tc,hte->che", x_full, d_query, preferred_element_type=f32)
        dx_part = (jnp.einsum("hte,che->tc", d_query, wq_loc, preferred_element_type=f32)
                   + jnp.einsum("te,ce->tc", d_key, wk_loc, preferred_element_type=f32)
                   + jnp.einsum("te,ce->tc", d_val, wv_loc, preferred_element_type=f32))
        dx_blk = lax.psum_scatter(dx_part, "tp", scatter_dimension=0, tiled=True).astype(bf16)
        slot = (jnp.arange(kv_heads) == kv_index)[:, None, None]
        wk_part = jnp.einsum("tc,te->ce", x_full, d_key, preferred_element_type=f32)
        wv_part = jnp.einsum("tc,te->ce", x_full, d_val, preferred_element_type=f32)
        wk_buf = jnp.where(slot, wk_part[None], 0.0).reshape(kv_heads * model_dim, head_dim)
        wv_buf = jnp.where(slot, wv_part[None], 0.0).reshape(kv_heads * model_dim, head_dim)
        dwk_blk = lax.psum_scatter(wk_buf, "tp", scatter_dimension=0, tiled=True)
        dwv_blk = lax.psum_scatter(wv_buf, "tp", scatter_dimension=0, tiled=True)
        return dx_blk, grad_wq, grad_wo, dwk_blk, dwv_blk

    tok_spec = P(("dp", "tp"))
    return jax.shard_map(
        local_grads,
        mesh=mesh,
        in_specs=(tok_spec, tok_spec, P(None, "tp", None), P(), P(), P("tp")),
        out_specs=(tok_spec, P("dp", "tp", None), tok_spec, tok_spec, tok_spec),
        check_vma=False,
    )
```

profile of v0, /device:TPU:0, one launch (start us, length us, event | category | flops | bytes accessed | tf_op | source)
XLA Modules:
  0.0 695.9 jit_solution(2332290099659745011)
XLA Ops:
  8.7 88.0 %all-gather.5.cloned.1.call-done = bf16[4096,2048]{1,0:T(8,128)(2,1)} async-done(((bf16[512,2048]{1,0:T(8,128)(2,1)}), bf16[4096,2048]{1,0:T(8,128)(2,1)}) %all-gather.5.cloned.1.call-update) | async-done | bytes 16777232 | tf_op jit(solution)/shard_map/all_gather | solution.py:21
  96.7 10.6 %fusion.10 = bf16[4096,256]{0,1:T(8,128)(2,1)S(1)} fusion(bf16[4096,2048]{1,0:T(8,128)(2,1)} %all-gather.5.cloned.1.call-done, bf16[1,256,2048]{2,1,0:T(8,128)(2,1)} %param.11), kind=kOutput, calls=%fused_computation.18 | convolution fusion | flops 4296015872 | bytes 19922944 | tf_op jit(solution)/shard_map/tc,hec->hte/dot_general | solution.py:32
  110.3 72.3 %all-gather.3.cloned.1.call-done = bf16[4096,2048]{1,0:T(8,128)(2,1)} async-done(((bf16[512,2048]{1,0:T(8,128)(2,1)}), bf16[4096,2048]{1,0:T(8,128)(2,1)}) %all-gather.3.cloned.1.call-update) | async-done | bytes 16777232 | tf_op jit(solution)/shard_map/all_gather | solution.py:20
  182.7 9.6 %convolution_convert_fusion = bf16[4096,256]{1,0:T(8,128)(2,1)} fusion(bf16[4096,2048]{1,0:T(8,128)(2,1)} %all-gather.3.cloned.1.call-done, bf16[2048,1,256]{2,0,1:T(8,128)(2,1)S(1)} %copy-done), kind=kOutput, calls=%fused_computation.14 | convolution fusion | flops 4296015872 | bytes 19922944 | tf_op jit(solution)/shard_map/dot_general | solution.py:24
  192.3 12.0 %fusion.9 = bf16[4096,256]{0,1:T(8,128)(2,1)} fusion(bf16[4096,2048]{1,0:T(8,128)(2,1)} %all-gather.3.cloned.1.call-done, bf16[2048,1,256]{2,0,1:T(8,128)(2,1)} %param.8), kind=kOutput, calls=%fused_computation.17 | convolution fusion | flops 4296015872 | bytes 19922944 | tf_op jit(solution)/shard_map/tc,che->hte/dot_general | solution.py:23
  204.3 28.5 %fusion.26 = (f32[4096]{0:T(1024)S(1)}, f32[4096,4096]{1,0:T(8,128)}) fusion(bf16[4096,256]{0,1:T(8,128)(2,1)} %fusion.9, bf16[4096,256]{1,0:T(8,128)(2,1)} %convolution_convert_fusion), kind=kOutput, calls=%fused_computation.38 | convolution fusion | flops 8657039360 | bytes 71319552 | tf_op jit(solution)/shard_map/hqe,ke->hqk/dot_general | solution.py:27
  232.8 21.1 %fusion.1 = f32[4096]{0:T(1024)S(1)} fusion(f32[4096,4096]{1,0:T(8,128)} %get-tuple-element.11, f32[4096]{0:T(1024)S(1)} %get-tuple-element.10), kind=kLoop, calls=%fused_computation.5 | loop fusion | flops 33550336 | bytes 67141632 | tf_op jit(solution)/shard_map/reduce_sum | solution.py:29
  253.9 24.5 %fusion.6 = bf16[4096,256]{1,0:T(8,128)(2,1)} fusion(bf16[4096,256]{0,1:T(8,128)(2,1)S(1)} %fusion.10, f32[4096,4096]{1,0:T(8,128)} %get-tuple-element.11, f32[4096]{0:T(1024)S(1)} %fusion.1, f32[4096]{0:T(1024)S(1)} %get-tuple-element.10), kind=kOutput, calls=%fused_computation.13 | convolution fusion | flops 8641314816 | bytes 71335936 | tf_op jit(solution)/shard_map/hqk,hqe->ke/dot_general | solution.py:39
  278.4 10.1 %fusion.15 = f32[4096,256]{1,0:T(8,128)} fusion(bf16[4096,2048]{1,0:T(8,128)(2,1)} %all-gather.3.cloned.1.call-done, bf16[2048,1,256]{2,0,1:T(8,128)(2,1)S(1)} %copy-done.3), kind=kOutput, calls=%fused_computation.28 | convolution fusion | flops 4294967296 | bytes 22020096 | tf_op jit(solution)/shard_map/dot_general | solution.py:25
  288.5 35.4 %online-softmax = f32[4096,256]{1,0:T(8,128)} custom-call(f32[4096,4096]{1,0:T(8,128)} %get-tuple-element.11, f32[4096,256]{1,0:T(8,128)} %fusion.15), custom_call_target="tpu_custom_call" | custom-call | tf_op online-softmax
  323.9 4.2 multiply_reduce_fusion
  328.5 41.0 %multiply_convert_fusion = bf16[4096,4096]{1,0:T(8,128)(2,1)} fusion(f32[4096]{0:T(1024)S(1)} %multiply_reduce_fusion, bf16[4096,256]{0,1:T(8,128)(2,1)S(1)} %fusion.10, f32[4096,256]{1,0:T(8,128)S(1)} %copy-done.2, f32[4096]{0:T(1024)S(1)} %fusion.1, f32[4096,4096]{1,0:T(8,128)} %get-tuple-element.11, f32[4096]{0:T(1024)S(1)} %get-tuple-element.10), kind=kOutput, calls=%fused_computation | convolution fusion | flops 8674869248 | bytes 107003904 | tf_op jit(solution)/shard_map/hqe,ke->hqk/dot_general | solution.py:34
  369.5 17.5 %fusion.5 = bf16[4096,256]{1,0:T(8,128)(2,1)} fusion(bf16[4096,4096]{1,0:T(8,128)(2,1)} %multiply_convert_fusion, bf16[4096,256]{0,1:T(8,128)(2,1)S(1)} %copy-done.5), kind=kOutput, calls=%fused_computation.12 | convolution fusion | flops 8592031744 | bytes 37748736 | tf_op jit(solution)/shard_map/hqk,hqe->ke/dot_general | solution.py:38
  387.0 15.6 %fusion.4 = bf16[4096,256]{1,0:T(8,128)(2,1)S(1)} fusion(bf16[4096,4096]{1,0:T(8,128)(2,1)} %multiply_convert_fusion, bf16[4096,256]{1,0:T(8,128)(2,1)S(1)} %copy-done.6), kind=kOutput, calls=%fused_computation.11 | convolution fusion | flops 8592031744 | bytes 37748736 | tf_op jit(solution)/shard_map/hqk,ke->hqe/dot_general | solution.py:37
  402.7 9.8 %fusion.11 = f32[2048,256]{0,1:T(8,128)} fusion(bf16[4096,256]{1,0:T(8,128)(2,1)S(1)} %copy-done.1, bf16[4096,2048]{1,0:T(8,128)(2,1)} %all-gather.3.cloned.1.call-done, pred[]{:T(512)S(6)} %eq.5), kind=kOutput, calls=%fused_computation.23 | convolution fusion | flops 4295491584 | bytes 20971520 | tf_op jit(solution)/shard_map/tc,te->ce/dot_general | solution.py:47
  412.5 12.2 %fusion.12 = f32[2048,256]{0,1:T(8,128)} fusion(bf16[4096,256]{1,0:T(8,128)(2,1)} %fusion.5, bf16[4096,2048]{1,0:T(8,128)(2,1)} %all-gather.3.cloned.1.call-done, pred[]{:T(512)S(6)} %eq.5), kind=kOutput, calls=%fused_computation.25 | convolution fusion | flops 4295491584 | bytes 20971520 | tf_op jit(solution)/shard_map/tc,te->ce/dot_general | solution.py:46
  424.7 15.0 %fusion.18 = f32[4096,2048]{1,0:T(8,128)} fusion(bf16[4096,256]{1,0:T(8,128)(2,1)} %fusion.5, bf16[2048,1,256]{2,0,1:T(8,128)(2,1)S(1)} %copy-done), kind=kOutput, calls=%fused_computation.31 | convolution fusion | flops 4294967296 | bytes 36700160 | tf_op jit(solution)/shard_map/te,ce->tc/dot_general | solution.py:42
  439.7 13.1 %fusion.21 = f32[4096,2048]{1,0:T(8,128)} fusion(bf16[4096,256]{1,0:T(8,128)(2,1)S(1)} %fusion.4, bf16[2048,1,256]{2,0,1:T(8,128)(2,1)S(1)} %copy-done.4), kind=kOutput, calls=%fused_computation.34 | convolution fusion | flops 4294967296 | bytes 36700160 | tf_op jit(solution)/shard_map/hte,che->tc/dot_general | solution.py:41
  452.9 34.6 %add_add_fusion = f32[4096,2048]{1,0:T(8,128)} fusion(f32[4096,2048]{1,0:T(8,128)} %fusion.21, f32[4096,2048]{1,0:T(8,128)} %fusion.18, bf16[4096,256]{1,0:T(8,128)(2,1)} %fusion.6, bf16[2048,1,256]{2,0,1:T(8,128)(2,1)} %param.10), kind=kOutput, calls=%fused_computation.6 | convolution fusion | flops 4311744512 | bytes 103809024 | tf_op jit(solution)/shard_map/te,ce->tc/dot_general | solution.py:43
  487.5 9.5 %convolution_bitcast_fusion.1 = f32[2048,1,256]{0,2,1:T(8,128)} fusion(bf16[4096,256]{1,0:T(8,128)(2,1)S(1)} %fusion.4, bf16[4096,2048]{1,0:T(8,128)(2,1)} %all-gather.3.cloned.1.call-done), kind=kOutput, calls=%fused_computation.21 | convolution fusion | flops 4294967296 | bytes 20971520 | tf_op jit(solution)/shard_map/tc,hte->che/dot_general | solution.py:40
  496.9 6.0 copy.12
  503.0 12.9 %convolution_bitcast_fusion = f32[1,256,2048]{2,1,0:T(8,128)} fusion(bf16[4096,2048]{1,0:T(8,128)(2,1)} %all-gather.5.cloned.1.call-done, f32[4096,256]{1,0:T(8,128)} %online-softmax), kind=kOutput, calls=%fused_computation.20 | convolution fusion | flops 4296015872 | bytes 23068672 | tf_op jit(solution)/shard_map/hte,tc->hec/dot_general | solution.py:33
  519.4 165.7 %reduce-scatter.4.cloned.1.call-done = f32[512,2048]{1,0:T(8,128)} async-done(((f32[4096,2048]{1,0:T(8,128)}), f32[512,2048]{1,0:T(8,128)}) %reduce-scatter.4.cloned.1.call-update) | async-done | bytes 4194320 | tf_op jit(solution)/shard_map/reduce_scatter | solution.py:44
  685.2 3.8 convert_element_type.63
  (29 shorter events, 8.6 us)
Async XLA Ops:
  7.2 175.5 %copy-start = (bf16[2048,1,256]{2,0,1:T(8,128)(2,1)S(1)}, bf16[2048,1,256]{2,0,1:T(8,128)(2,1)}, u32[]{:S(2)}) copy-start(bf16[2048,1,256]{2,0,1:T(8,128)(2,1)} %param.9) | copy-start | bytes 3145732
  7.2 89.6 %all-gather.5.cloned.1.call-start = ((), (), s32[]{:S(2)}) async-start(), calls=%async_computation.4 | async-start | bytes 18874368 | tf_op jit(solution)/shard_map/all_gather | solution.py:21
  7.9 174.8 %all-gather.3.cloned.1.call-start = ((), (), s32[]{:S(2)}) async-start(), calls=%async_computation.3 | async-start | bytes 18874368 | tf_op jit(solution)/shard_map/all_gather | solution.py:20
  8.7 507.2 %reduce-scatter.8.cloned.1.call-start = ((), (), s32[]{:S(2)}) async-start(), calls=%async_computation.7 | async-start | bytes 2359296 | tf_op jit(solution)/shard_map/reduce_scatter | solution.py:51
  253.9 24.5 %copy-start.3 = (bf16[2048,1,256]{2,0,1:T(8,128)(2,1)S(1)}, bf16[2048,1,256]{2,0,1:T(8,128)(2,1)}, u32[]{:S(2)}) copy-start(bf16[2048,1,256]{2,0,1:T(8,128)(2,1)} %param.10) | copy-start | bytes 3145732
  323.9 4.6 copy-start.2
  328.5 41.0 %copy-start.5 = (bf16[4096,256]{0,1:T(8,128)(2,1)S(1)}, bf16[4096,256]{0,1:T(8,128)(2,1)}, u32[]{:S(2)}) copy-start(bf16[4096,256]{0,1:T(8,128)(2,1)} %fusion.9) | copy-start | bytes 6291460
  369.5 17.5 %copy-start.6 = (bf16[4096,256]{1,0:T(8,128)(2,1)S(1)}, bf16[4096,256]{1,0:T(8,128)(2,1)}, u32[]{:S(2)}) copy-start(bf16[4096,256]{1,0:T(8,128)(2,1)} %convolution_convert_fusion) | copy-start | bytes 6291460
  387.0 15.6 %copy-start.1 = (bf16[4096,256]{1,0:T(8,128)(2,1)S(1)}, bf16[4096,256]{1,0:T(8,128)(2,1)}, u32[]{:S(2)}) copy-start(bf16[4096,256]{1,0:T(8,128)(2,1)} %fusion.6) | copy-start | bytes 6291460
  412.4 105.2 %reduce-scatter.6.cloned.1.call-start = ((), (), s32[]{:S(2)}) async-start(), calls=%async_computation.6 | async-start | bytes 2359296 | tf_op jit(solution)/shard_map/reduce_scatter | solution.py:50
  424.7 15.0 %copy-start.4 = (bf16[2048,1,256]{2,0,1:T(8,128)(2,1)S(1)}, bf16[2048,1,256]{2,0,1:T(8,128)(2,1)}, u32[]{:S(2)}) copy-start(bf16[2048,1,256]{2,0,1:T(8,128)(2,1)} %param.8) | copy-start | bytes 3145732
  452.8 232.3 %reduce-scatter.4.cloned.1.call-start = ((), (), s32[]{:S(2)}) async-start(), calls=%async_computation.5 | async-start | bytes 37748736 | tf_op jit(solution)/shard_map/reduce_scatter | solution.py:44
Sparse Core Ops, SparseCore 0:
  9.8 86.8 all-gather.4
  98.6 84.0 all-gather.2
  412.6 32.5 reduce-scatter.7
  453.0 32.5 reduce-scatter.5
  488.9 196.2 reduce-scatter.3
where the time goes:
time: 705 us; the launch traced here: 696 us
  waiting for transfers between devices  328 us (47%)
  matrix products  276 us (39%)
  Pallas kernels  35.4 us (5%)
  other arithmetic  29.1 us (4%)
  between operations  14.3 us (2%)
  local copies, waits for them, and re-layouts  13 us (2%)
    reduce_scatter x1, waiting for transfers between devices, local_grads(): lax.psum_scatter(dx_part, 'tp', scatter_dimension=0, tiled=True)  166 us
    all_gather x1, waiting for transfers between devices, local_grads(): dy_full = lax.all_gather(dy_blk, 'tp', axis=0, tiled=True)  88 us
    all_gather x1, waiting for transfers between devices, local_grads(): x_full = lax.all_gather(x_blk, 'tp', axis=0, tiled=True)  72.3 us
    dot_general x1, matrix products, local_grads(): jnp.einsum('hqe,ke->hqk', d_out, val_rows, preferred_element_type=f32)  41 us
    unnamed x1, Pallas kernels  35.4 us
    dot_general x1, matrix products, local_grads(): jnp.einsum('te,ce->tc', d_val, wv_loc, preferred_element_type=f32)  34.6 us
    dot_general x1, matrix products, local_grads(): jnp.einsum('hqe,ke->hqk', queries, key_rows, preferred_element_type=f32)  28.5 us
    dot_general x1, matrix products, local_grads(): jnp.einsum('hqk,hqe->ke', prob_bf, d_out, preferred_element_type=f32)  24.5 us
  transfers between devices with their start and end apart: 5, of which 3 were waited for; matrix products, arithmetic and copies ran while one was open for 17% of the time, Pallas kernels for 0%

commit v1 on v0

v1 whole, which is shorter than its diff:
```python
import functools

import jax
import jax.numpy as jnp
from jax import lax
from jax.experimental import pallas as pl
from jax.experimental.pallas import tpu as pltpu
from jax.sharding import PartitionSpec as P

F32 = jnp.float32
BF16 = jnp.bfloat16
LOG2E = 1.4426950408889634
VMEM_BYTES = 60 * 1024 * 1024
NN = (((1,), (0,)), ((), ()))
NT = (((1,), (1,)), ((), ()))


def dot(a, b, dims=NN):
    return lax.dot_general(a, b, dims, preferred_element_type=F32)


def cost(flops, bytes_accessed, trans=0):
    return pl.CostEstimate(flops=int(flops), bytes_accessed=int(bytes_accessed), transcendentals=int(trans))


def params(**kw):
    return pltpu.CompilerParams(vmem_limit_bytes=VMEM_BYTES, **kw)


def whole(shape):
    return pl.BlockSpec(shape, lambda *_: (0,) * len(shape))


def qkv_body(x_ref, wq_ref, wk_ref, wv_ref, q_ref, qt_ref, k_ref, kt_ref, v_ref, vt_ref):
    x = x_ref[...]
    for w_ref, o_ref, ot_ref in ((wq_ref, q_ref, qt_ref), (wk_ref, k_ref, kt_ref), (wv_ref, v_ref, vt_ref)):
        acc = dot(x, w_ref[...])
        o_ref[...] = acc.astype(BF16)
        ot_ref[...] = acc.T.astype(BF16)


def project_qkv(x, wq, wk, wv, rows):
    tokens, model = x.shape
    head = wq.shape[1]
    nat = pl.BlockSpec((rows, head), lambda i: (i, 0))
    tra = pl.BlockSpec((head, rows), lambda i: (0, i))
    return pl.pallas_call(
        qkv_body,
        grid=(tokens // rows,),
        in_specs=[pl.BlockSpec((rows, model), lambda i: (i, 0))] + [whole((model, head))] * 3,
        out_specs=[nat, tra] * 3,
        out_shape=[jax.ShapeDtypeStruct((tokens, head), BF16), jax.ShapeDtypeStruct((head, tokens), BF16)] * 3,
        compiler_params=params(),
        cost_estimate=cost(6 * tokens * model * head, 2 * tokens * model),
        name="qkv",
    )(x, wq, wk, wv)


def fwd_body(c2, blk, qt_ref, k_ref, vt_ref, ot_ref, m_ref, rl_ref, s_ref, acc_ref):
    i = pl.program_id(0)
    qt = qt_ref[...]

    def score(j, m):
        at = pl.ds(pl.multiple_of(j * blk, blk), blk)
        s = dot(k_ref[at, :], qt) * c2
        s_ref[at, :] = s
        return jnp.maximum(m, jnp.max(s, axis=0, keepdims=True))

    m = lax.fori_loop(0, i, score, jnp.full((1, blk), -jnp.inf, F32))
    at = pl.ds(pl.multiple_of(i * blk, blk), blk)
    s = dot(k_ref[at, :], qt) * c2
    key = lax.broadcasted_iota(jnp.int32, (blk, blk), 0)
    qry = lax.broadcasted_iota(jnp.int32, (blk, blk), 1)
    s = jnp.where(key <= qry, s, -jnp.inf)
    s_ref[at, :] = s
    m = jnp.maximum(m, jnp.max(s, axis=0, keepdims=True))

    def expo(j, l):
        at = pl.ds(pl.multiple_of(j * blk, blk), blk)
        p = jnp.exp2(s_ref[at, :] - m)
        s_ref[at, :] = p
        return l + jnp.sum(p, axis=0, keepdims=True)

    l = lax.fori_loop(0, i + 1, expo, jnp.zeros((1, blk), F32))
    rl = 1.0 / l
    acc_ref[...] = jnp.zeros_like(acc_ref)

    def out(j, _):
        at = pl.ds(pl.multiple_of(j * blk, blk), blk)
        acc_ref[...] += dot(vt_ref[:, at], (s_ref[at, :] * rl).astype(BF16))
        return 0

    lax.fori_loop(0, i + 1, out, 0)
    ot_ref[...] = acc_ref[...].astype(BF16)
    m_ref[...] = m
    rl_ref[...] = rl


def attend(qt, k, vt, blk, c2):
    head, tokens = qt.shape
    col = pl.BlockSpec((head, blk), lambda i: (0, i))
    row = pl.BlockSpec((1, blk), lambda i: (0, i))
    return pl.pallas_call(
        functools.partial(fwd_body, c2, blk),
        grid=(tokens // blk,),
        in_specs=[col, whole((tokens, head)), whole((head, tokens))],
        out_specs=[col, row, row],
        out_shape=[jax.ShapeDtypeStruct((head, tokens), BF16)] + [jax.ShapeDtypeStruct((1, tokens), F32)] * 2,
        scratch_shapes=[pltpu.VMEM((tokens, blk), F32), pltpu.VMEM((head, blk), F32)],
        compiler_params=params(),
        cost_estimate=cost(2 * tokens * tokens * head, 8 * tokens * head, tokens * tokens // 2),
        name="fwd",
    )(qt, k, vt)


def dout_body(dy_ref, wo_ref, ot_ref, do_ref, dot_ref, delta_ref, dwo_ref):
    @pl.when(pl.program_id(0) == 0)
    def _():
        dwo_ref[...] = jnp.zeros_like(dwo_ref)

    dy = dy_ref[...]
    d_out = dot(dy, wo_ref[...], NT).astype(BF16)
    do_ref[...] = d_out
    d_out_t = d_out.astype(F32).T
    dot_ref[...] = d_out_t.astype(BF16)
    delta_ref[...] = jnp.sum(d_out_t * ot_ref[...].astype(F32), axis=0, keepdims=True)
    dwo_ref[...] += dot(ot_ref[...], dy)


def grad_out(dy, wo, ot, rows):
    tokens, model = dy.shape
    head = wo.shape[0]
    return pl.pallas_call(
        dout_body,
        grid=(tokens // rows,),
        in_specs=[
            pl.BlockSpec((rows, model), lambda i: (i, 0)),
            whole((head, model)),
            pl.BlockSpec((head, rows), lambda i: (0, i)),
        ],
        out_specs=[
            pl.BlockSpec((rows, head), lambda i: (i, 0)),
            pl.BlockSpec((head, rows), lambda i: (0, i)),
            pl.BlockSpec((1, rows), lambda i: (0, i)),
            whole((head, model)),
        ],
        out_shape=[
            jax.ShapeDtypeStruct((tokens, head), BF16),
            jax.ShapeDtypeStruct((head, tokens), BF16),
            jax.ShapeDtypeStruct((1, tokens), F32),
            jax.ShapeDtypeStruct((head, model), F32),
        ],
        compiler_params=params(),
        cost_estimate=cost(4 * tokens * model * head, 2 * tokens * model),
        name="dout",
    )(dy, wo, ot)


def bwd_body(c2, scale, blk, n, q_ref, qt_ref, k_ref, kt_ref, v_ref, do_ref, dot_ref, m_ref, rl_ref, delta_ref,
             dq_ref, dqt_ref, dk_ref, dkt_ref, dv_ref, dvt_ref, dk_acc, dv_acc, dq_acc):
    dq_acc[...] = jnp.zeros_like(dq_acc)

    def pair(j, i, masked):
        at_k = pl.ds(pl.multiple_of(j * blk, blk), blk)
        at_q = pl.ds(pl.multiple_of(i * blk, blk), blk)
        s = dot(k_ref[at_k, :], qt_ref[:, at_q])
        p = jnp.exp2(s * c2 - m_ref[:, at_q]) * rl_ref[:, at_q]
        if masked:
            key = lax.broadcasted_iota(jnp.int32, (blk, blk), 0)
            qry = lax.broadcasted_iota(jnp.int32, (blk, blk), 1)
            p = jnp.where(key <= qry, p, 0.0)
        dp = dot(v_ref[at_k, :], dot_ref[:, at_q])
        ds = (p * (dp - delta_ref[:, at_q])).astype(BF16)
        dv = dot(p.astype(BF16), do_ref[at_q, :])
        dk = dot(ds, q_ref[at_q, :])
        dq_acc[:, at_q] += dot(kt_ref[:, at_k], ds)
        if masked:
            dv_acc[...] = dv
            dk_acc[...] = dk
        else:
            dv_acc[...] += dv
            dk_acc[...] += dk

    def column(j, _):
        pair(j, j, True)

        def rest(i, _):
            pair(j, i, False)
            return 0

        lax.fori_loop(j + 1, n, rest, 0)
        at_k = pl.ds(pl.multiple_of(j * blk, blk), blk)
        dk = dk_acc[...] * scale
        dv = dv_acc[...]
        dk_ref[at_k, :] = dk.astype(BF16)
        dv_ref[at_k, :] = dv.astype(BF16)
        dkt_ref[:, at_k] = dk.T.astype(BF16)
        dvt_ref[:, at_k] = dv.T.astype(BF16)
        return 0

    lax.fori_loop(0, n, column, 0)

    def finish(i, _):
        at = pl.ds(pl.multiple_of(i * blk, blk), blk)
        dq = dq_acc[:, at] * scale
        dqt_ref[:, at] = dq.astype(BF16)
        dq_ref[at, :] = dq.T.astype(BF16)
        return 0

    lax.fori_loop(0, n, finish, 0)


def grad_attend(q, qt, k, kt, v, do, do_t, m, rl, delta, blk, c2, scale):
    tokens, head = q.shape
    nat = jax.ShapeDtypeStruct((tokens, head), BF16)
    tra = jax.ShapeDtypeStruct((head, tokens), BF16)
    vm = pl.BlockSpec(memory_space=pltpu.VMEM)
    return pl.pallas_call(
        functools.partial(bwd_body, c2, scale, blk, tokens // blk),
        in_specs=[vm] * 10,
        out_specs=[vm] * 6,
        out_shape=[nat, tra] * 3,
        scratch_shapes=[pltpu.VMEM((blk, head), F32)] * 2 + [pltpu.VMEM((head, tokens), F32)],
        compiler_params=params(),
        cost_estimate=cost(5 * tokens * tokens * head, 16 * tokens * head, tokens * tokens // 2),
        name="bwd",
    )(q, qt, k, kt, v, do, do_t, m, rl, delta)


def dw_body(x_ref, dqt_ref, dkt_ref, dvt_ref, dwq_ref, dwkv_ref):
    x = x_ref[...]
    head = dqt_ref.shape[0]
    dwq_ref[...] = dot(dqt_ref[...], x).T
    dwkv_ref[:, :head] = dot(dkt_ref[...], x).T
    dwkv_ref[:, head:] = dot(dvt_ref[...], x).T


def grad_w(x, dqt, dkt, dvt, cols):
    tokens, model = x.shape
    head = dqt.shape[0]
    return pl.pallas_call(
        dw_body,
        grid=(model // cols,),
        in_specs=[pl.BlockSpec((tokens, cols), lambda i: (0, i))] + [whole((head, tokens))] * 3,
        out_specs=[pl.BlockSpec((cols, head), lambda i: (i, 0)), pl.BlockSpec((cols, 2 * head), lambda i: (i, 0))],
        out_shape=[jax.ShapeDtypeStruct((model, head), F32), jax.ShapeDtypeStruct((model, 2 * head), F32)],
        compiler_params=params(),
        cost_estimate=cost(6 * tokens * model * head, 2 * tokens * model),
        name="dw",
    )(x, dqt, dkt, dvt)


def split3(x):
    hi = x.astype(BF16)
    r = x - hi.astype(F32)
    mid = r.astype(BF16)
    lo = (r - mid.astype(F32)).astype(BF16)
    return hi, mid, lo


def dx_body(n, rows, cols, dq_ref, dk_ref, dv_ref, wq_ref, wk_ref, wv_ref, dx_ref, got, parts, send, recv, local):
    me = lax.axis_index("tp")
    barrier = pltpu.get_barrier_semaphore()
    for p in range(1, n):
        pl.semaphore_signal(barrier, inc=1, device_id={"tp": lax.rem(me + p, n)}, device_id_type=pl.DeviceIdType.MESH)
    pl.semaphore_wait(barrier, n - 1)
    copies = []
    for t, src in enumerate((dk_ref, dv_ref, dq_ref)):
        for p in range(1, n):
            to = lax.rem(me + p, n)
            copy = pltpu.make_async_remote_copy(
                src_ref=src.at[pl.ds(pl.multiple_of(to * rows, rows), rows), :],
                dst_ref=got.at[t, p],
                send_sem=send.at[t, p],
                recv_sem=recv.at[t, p],
                device_id={"tp": to},
                device_id_type=pl.DeviceIdType.MESH,
            )
            copy.start()
            copies.append(copy)
        own = pltpu.make_async_copy(src.at[pl.ds(pl.multiple_of(me * rows, rows), rows), :], got.at[t, 0], local.at[t])
        own.start()
        copies.append(own)
    for copy in copies:
        copy.wait()
    for t in range(2):
        total = got[t, 0].astype(F32)
        for p in range(1, n):
            total += got[t, p].astype(F32)
        for e, part in enumerate(split3(total)):
            parts[t, e] = part

    def column(b, _):
        at = pl.ds(pl.multiple_of(b * cols, cols), cols)
        acc = None
        for t, w_ref in ((0, wk_ref), (1, wv_ref)):
            w = w_ref[at, :]
            for e in range(3):
                d = dot(parts[t, e], w, NT)
                acc = d if acc is None else acc + d
        for p in range(n):
            acc += dot(got[2, p], wq_ref[lax.rem(me + n - p, n), at, :], NT)
        dx_ref[:, at] = acc.astype(BF16)
        return 0

    lax.fori_loop(0, wk_ref.shape[0] // cols, column, 0)


def grad_x(dq, dk, dv, wq_all, wk, wv, n, cols):
    tokens, head = dq.shape
    model = wk.shape[0]
    rows = tokens // n
    hbm = pl.BlockSpec(memory_space=pl.ANY)
    vm = pl.BlockSpec(memory_space=pltpu.VMEM)
    return pl.pallas_call(
        functools.partial(dx_body, n, rows, cols),
        in_specs=[hbm] * 3 + [vm] * 3,
        out_specs=vm,
        out_shape=jax.ShapeDtypeStruct((rows, model), BF16),
        scratch_shapes=[
            pltpu.VMEM((3, n, rows, head), BF16),
            pltpu.VMEM((2, 3, rows, head), BF16),
            pltpu.SemaphoreType.DMA((3, n)),
            pltpu.SemaphoreType.DMA((3, n)),
            pltpu.SemaphoreType.DMA((3,)),
        ],
        compiler_params=params(collective_id=0, has_side_effects=True),
        cost_estimate=cost(60e9, 16e6),
        name="dx",
    )(dq, dk, dv, wq_all, wk, wv)


def solution(mesh):
    n = mesh.shape["tp"]

    def local_grads(x_blk, dy_blk, wq_loc, w_k, w_v, wo_loc):
        model, kv_heads, head = w_k.shape
        scale = head ** -0.5
        c2 = scale * LOG2E
        wq = wq_loc.reshape(model, head)
        wk = w_k.reshape(model, head)
        wv = w_v.reshape(model, head)
        wo = wo_loc.reshape(head, model)
        x = lax.all_gather(x_blk, "tp", axis=0, tiled=True)
        dy = lax.all_gather(dy_blk, "tp", axis=0, tiled=True)
        wq_all = lax.all_gather(wq, "tp", axis=0, tiled=False)
        q, qt, k, kt, v, vt = project_qkv(x, wq, wk, wv, 512)
        ot, m, rl = attend(qt, k, vt, 512, c2)
        do, do_t, delta, dwo = grad_out(dy, wo, ot, 512)
        dq, dqt, dk, dkt, dv, dvt = grad_attend(q, qt, k, kt, v, do, do_t, m, rl, delta, 512, c2, scale)
        dwq, dwkv = grad_w(x, dqt, dkt, dvt, 512)
        dwkv_blk = lax.psum_scatter(dwkv, "tp", scatter_dimension=0, tiled=True)
        dx = grad_x(dq, dk, dv, wq_all, wk, wv, n, 512)
        return (dx, dwq.reshape(model, 1, head), dwo.reshape(1, head, model), dwkv_blk[:, :head], dwkv_blk[:, head:])

    tok_spec = P(("dp", "tp"))
    return jax.shard_map(
        local_grads,
        mesh=mesh,
        in_specs=(tok_spec, tok_spec, P(None, "tp", None), P(), P(), P("tp")),
        out_specs=(tok_spec, P("dp", "tp", None), tok_spec, tok_spec, tok_spec),
        check_vma=False,
    )
```

time: 705 us -> 387 us (0.55); the launches traced: 696 us -> 385 us
  matrix products: 276 us -> 0 us
  waiting for transfers between devices: 328 us -> 125 us
  Pallas kernels: 35.4 us -> 231 us
  other arithmetic: 29.1 us -> 0 us
    dot_general x16 -> x0, matrix products: 276 us -> none  [the longest x1 41 us: local_grads(): jnp.einsum('hqe,ke->hqk', d_out, val_rows, preferred_element_type=f32)]
    pallas_call x0 -> x6, Pallas kernels: none -> 231 us  [the longest x1 101 us: grad_x(): pl.pallas_call(functools.partial(dx_body, n, rows, cols), in_specs=[hbm]...]
    reduce_scatter x3 -> x1, waiting for transfers between devices: 166 us -> 0.01 us  [local_grads(): dwkv_blk = lax.psum_scatter(dwkv, 'tp', scatter_dimension=0, tiled=True)]
    all_gather x2 -> x3, waiting for transfers between devices: 160 us -> 123 us  [the longest x1 87.3 us: local_grads(): x = lax.all_gather(x_blk, 'tp', axis=0, tiled=True)]
    unnamed x1 -> x0, Pallas kernels: 35.4 us -> none
    reduce_sum x1 -> x0, other arithmetic: 21.1 us -> none  [local_grads(): attn_prob = jax.nn.softmax(scores, axis=-1)]
  transfers between devices with their start and end apart: 5 -> 4, of which waited for: 3 -> 2; matrix products, arithmetic and copies ran while one was open for 17% -> 3% of each run, Pallas kernels for 0% -> 60%
where the time goes in v1:
time: 387 us; the launch traced here: 385 us
  Pallas kernels  231 us (60%)
  waiting for transfers between devices  125 us (32%)
  local copies, waits for them, and re-layouts  15.2 us (4%)
  between operations  13.8 us (4%)
    pallas_call x1, Pallas kernels, grad_x(): pl.pallas_call(functools.partial(dx_body, n, rows, cols), in_specs=[hbm]...  101 us
    all_gather x1, waiting for transfers between devices, local_grads(): x = lax.all_gather(x_blk, 'tp', axis=0, tiled=True)  87.3 us
    pallas_call x1, Pallas kernels, grad_attend(): pl.pallas_call(functools.partial(bwd_body, c2, scale, blk, tokens // blk)...  44.3 us
    all_gather x1, waiting for transfers between devices, local_grads(): dy = lax.all_gather(dy_blk, 'tp', axis=0, tiled=True)  35.2 us
    pallas_call x1, Pallas kernels, attend(): pl.pallas_call(functools.partial(fwd_body, c2, blk), grid=(tokens // blk,...  31.8 us
    pallas_call x1, Pallas kernels, grad_w(): pl.pallas_call(dw_body, grid=(model // cols,), in_specs=[pl.BlockSpec((to...  19.4 us
    pallas_call x1, Pallas kernels, project_qkv(): pl.pallas_call(qkv_body, grid=(tokens // rows,), in_specs=[pl.BlockSpec((...  19 us
    pallas_call x1, Pallas kernels, grad_out(): pl.pallas_call(dout_body, grid=(tokens // rows,), in_specs=[pl.BlockSpec(...  15.7 us
  transfers between devices with their start and end apart: 4, of which 2 were waited for; matrix products, arithmetic and copies ran while one was open for 3% of the time, Pallas kernels for 60%

profile of v1, /device:TPU:0, one launch (start us, length us, event | category | flops | bytes accessed | tf_op | source)
XLA Modules:
  0.0 385.2 jit_solution(8868530007463594853)
XLA Ops:
  7.2 0.0 all-gather.5.cloned.1.call-start
  7.2 0.7 all-gather.5.cloned.1.call-update
  7.9 0.0 all-gather.7.cloned.1.call-start
  7.9 0.7 all-gather.7.cloned.1.call-update
  8.6 0.0 all-gather.9.cloned.1.call-start
  8.7 0.7 all-gather.9.cloned.1.call-update
  9.4 0.0 reduce-scatter.2.cloned.1.call-start
  9.4 87.3 %all-gather.5.cloned.1.call-done.x_ref = bf16[4096,2048]{1,0:T(8,128)(2,1)} async-done(((bf16[512,2048]{1,0:T(8,128)(2,1)}), bf16[4096,2048]{1,0:T(8,128)(2,1)}) %all-gather.5.cloned.1.call-update) | async-done | bytes 16777232 | tf_op jit(solution)/shard_map/all_gather | solution.py:344
  96.7 19.0 %qkv.1 = (bf16[4096,256]{1,0:T(8,128)(2,1)}, bf16[256,4096]{1,0:T(8,128)(2,1)}, bf16[4096,256]{1,0:T(8,128)(2,1)}, bf16[256,4096]{1,0:T(8,128)(2,1)}, bf16[4096,...) custom-call(bf16[4096,2048]{1,0:T(8,128)(2,1)} %all-gather.5.cloned.1.call-done.x_ref, bf16[2048,256]{1,0:T(8,128)(2,1)} %bitcast.8, ...), custom_call_target="tpu_custom_call" | custom-call | flops 12884901888 | bytes 16777216 | tf_op jit(solution)/shard_map/qkv/pallas_call | solution.py:47
  115.7 31.8 %fwd.1 = (bf16[256,4096]{1,0:T(8,128)(2,1)}, f32[1,4096]{1,0:T(1,128)}, f32[1,4096]{1,0:T(1,128)}) custom-call(bf16[256,4096]{1,0:T(8,128)(2,1)} %get-tuple-element.27.qt_ref, bf16[4096,256]{1,0:T(8,128)(2,1)} %get-tuple-element.28.k_ref, bf16[256,4096]{1,0:T(8,128)(2,1)} %get-tuple-element.31.vt_ref), custom_call_target="tpu_custom_call" | custom-call | flops 8589934592 | bytes 8388608 | tf_op jit(solution)/shard_map/fwd/pallas_call | solution.py:103
  147.5 35.2 %all-gather.7.cloned.1.call-done.dy_ref = bf16[4096,2048]{1,0:T(8,128)(2,1)} async-done(((bf16[512,2048]{1,0:T(8,128)(2,1)}), bf16[4096,2048]{1,0:T(8,128)(2,1)}) %all-gather.7.cloned.1.call-update) | async-done | bytes 16777232 | tf_op jit(solution)/shard_map/all_gather | solution.py:345
  182.7 15.7 %dout.1 = (bf16[4096,256]{1,0:T(8,128)(2,1)}, bf16[256,4096]{1,0:T(8,128)(2,1)}, f32[1,4096]{1,0:T(1,128)}, f32[256,2048]{1,0:T(8,128)}) custom-call(bf16[4096,2048]{1,0:T(8,128)(2,1)} %all-gather.7.cloned.1.call-done.dy_ref, bf16[256,2048]{1,0:T(8,128)(2,1)} %bitcast.10, bf16[256,4096]{1,0:T(8,128)(2,1)} %get-tuple-element.32.ot_ref), custom_call_target="tpu_custom_call" | custom-call | flops 8589934592 | bytes 16777216 | tf_op jit(solution)/shard_map/dout/pallas_call | solution.py:133
  198.4 44.3 %bwd.1 = (bf16[4096,256]{1,0:T(8,128)(2,1)}, bf16[256,4096]{1,0:T(8,128)(2,1)}, bf16[4096,256]{1,0:T(8,128)(2,1)}, bf16[256,4096]{1,0:T(8,128)(2,1)}, bf16[4096,...) custom-call(bf16[4096,256]{1,0:T(8,128)(2,1)} %get-tuple-element.26.q_ref, bf16[256,4096]{1,0:T(8,128)(2,1)} %get-tuple-element.27.qt_ref, ...), custom_call_target="tpu_custom_call" | custom-call | flops 21474836480 | bytes 16777216 | tf_op jit(solution)/shard_map/bwd/pallas_call | solution.py:218
  242.6 19.4 %dw.1 = (f32[2048,256]{1,0:T(8,128)}, f32[2048,512]{1,0:T(8,128)}) custom-call(bf16[4096,2048]{1,0:T(8,128)(2,1)} %all-gather.5.cloned.1.call-done.x_ref, bf16[256,4096]{1,0:T(8,128)(2,1)} %get-tuple-element.41.dqt_ref, bf16[256,4096]{1,0:T(8,128)(2,1)} %get-tuple-element.42.dkt_ref, bf16[256,4096]{1,0:T(8,128)(2,1)} %get-tuple-element.43.dvt_ref), custom_call_target="tpu_custom_call" | custom-call | flops 12884901888 | bytes 16777216 | tf_op jit(solution)/shard_map/dw/pallas_call | solution.py:241
  262.0 0.0 reduce-scatter.2.cloned.1.call-update
  262.0 0.0 all-gather.9.cloned.1.call-done
  262.0 0.0 copy-start
  262.0 101.4 %dx.1 = bf16[512,2048]{1,0:T(8,128)(2,1)} custom-call(bf16[4096,256]{1,0:T(8,128)(2,1)} %get-tuple-element.38.dq_ref, bf16[4096,256]{1,0:T(8,128)(2,1)} %get-tuple-element.39.dk_ref, bf16[4096,256]{1,0:T(8,128)(2,1)} %get-tuple-element.40.dv_ref, bf16[8,2048,256]{2,1,0:T(8,128)(2,1)} %bitcast.9, bf16[2048,256]{1,0:T(8,128)(2,1)} %bitcast.12, ...), custom_call_target="tpu_custom_call" | custom-call | flops 60000002048 | bytes 16000000 | tf_op jit(solution)/shard_map/dx/pallas_call | solution.py:315
  363.5 0.0 copy-done
  363.5 10.2 %copy.11 = f32[2048,1,256]{2,1,0:T(1,128)} copy(f32[2048,1,256]{2,0,1:T(8,128)S(1)} %bitcast.7) | data formatting | bytes 4194304
  373.6 0.0 reduce-scatter.2.cloned.1.call-done
  373.6 1.9 fusion
  375.5 3.2 copy.13
Async XLA Ops:
  7.2 89.6 %all-gather.5.cloned.1.call-start = ((), (), s32[]{:S(2)}) async-start(), calls=%async_computation.1 | async-start | bytes 18874368 | tf_op jit(solution)/shard_map/all_gather | solution.py:344
  7.9 174.8 %all-gather.7.cloned.1.call-start = ((), (), s32[]{:S(2)}) async-start(), calls=%async_computation.2 | async-start | bytes 18874368 | tf_op jit(solution)/shard_map/all_gather | solution.py:345
  8.6 253.4 %all-gather.9.cloned.1.call-start = ((), (), s32[]{:S(2)}) async-start(), calls=%async_computation.4 | async-start | bytes 9437184 | tf_op jit(solution)/shard_map/all_gather | solution.py:346
  9.4 364.3 %reduce-scatter.2.cloned.1.call-start = ((), (), s32[]{:S(2)}) async-start(), calls=%async_computation.3 | async-start | bytes 4718592 | tf_op jit(solution)/shard_map/reduce_scatter | solution.py:352
  262.0 101.4 %copy-start = (f32[2048,256]{1,0:T(8,128)S(1)}, f32[2048,256]{1,0:T(8,128)}, u32[]{:S(2)}) copy-start(f32[2048,256]{1,0:T(8,128)} %get-tuple-element.44) | copy-start | bytes 6291460
Sparse Core Ops, SparseCore 0:
  9.8 86.8 all-gather.4
  98.5 84.0 all-gather.6
  184.5 48.3 all-gather.8
  262.1 82.9 reduce-scatter.1

commit v2 on v1

--- a/solution.py
+++ b/solution.py
@@ -31,129 +31,285 @@
     return pl.BlockSpec(shape, lambda *_: (0,) * len(shape))
 
 
-def qkv_body(x_ref, wq_ref, wk_ref, wv_ref, q_ref, qt_ref, k_ref, kt_ref, v_ref, vt_ref):
-    x = x_ref[...]
-    for w_ref, o_ref, ot_ref in ((wq_ref, q_ref, qt_ref), (wk_ref, k_ref, kt_ref), (wv_ref, v_ref, vt_ref)):
-        acc = dot(x, w_ref[...])
-        o_ref[...] = acc.astype(BF16)
-        ot_ref[...] = acc.T.astype(BF16)
-
-
-def project_qkv(x, wq, wk, wv, rows):
-    tokens, model = x.shape
+class Gather:
+    CHUNKS = 4
+    X_ORDER = (0, 1, 2, 3)
+    Y_ORDER = (2, 3, 0, 1)
+    SEMS = [pltpu.SemaphoreType.DMA((7, CHUNKS)), pltpu.SemaphoreType.DMA((7, CHUNKS))]
+
+    def __init__(self, own_ref, full_ref, send, recv):
+        me = lax.axis_index("tp")
+        c, x, y = me % 2, (me // 2) % 2, me // 4
+        self.me = me
+        self.xn = me + 2 - 4 * x
+        self.yn = me + 4 - 8 * y
+        self.dg = self.xn + 4 - 8 * y
+        self.flip = 1 - 2 * c
+        self.sib = me + self.flip
+        self.own, self.full, self.send, self.recv = own_ref, full_ref, send, recv
+        self.rows = own_ref.shape[0]
+        self.piece = self.rows // self.CHUNKS
+        self.sent = []
+
+    def enter(self):
+        barrier = pltpu.get_barrier_semaphore()
+        for dev in (self.xn, self.yn, self.sib):
+            pl.semaphore_signal(barrier, inc=1, device_id={"tp": dev}, device_id_type=pl.DeviceIdType.MESH)
+        pl.semaphore_wait(barrier, 3)
+
+    def at(self, dev, q):
+        return pl.ds(pl.multiple_of(dev * self.rows + q * self.piece, self.piece), self.piece)
+
+    def copy(self, src, shard, q, slot, to):
+        return pltpu.make_async_remote_copy(
+            src_ref=src,
+            dst_ref=self.full.at[self.at(shard, q), :],
+            send_sem=self.send.at[slot, q],
+            recv_sem=self.recv.at[slot, q],
+            device_id={"tp": to},
+            device_id_type=pl.DeviceIdType.MESH,
+        )
+
+    def push(self, src, shard, q, slot, to):
+        copy = self.copy(src, shard, q, slot, to)
+        copy.start()
+        self.sent.append(copy)
+
+    def start(self):
+        for s in range(self.CHUNKS):
+            for slot, to, q in ((0, self.xn, self.X_ORDER[s]), (1, self.yn, self.Y_ORDER[s]), (3, self.sib, s)):
+                self.push(self.own.at[pl.ds(q * self.piece, self.piece), :], self.me, q, slot, to)
+
+    def take(self, shard, q, slot):
+        self.copy(self.full.at[self.at(shard, q), :], shard, q, slot, self.sib).wait_recv()
+
+    def hand(self, shard, q, slot, to):
+        self.push(self.full.at[self.at(shard, q), :], shard, q, slot, to)
+
+    def step(self, s):
+        q = self.X_ORDER[s]
+        self.take(self.xn, q, 0)
+        if s < 2:
+            self.hand(self.xn, q, 2, self.yn)
+        self.hand(self.xn, q, 4, self.sib)
+        q = self.Y_ORDER[s]
+        self.take(self.yn, q, 1)
+        if s < 2:
+            self.hand(self.yn, q, 2, self.xn)
+        self.hand(self.yn, q, 5, self.sib)
+
+    def last(self, s):
+        for q in (self.Y_ORDER[s], self.X_ORDER[s]):
+            self.take(self.dg, q, 2)
+            self.hand(self.dg, q, 6, self.sib)
+
+    def from_sib(self, slot, qs=range(CHUNKS)):
+        shard = {3: self.me, 4: self.xn, 5: self.yn, 6: self.dg}[slot] + self.flip
+        for q in qs:
+            self.take(shard, q, slot)
+
+    def near(self, k):
+        return self.xn + (self.yn - self.xn) * (k // 2) + self.flip * (k % 2)
+
+    def finish(self):
+        for copy in self.sent:
+            copy.wait_send()
+
+
+def qkv_body(x_ref, wq_ref, wk_ref, wv_ref, full_ref, q_ref, qt_ref, k_ref, kt_ref, v_ref, vt_ref,
+             buf, send, recv, local):
+    g = Gather(x_ref, buf, send, recv)
+    rows = g.rows
+
+    def project(x, start, count):
+        at = pl.ds(pl.multiple_of(start, count), count)
+        for w_ref, o_ref, ot_ref in ((wq_ref, q_ref, qt_ref), (wk_ref, k_ref, kt_ref), (wv_ref, v_ref, vt_ref)):
+            acc = dot(x, w_ref[...])
+            o_ref[at, :] = acc.astype(BF16)
+            ot_ref[:, at] = acc.T.astype(BF16)
+
+    out = []
+
+    def save(src, start, count):
+        at = pl.ds(pl.multiple_of(start, count), count)
+        copy = pltpu.make_async_copy(src, full_ref.at[at, :], local.at[len(out)])
+        copy.start()
+        out.append(copy)
+
+    def shard_of_buf(dev):
+        return buf.at[pl.ds(pl.multiple_of(dev * rows, rows), rows), :]
+
+    g.enter()
+    g.start()
+    save(x_ref, g.me * rows, rows)
+    project(x_ref[...], g.me * rows, rows)
+    g.step(0)
+    g.from_sib(3)
+    save(shard_of_buf(g.sib), g.sib * rows, rows)
+    g.step(1)
+
+    def project_shard(dev):
+        start = pl.multiple_of(dev * rows, rows)
+        project(buf[pl.ds(start, rows), :], start, rows)
+
+    g.step(2)
+    g.step(3)
+    g.from_sib(4)
+    g.from_sib(5)
+    for k in range(4):
+        save(shard_of_buf(g.near(k)), g.near(k) * rows, rows)
+
+    def five(k, _):
+        project_shard(jnp.where(k == 4, g.sib, g.near(k % 4)))
+        return 0
+
+    lax.fori_loop(0, 5, five, 0)
+    g.last(0)
+    g.last(1)
+
+    project_shard(g.dg)
+    save(shard_of_buf(g.dg), g.dg * rows, rows)
+    g.from_sib(6)
+    save(shard_of_buf(g.dg + g.flip), (g.dg + g.flip) * rows, rows)
+    project_shard(g.dg + g.flip)
+    g.finish()
+    for copy in out:
+        copy.wait()
+
+
+def project_qkv(x_blk, wq, wk, wv, n):
+    rows, model = x_blk.shape
+    tokens = rows * n
     head = wq.shape[1]
-    nat = pl.BlockSpec((rows, head), lambda i: (i, 0))
-    tra = pl.BlockSpec((head, rows), lambda i: (0, i))
+    vm = pl.BlockSpec(memory_space=pltpu.VMEM)
+    hbm = pl.BlockSpec(memory_space=pl.ANY)
+    pair = [jax.ShapeDtypeStruct((tokens, head), BF16), jax.ShapeDtypeStruct((head, tokens), BF16)]
     return pl.pallas_call(
         qkv_body,
-        grid=(tokens // rows,),
-        in_specs=[pl.BlockSpec((rows, model), lambda i: (i, 0))] + [whole((model, head))] * 3,
-        out_specs=[nat, tra] * 3,
-        out_shape=[jax.ShapeDtypeStruct((tokens, head), BF16), jax.ShapeDtypeStruct((head, tokens), BF16)] * 3,
-        compiler_params=params(),
+        in_specs=[vm] * 4,
+        out_specs=[hbm] + [vm] * 6,
+        out_shape=[jax.ShapeDtypeStruct((tokens, model), BF16)] + pair * 3,
+        scratch_shapes=[pltpu.VMEM((tokens, model), BF16)] + Gather.SEMS + [pltpu.SemaphoreType.DMA((n,))],
+        compiler_params=params(collective_id=1, has_side_effects=True),
         cost_estimate=cost(6 * tokens * model * head, 2 * tokens * model),
         name="qkv",
-    )(x, wq, wk, wv)
-
-
-def fwd_body(c2, blk, qt_ref, k_ref, vt_ref, ot_ref, m_ref, rl_ref, s_ref, acc_ref):
-    i = pl.program_id(0)
-    qt = qt_ref[...]
-
-    def score(j, m):
-        at = pl.ds(pl.multiple_of(j * blk, blk), blk)
-        s = dot(k_ref[at, :], qt) * c2
-        s_ref[at, :] = s
-        return jnp.maximum(m, jnp.max(s, axis=0, keepdims=True))
-
-    m = lax.fori_loop(0, i, score, jnp.full((1, blk), -jnp.inf, F32))
-    at = pl.ds(pl.multiple_of(i * blk, blk), blk)
-    s = dot(k_ref[at, :], qt) * c2
-    key = lax.broadcasted_iota(jnp.int32, (blk, blk), 0)
-    qry = lax.broadcasted_iota(jnp.int32, (blk, blk), 1)
-    s = jnp.where(key <= qry, s, -jnp.inf)
-    s_ref[at, :] = s
-    m = jnp.maximum(m, jnp.max(s, axis=0, keepdims=True))
-
-    def expo(j, l):
-        at = pl.ds(pl.multiple_of(j * blk, blk), blk)
-        p = jnp.exp2(s_ref[at, :] - m)
-        s_ref[at, :] = p
-        return l + jnp.sum(p, axis=0, keepdims=True)
-
-    l = lax.fori_loop(0, i + 1, expo, jnp.zeros((1, blk), F32))
-    rl = 1.0 / l
-    acc_ref[...] = jnp.zeros_like(acc_ref)
-
-    def out(j, _):
-        at = pl.ds(pl.multiple_of(j * blk, blk), blk)
-        acc_ref[...] += dot(vt_ref[:, at], (s_ref[at, :] * rl).astype(BF16))
+    )(x_blk, wq, wk, wv)
+
+
+def fwd_body(c2, blk, dy_ref, wo_ref, qt_ref, k_ref, vt_ref, ot_ref, m_ref, rl_ref, do_ref, dot_ref, delta_ref,
+             dwo_ref, buf, s_ref, acc_ref, send, recv):
+    g = Gather(dy_ref, buf, send, recv)
+    rows = g.rows
+
+    def attend(i, _):
+        at_i = pl.ds(pl.multiple_of(i * blk, blk), blk)
+        qt = qt_ref[:, at_i]
+
+        def score(j, m):
+            at = pl.ds(pl.multiple_of(j * blk, blk), blk)
+            s = dot(k_ref[at, :], qt) * c2
+            s_ref[at, :] = s
+            return jnp.maximum(m, jnp.max(s, axis=0, keepdims=True))
+
+        m = lax.fori_loop(0, i, score, jnp.full((1, blk), -jnp.inf, F32))
+        s = dot(k_ref[at_i, :], qt) * c2
+        key = lax.broadcasted_iota(jnp.int32, (blk, blk), 0)
+        qry = lax.broadcasted_iota(jnp.int32, (blk, blk), 1)
+        s = jnp.where(key <= qry, s, -jnp.inf)
+        s_ref[at_i, :] = s
+        m = jnp.maximum(m, jnp.max(s, axis=0, keepdims=True))
+
+        def expo(j, l):
+            at = pl.ds(pl.multiple_of(j * blk, blk), blk)
+            p = jnp.exp2(s_ref[at, :] - m)
+            s_ref[at, :] = p
+            return l + jnp.sum(p, axis=0, keepdims=True)
+
+        l = lax.fori_loop(0, i + 1, expo, jnp.zeros((1, blk), F32))
+        rl = 1.0 / l
+        acc_ref[...] = jnp.zeros_like(acc_ref)
+
+        def out(j, _):
+            at = pl.ds(pl.multiple_of(j * blk, blk), blk)
+            acc_ref[...] += dot(vt_ref[:, at], (s_ref[at, :] * rl).astype(BF16))
+            return 0
+
+        lax.fori_loop(0, i + 1, out, 0)
+        ot_ref[:, at_i] = acc_ref[...].astype(BF16)
+        m_ref[:, at_i] = m
+        rl_ref[:, at_i] = rl
         return 0
 
-    lax.fori_loop(0, i + 1, out, 0)
-    ot_ref[...] = acc_ref[...].astype(BF16)
-    m_ref[...] = m
-    rl_ref[...] = rl
-
-
-def attend(qt, k, vt, blk, c2):
+    def grad_out(dy, start):
+        at = pl.ds(pl.multiple_of(start, rows), rows)
+        d_out = dot(dy, wo_ref[...], NT).astype(BF16)
+        do_ref[at, :] = d_out
+        d_out_t = d_out.astype(F32).T
+        dot_ref[:, at] = d_out_t.astype(BF16)
+        ot = ot_ref[:, at]
+        delta_ref[:, at] = jnp.sum(d_out_t * ot.astype(F32), axis=0, keepdims=True)
+        dwo_ref[...] += dot(ot, dy)
+
+    def grad_out_shard(dev):
+        start = pl.multiple_of(dev * rows, rows)
+        grad_out(buf[pl.ds(start, rows), :], start)
+
+    g.enter()
+    g.start()
+    dwo_ref[...] = jnp.zeros_like(dwo_ref)
+    n = k_ref.shape[0] // blk
+    cuts = (0, n // 2, 3 * n // 4, n)
+    for s in range(2):
+        lax.fori_loop(cuts[s], cuts[s + 1], attend, 0)
+        g.step(s)
+    lax.fori_loop(cuts[2], cuts[3], attend, 0)
+    g.step(2)
+    g.from_sib(3)
+    grad_out(dy_ref[...], g.me * rows)
+    g.step(3)
+    g.from_sib(4)
+    g.from_sib(5)
+
+    def five(k, _):
+        grad_out_shard(jnp.where(k == 4, g.sib, g.near(k % 4)))
+        return 0
+
+    lax.fori_loop(0, 5, five, 0)
+    g.last(0)
+    g.last(1)
+    grad_out_shard(g.dg)
+    g.from_sib(6)
+    grad_out_shard(g.dg + g.flip)
+    g.finish()
+
+
+def attend_and_gather(dy_blk, wo, qt, k, vt, n, blk, c2):
+    rows, model = dy_blk.shape
     head, tokens = qt.shape
-    col = pl.BlockSpec((head, blk), lambda i: (0, i))
-    row = pl.BlockSpec((1, blk), lambda i: (0, i))
+    vm = pl.BlockSpec(memory_space=pltpu.VMEM)
     return pl.pallas_call(
         functools.partial(fwd_body, c2, blk),
-        grid=(tokens // blk,),
-        in_specs=[col, whole((tokens, head)), whole((head, tokens))],
-        out_specs=[col, row, row],
-        out_shape=[jax.ShapeDtypeStruct((head, tokens), BF16)] + [jax.ShapeDtypeStruct((1, tokens), F32)] * 2,
-        scratch_shapes=[pltpu.VMEM((tokens, blk), F32), pltpu.VMEM((head, blk), F32)],
-        compiler_params=params(),
-        cost_estimate=cost(2 * tokens * tokens * head, 8 * tokens * head, tokens * tokens // 2),
-        name="fwd",
-    )(qt, k, vt)
-
-
-def dout_body(dy_ref, wo_ref, ot_ref, do_ref, dot_ref, delta_ref, dwo_ref):
-    @pl.when(pl.program_id(0) == 0)
-    def _():
-        dwo_ref[...] = jnp.zeros_like(dwo_ref)
-
-    dy = dy_ref[...]
-    d_out = dot(dy, wo_ref[...], NT).astype(BF16)
-    do_ref[...] = d_out
-    d_out_t = d_out.astype(F32).T
-    dot_ref[...] = d_out_t.astype(BF16)
-    delta_ref[...] = jnp.sum(d_out_t * ot_ref[...].astype(F32), axis=0, keepdims=True)
-    dwo_ref[...] += dot(ot_ref[...], dy)
-
-
-def grad_out(dy, wo, ot, rows):
-    tokens, model = dy.shape
-    head = wo.shape[0]
-    return pl.pallas_call(
-        dout_body,
-        grid=(tokens // rows,),
-        in_specs=[
-            pl.BlockSpec((rows, model), lambda i: (i, 0)),
-            whole((head, model)),
-            pl.BlockSpec((head, rows), lambda i: (0, i)),
-        ],
-        out_specs=[
-            pl.BlockSpec((rows, head), lambda i: (i, 0)),
-            pl.BlockSpec((head, rows), lambda i: (0, i)),
-            pl.BlockSpec((1, rows), lambda i: (0, i)),
-            whole((head, model)),
-        ],
+        in_specs=[vm] * 5,
+        out_specs=[vm] * 7,
         out_shape=[
+            jax.ShapeDtypeStruct((head, tokens), BF16),
+            jax.ShapeDtypeStruct((1, tokens), F32),
+            jax.ShapeDtypeStruct((1, tokens), F32),
             jax.ShapeDtypeStruct((tokens, head), BF16),
             jax.ShapeDtypeStruct((head, tokens), BF16),
             jax.ShapeDtypeStruct((1, tokens), F32),
             jax.ShapeDtypeStruct((head, model), F32),
         ],
-        compiler_params=params(),
-        cost_estimate=cost(4 * tokens * model * head, 2 * tokens * model),
-        name="dout",
-    )(dy, wo, ot)
+        scratch_shapes=[
+            pltpu.VMEM((tokens, model), BF16),
+            pltpu.VMEM((tokens, blk), F32),
+            pltpu.VMEM((head, blk), F32),
+        ] + Gather.SEMS,
+        compiler_params=params(collective_id=2, has_side_effects=True),
+        cost_estimate=cost(2 * tokens * tokens * head + 4 * tokens * model * head, 8 * tokens * head,
+                           tokens * tokens // 2),
+        name="fwd",
+    )(dy_blk, wo, qt, k, vt)
 
 
 def bwd_body(c2, scale, blk, n, q_ref, qt_ref, k_ref, kt_ref, v_ref, do_ref, dot_ref, m_ref, rl_ref, delta_ref,
@@ -341,12 +497,10 @@
         wk = w_k.reshape(model, head)
         wv = w_v.reshape(model, head)
         wo = wo_loc.reshape(head, model)
-        x = lax.all_gather(x_blk, "tp", axis=0, tiled=True)
-        dy = lax.all_gather(dy_blk, "tp", axis=0, tiled=True)
-        wq_all = lax.all_gather(wq, "tp", axis=0, tiled=False)
-        q, qt, k, kt, v, vt = project_qkv(x, wq, wk, wv, 512)
-        ot, m, rl = attend(qt, k, vt, 512, c2)
-        do, do_t, delta, dwo = grad_out(dy, wo, ot, 512)
+        x, q, qt, k, kt, v, vt = project_qkv(x_blk, wq, wk, wv, n)
+        ot, m, rl, do, do_t, delta, dwo = attend_and_gather(dy_blk, wo, qt, k, vt, n, 512, c2)
+        wq_late, do = lax.optimization_barrier((wq, do))
+        wq_all = lax.all_gather(wq_late, "tp", axis=0, tiled=False)
         dq, dqt, dk, dkt, dv, dvt = grad_attend(q, qt, k, kt, v, do, do_t, m, rl, delta, 512, c2, scale)
         dwq, dwkv = grad_w(x, dqt, dkt, dvt, 512)
         dwkv_blk = lax.psum_scatter(dwkv, "tp", scatter_dimension=0, tiled=True)

time: 387 us -> 427 us (1.10)
  Pallas kernels: 231 us -> 314 us
  waiting for transfers between devices: 125 us -> 80.9 us
    pallas_call x3 -> x2, Pallas kernels: 66.4 us -> 166 us  [the longest x1 85.1 us: project_qkv(): pl.pallas_call(qkv_body, in_specs=[vm] * 4, out_specs=[hbm] + [vm] * 6, o...]
    all_gather x3 -> x1, waiting for transfers between devices: 123 us -> 48.3 us  [local_grads(): wq_all = lax.all_gather(wq_late, 'tp', axis=0, tiled=False)]
    reduce_scatter x1, waiting for transfers between devices: 0.01 us -> 31.9 us  [local_grads(): dwkv_blk = lax.psum_scatter(dwkv, 'tp', scatter_dimension=0, tiled=True)]
    pallas_call x1, Pallas kernels: 101 us -> 84.5 us  [grad_x(): pl.pallas_call(functools.partial(dx_body, n, rows, cols), in_specs=[hbm]...]
    unnamed x4 -> x7, local copies, waits for them, and re-layouts: 13.3 us -> 15.4 us
  transfers between devices with their start and end apart: 4 -> 2, of which waited for: 2 -> 2; matrix products, arithmetic and copies ran while one was open for 3% -> 3% of each run, Pallas kernels for 60% -> 0%
where the time goes in v2:
time: 427 us
  Pallas kernels  314 us (74%)
  waiting for transfers between devices  80.9 us (19%)
  local copies, waits for them, and re-layouts  17.2 us (4%)
  between operations  14.1 us (3%)
    pallas_call x1, Pallas kernels, project_qkv(): pl.pallas_call(qkv_body, in_specs=[vm] * 4, out_specs=[hbm] + [vm] * 6, o...  85.1 us
    pallas_call x1, Pallas kernels, grad_x(): pl.pallas_call(functools.partial(dx_body, n, rows, cols), in_specs=[hbm]...  84.5 us
    pallas_call x1, Pallas kernels, attend_and_gather(): pl.pallas_call(functools.partial(fwd_body, c2, blk), in_specs=[vm] * 5, o...  81 us
    all_gather x1, waiting for transfers between devices, local_grads(): wq_all = lax.all_gather(wq_late, 'tp', axis=0, tiled=False)  48.3 us
    pallas_call x1, Pallas kernels, grad_attend(): pl.pallas_call(functools.partial(bwd_body, c2, scale, blk, tokens // blk)...  44.3 us
    reduce_scatter x1, waiting for transfers between devices, local_grads(): dwkv_blk = lax.psum_scatter(dwkv, 'tp', scatter_dimension=0, tiled=True)  31.9 us
    pallas_call x1, Pallas kernels, grad_w(): pl.pallas_call(dw_body, grid=(model // cols,), in_specs=[pl.BlockSpec((to...  19.4 us
    unnamed x7, local copies, waits for them, and re-layouts  15.4 us
  transfers between devices with their start and end apart: 2, of which 2 were waited for; matrix products, arithmetic and copies ran while one was open for 3% of the time, Pallas kernels for 0%

profile of v2, /device:TPU:0, one launch (start us, length us, event | category | flops | bytes accessed | tf_op | source)
XLA Modules:
  0.0 426.5 jit_solution(9003759289518754483)
XLA Ops:
  7.2 0.0 reduce-scatter.2.cloned.1.call-start
  7.2 85.1 %qkv.1 = (bf16[4096,2048]{1,0:T(8,128)(2,1)}, bf16[4096,256]{1,0:T(8,128)(2,1)}, bf16[256,4096]{1,0:T(8,128)(2,1)}, bf16[4096,256]{1,0:T(8,128)(2,1)}, bf16[256,...) custom-call(bf16[512,2048]{1,0:T(8,128)(2,1)} %x_ref.1, bf16[2048,256]{1,0:T(8,128)(2,1)} %bitcast.9, ...), custom_call_target="tpu_custom_call" | custom-call | flops 12884901888 | bytes 16777216 | tf_op jit(solution)/shard_map/qkv/pallas_call | solution.py:187
  92.3 81.0 %fwd.1 = (bf16[256,4096]{1,0:T(8,128)(2,1)}, f32[1,4096]{1,0:T(1,128)}, f32[1,4096]{1,0:T(1,128)}, bf16[4096,256]{1,0:T(8,128)(2,1)}, bf16[256,4096]{1,0:T(8,128...) custom-call(bf16[512,2048]{1,0:T(8,128)(2,1)} %dy_ref.1, bf16[256,2048]{1,0:T(8,128)(2,1)} %bitcast.12, ...), custom_call_target="tpu_custom_call" | custom-call | flops 17179869184 | bytes 8388608 | tf_op jit(solution)/shard_map/fwd/pallas_call | solution.py:290
  173.3 44.3 %bwd.1 = (bf16[4096,256]{1,0:T(8,128)(2,1)}, bf16[256,4096]{1,0:T(8,128)(2,1)}, bf16[4096,256]{1,0:T(8,128)(2,1)}, bf16[256,4096]{1,0:T(8,128)(2,1)}, bf16[4096,...) custom-call(bf16[4096,256]{1,0:T(8,128)(2,1)} %get-tuple-element.28.q_ref, bf16[256,4096]{1,0:T(8,128)(2,1)} %get-tuple-element.29.qt_ref, ...), custom_call_target="tpu_custom_call" | custom-call | flops 21474836480 | bytes 16777216 | tf_op jit(solution)/shard_map/bwd/pallas_call | solution.py:374
  217.6 19.4 %dw.1 = (f32[2048,256]{1,0:T(8,128)}, f32[2048,512]{1,0:T(8,128)}) custom-call(bf16[4096,2048]{1,0:T(8,128)(2,1)} %get-tuple-element.44.x_ref, bf16[256,4096]{1,0:T(8,128)(2,1)} %get-tuple-element.45.dqt_ref, bf16[256,4096]{1,0:T(8,128)(2,1)} %get-tuple-element.46.dkt_ref, bf16[256,4096]{1,0:T(8,128)(2,1)} %get-tuple-element.47.dvt_ref), custom_call_target="tpu_custom_call" | custom-call | flops 12884901888 | bytes 16777216 | tf_op jit(solution)/shard_map/dw/pallas_call | solution.py:397
  237.0 0.0 copy-start.1
  237.0 0.0 reduce-scatter.2.cloned.1.call-update
  237.0 0.0 all-gather.3.cloned.1.call-start
  237.1 0.7 all-gather.3.cloned.1.call-update
  237.8 0.8 copy-done.1
  238.6 9.9 %copy.11 = f32[2048,1,256]{2,1,0:T(1,128)} copy(f32[2048,1,256]{2,0,1:T(8,128)S(1)} %bitcast.8) | data formatting | bytes 4194304
  248.5 31.9 %reduce-scatter.2.cloned.1.call-done = f32[256,512]{1,0:T(8,128)} async-done(((f32[2048,512]{1,0:T(8,128)}), f32[256,512]{1,0:T(8,128)}) %reduce-scatter.2.cloned.1.call-update) | async-done | bytes 524304 | tf_op jit(solution)/shard_map/reduce_scatter | solution.py:506
  280.4 1.9 fusion
  282.2 48.3 %all-gather.3.cloned.1.call-done = bf16[16384,256]{1,0:T(8,128)(2,1)} async-done(((bf16[2048,256]{1,0:T(8,128)(2,1)}), bf16[16384,256]{1,0:T(8,128)(2,1)}) %all-gather.3.cloned.1.call-update) | async-done | bytes 8388624 | tf_op jit(solution)/shard_map/all_gather | solution.py:503
  330.5 84.5 %dx.1 = bf16[512,2048]{1,0:T(8,128)(2,1)} custom-call(bf16[4096,256]{1,0:T(8,128)(2,1)} %get-tuple-element.40.dq_ref, bf16[4096,256]{1,0:T(8,128)(2,1)} %get-tuple-element.41.dk_ref, bf16[4096,256]{1,0:T(8,128)(2,1)} %get-tuple-element.42.dv_ref, bf16[8,2048,256]{2,1,0:T(8,128)(2,1)} %bitcast.11, bf16[2048,256]{1,0:T(8,128)(2,1)} %bitcast.14, ...), custom_call_target="tpu_custom_call" | custom-call | flops 60000002048 | bytes 16000000 | tf_op jit(solution)/shard_map/dx/pallas_call | solution.py:471
  415.1 0.0 copy-start
  415.1 3.3 copy.14
  418.4 0.0 copy-done
  418.4 1.3 copy.15
Async XLA Ops:
  7.2 273.2 %reduce-scatter.2.cloned.1.call-start = ((), (), s32[]{:S(2)}) async-start(), calls=%async_computation.1 | async-start | bytes 4718592 | tf_op jit(solution)/shard_map/reduce_scatter | solution.py:506
  237.0 1.6 copy-start.1
  237.0 93.5 %all-gather.3.cloned.1.call-start = ((), (), s32[]{:S(2)}) async-start(), calls=%async_computation.2 | async-start | bytes 9437184 | tf_op jit(solution)/shard_map/all_gather | solution.py:503
  415.1 3.3 copy-start
Sparse Core Ops, SparseCore 0:
  237.1 43.1 reduce-scatter.1
  282.2 48.3 all-gather.2

commit v3 on v2

--- a/solution.py
+++ b/solution.py
@@ -71,9 +71,8 @@
         )
 
     def push(self, src, shard, q, slot, to):
-        copy = self.copy(src, shard, q, slot, to)
-        copy.start()
-        self.sent.append(copy)
+        self.copy(src, shard, q, slot, to).start()
+        self.sent.append((slot, q))
 
     def start(self):
         for s in range(self.CHUNKS):
@@ -112,8 +111,8 @@
         return self.xn + (self.yn - self.xn) * (k // 2) + self.flip * (k % 2)
 
     def finish(self):
-        for copy in self.sent:
-            copy.wait_send()
+        for slot, q in self.sent:
+            self.copy(self.full.at[self.at(self.me, q), :], self.me, q, slot, self.sib).wait_send()
 
 
 def qkv_body(x_ref, wq_ref, wk_ref, wv_ref, full_ref, q_ref, qt_ref, k_ref, kt_ref, v_ref, vt_ref,
@@ -312,13 +311,47 @@
     )(dy_blk, wo, qt, k, vt)
 
 
-def bwd_body(c2, scale, blk, n, q_ref, qt_ref, k_ref, kt_ref, v_ref, do_ref, dot_ref, m_ref, rl_ref, delta_ref,
-             dq_ref, dqt_ref, dk_ref, dkt_ref, dv_ref, dvt_ref, dk_acc, dv_acc, dq_acc):
+def enter_all(n):
+    me = lax.axis_index("tp")
+    barrier = pltpu.get_barrier_semaphore()
+    for p in range(1, n):
+        pl.semaphore_signal(barrier, inc=1, device_id={"tp": lax.rem(me + p, n)}, device_id_type=pl.DeviceIdType.MESH)
+    pl.semaphore_wait(barrier, n - 1)
+    return me
+
+
+def remote(src, dst, send, recv, to):
+    return pltpu.make_async_remote_copy(
+        src_ref=src, dst_ref=dst, send_sem=send, recv_sem=recv, device_id={"tp": to},
+        device_id_type=pl.DeviceIdType.MESH,
+    )
+
+
+def bwd_body(c2, scale, blk, n, cols, q_ref, qt_ref, k_ref, kt_ref, v_ref, do_ref, dot_ref, m_ref, rl_ref, delta_ref,
+             wq_ref, x_ref, dq_ref, wq_all, got, dwq_ref, dwkv_ref,
+             nat, tra, dk_acc, dv_acc, dq_acc, xs, dwq_s, send, recv, send_kv, recv_kv, load, store, local):
+    head = q_ref.shape[1]
+    model = x_ref.shape[1]
+    me = enter_all(n)
+    g = Gather(wq_ref, wq_all, send, recv)
+    g.start()
+    own_w = pltpu.make_async_copy(wq_ref, wq_all.at[pl.ds(pl.multiple_of(me * model, model), model), :], local.at[0])
+    own_w.start()
+
+    def fetch(b):
+        at = pl.ds(pl.multiple_of(b * cols, cols), cols)
+        return pltpu.make_async_copy(x_ref.at[:, at], xs.at[b % 2], load.at[b % 2])
+
+    fetch(0).start()
+    fetch(1).start()
     dq_acc[...] = jnp.zeros_like(dq_acc)
 
+    def rows(j):
+        return pl.ds(pl.multiple_of(j * blk, blk), blk)
+
     def pair(j, i, masked):
-        at_k = pl.ds(pl.multiple_of(j * blk, blk), blk)
-        at_q = pl.ds(pl.multiple_of(i * blk, blk), blk)
+        at_k = rows(j)
+        at_q = rows(i)
         s = dot(k_ref[at_k, :], qt_ref[:, at_q])
         p = jnp.exp2(s * c2 - m_ref[:, at_q]) * rl_ref[:, at_q]
         if masked:
@@ -337,7 +370,16 @@
             dv_acc[...] += dv
             dk_acc[...] += dk
 
-    def column(j, _):
+    def kv_copy(t, p, to):
+        return remote(nat.at[t, rows(to), :], got.at[t, p], send_kv.at[t, p], recv_kv.at[t, p], to)
+
+    def send_block(p):
+        to = lax.rem(me + p, n)
+        for t in range(2):
+            kv_copy(t, p, to).start()
+
+    def column(step, _):
+        j = lax.rem(me + step, n)
         pair(j, j, True)
 
         def rest(i, _):
@@ -345,65 +387,112 @@
             return 0
 
         lax.fori_loop(j + 1, n, rest, 0)
-        at_k = pl.ds(pl.multiple_of(j * blk, blk), blk)
-        dk = dk_acc[...] * scale
-        dv = dv_acc[...]
-        dk_ref[at_k, :] = dk.astype(BF16)
-        dv_ref[at_k, :] = dv.astype(BF16)
-        dkt_ref[:, at_k] = dk.T.astype(BF16)
-        dvt_ref[:, at_k] = dv.T.astype(BF16)
+        at_k = rows(j)
+        for t, grad in ((0, dk_acc[...] * scale), (1, dv_acc[...])):
+            nat[t, at_k, :] = grad.astype(BF16)
+            tra[pl.ds((t + 1) * head, head), at_k] = grad.T.astype(BF16)
+
+        for s, when in ((0, 1), (1, 2), (2, 4), (3, 5)):
+            @pl.when(step == when)
+            def _(s=s):
+                g.step(s)
+
+        @pl.when(step >= 2)
+        def _():
+            send_block(step - 1)
+
         return 0
 
     lax.fori_loop(0, n, column, 0)
 
     def finish(i, _):
-        at = pl.ds(pl.multiple_of(i * blk, blk), blk)
-        dq = dq_acc[:, at] * scale
-        dqt_ref[:, at] = dq.astype(BF16)
-        dq_ref[at, :] = dq.T.astype(BF16)
+        dq = dq_acc[:, rows(i)] * scale
+        tra[pl.ds(0, head), rows(i)] = dq.astype(BF16)
+        dq_ref[rows(i), :] = dq.T.astype(BF16)
         return 0
 
     lax.fori_loop(0, n, finish, 0)
-
-
-def grad_attend(q, qt, k, kt, v, do, do_t, m, rl, delta, blk, c2, scale):
+    send_block(n - 1)
+    own = [pltpu.make_async_copy(nat.at[t, rows(me), :], got.at[t, 0], local.at[1 + t]) for t in range(2)]
+    for copy in own:
+        copy.start()
+    g.last(0)
+    g.last(1)
+
+    def put(b):
+        at = pl.ds(pl.multiple_of(b * cols, cols), cols)
+        return pltpu.make_async_copy(dwq_s.at[b % 2], dwq_ref.at[at, 0, :], store.at[b % 2])
+
+    def weights(b, _):
+        at = pl.ds(pl.multiple_of(b * cols, cols), cols)
+        fetch(b).wait()
+        grad = dot(tra[...], xs[b % 2]).T
+
+        @pl.when(b + 2 < model // cols)
+        def _():
+            fetch(b + 2).start()
+
+        @pl.when(b >= 2)
+        def _():
+            put(b - 2).wait()
+
+        dwq_s[b % 2] = grad[:, :head]
+        dwkv_ref[at, :] = grad[:, head:]
+        put(b).start()
+        return 0
+
+    lax.fori_loop(0, model // cols, weights, 0)
+    for b in (model // cols - 2, model // cols - 1):
+        put(b).wait()
+    for slot in (3, 4, 5, 6):
+        g.from_sib(slot)
+    g.finish()
+    own_w.wait()
+    for copy in own:
+        copy.wait()
+    for t in range(2):
+        for p in range(1, n):
+            copy = kv_copy(t, p, lax.rem(me + p, n))
+            copy.wait_send()
+            copy.wait_recv()
+
+
+def grad_attend(q, qt, k, kt, v, do, do_t, m, rl, delta, wq, x, n, c2, scale, cols):
     tokens, head = q.shape
-    nat = jax.ShapeDtypeStruct((tokens, head), BF16)
-    tra = jax.ShapeDtypeStruct((head, tokens), BF16)
+    model = x.shape[1]
+    blk = tokens // n
     vm = pl.BlockSpec(memory_space=pltpu.VMEM)
+    hbm = pl.BlockSpec(memory_space=pl.ANY)
     return pl.pallas_call(
-        functools.partial(bwd_body, c2, scale, blk, tokens // blk),
-        in_specs=[vm] * 10,
-        out_specs=[vm] * 6,
-        out_shape=[nat, tra] * 3,
-        scratch_shapes=[pltpu.VMEM((blk, head), F32)] * 2 + [pltpu.VMEM((head, tokens), F32)],
-        compiler_params=params(),
+        functools.partial(bwd_body, c2, scale, blk, n, cols),
+        in_specs=[vm] * 11 + [hbm],
+        out_specs=[vm, hbm, hbm, hbm, vm],
+        out_shape=[
+            jax.ShapeDtypeStruct((tokens, head), BF16),
+            jax.ShapeDtypeStruct((n * model, head), BF16),
+            jax.ShapeDtypeStruct((2, n, blk, head), BF16),
+            jax.ShapeDtypeStruct((model, 1, head), F32),
+            jax.ShapeDtypeStruct((model, 2 * head), F32),
+        ],
+        scratch_shapes=[
+            pltpu.VMEM((2, tokens, head), BF16),
+            pltpu.VMEM((3 * head, tokens), BF16),
+            pltpu.VMEM((blk, head), F32),
+            pltpu.VMEM((blk, head), F32),
+            pltpu.VMEM((head, tokens), F32),
+            pltpu.VMEM((2, tokens, cols), BF16),
+            pltpu.VMEM((2, cols, head), F32),
+        ] + Gather.SEMS + [
+            pltpu.SemaphoreType.DMA((2, n)),
+            pltpu.SemaphoreType.DMA((2, n)),
+            pltpu.SemaphoreType.DMA((2,)),
+            pltpu.SemaphoreType.DMA((2,)),
+            pltpu.SemaphoreType.DMA((3,)),
+        ],
+        compiler_params=params(collective_id=3, has_side_effects=True),
         cost_estimate=cost(5 * tokens * tokens * head, 16 * tokens * head, tokens * tokens // 2),
         name="bwd",
-    )(q, qt, k, kt, v, do, do_t, m, rl, delta)
-
-
-def dw_body(x_ref, dqt_ref, dkt_ref, dvt_ref, dwq_ref, dwkv_ref):
-    x = x_ref[...]
-    head = dqt_ref.shape[0]
-    dwq_ref[...] = dot(dqt_ref[...], x).T
-    dwkv_ref[:, :head] = dot(dkt_ref[...], x).T
-    dwkv_ref[:, head:] = dot(dvt_ref[...], x).T
-
-
-def grad_w(x, dqt, dkt, dvt, cols):
-    tokens, model = x.shape
-    head = dqt.shape[0]
-    return pl.pallas_call(
-        dw_body,
-        grid=(model // cols,),
-        in_specs=[pl.BlockSpec((tokens, cols), lambda i: (0, i))] + [whole((head, tokens))] * 3,
-        out_specs=[pl.BlockSpec((cols, head), lambda i: (i, 0)), pl.BlockSpec((cols, 2 * head), lambda i: (i, 0))],
-        out_shape=[jax.ShapeDtypeStruct((model, head), F32), jax.ShapeDtypeStruct((model, 2 * head), F32)],
-        compiler_params=params(),
-        cost_estimate=cost(6 * tokens * model * head, 2 * tokens * model),
-        name="dw",
-    )(x, dqt, dkt, dvt)
+    )(q, qt, k, kt, v, do, do_t, m, rl, delta, wq, x)
 
 
 def split3(x):
@@ -414,76 +503,160 @@
     return hi, mid, lo
 
 
-def dx_body(n, rows, cols, dq_ref, dk_ref, dv_ref, wq_ref, wk_ref, wv_ref, dx_ref, got, parts, send, recv, local):
-    me = lax.axis_index("tp")
-    barrier = pltpu.get_barrier_semaphore()
-    for p in range(1, n):
-        pl.semaphore_signal(barrier, inc=1, device_id={"tp": lax.rem(me + p, n)}, device_id_type=pl.DeviceIdType.MESH)
-    pl.semaphore_wait(barrier, n - 1)
-    copies = []
-    for t, src in enumerate((dk_ref, dv_ref, dq_ref)):
+def dx_body(n, cols, dq_ref, got_hbm, wq_hbm, wk_ref, wv_ref, dwkv_ref, dx_ref, dwk_ref, dwv_ref,
+            gq, gkv, wq_s, parts, acc, r0, r1, r2, sum1, sum2,
+            send, recv, s0, e0, s1, e1, s2, e2, load):
+    rows, head = gq.shape[1], gq.shape[2]
+    model = wk_ref.shape[0]
+    part = dwkv_ref.shape[0] // n
+    me = enter_all(n)
+    c, x, y = me % 2, (me // 2) % 2, me // 4
+    xn = me + 2 - 4 * x
+    yn = me + 4 - 8 * y
+    dg = xn + 4 - 8 * y
+    flip = 1 - 2 * c
+    sib = me + flip
+    chips = (me, xn, yn, dg)
+
+    def at(dev, size):
+        return pl.ds(pl.multiple_of(dev * size, size), size)
+
+    first = [remote(dwkv_ref.at[at(d + flip, part), :], r0.at[i], s0.at[i], e0.at[i], sib)
+             for i, d in enumerate(chips)]
+    for copy in first:
+        copy.start()
+
+    def q_copy(p):
+        to = lax.rem(me + p, n)
+        return remote(dq_ref.at[at(to, rows), :], gq.at[p], send.at[p], recv.at[p], to)
+
+    loads = [pltpu.make_async_copy(got_hbm, gkv, load.at[0]), pltpu.make_async_copy(wq_hbm, wq_s, load.at[1]),
+             pltpu.make_async_copy(dq_ref.at[at(me, rows), :], gq.at[0], load.at[2])]
+    for copy in loads:
+        copy.start()
+    order = (4, 2, 6, 1, 3, 5, 7)
+    early = 3
+    for p in order[:early]:
+        q_copy(p).start()
+
+    for copy in first:
+        copy.wait_recv()
+    for i, d in enumerate(chips):
+        sum1[i] = dwkv_ref[at(d, part), :] + r0[i]
+
+    loads[0].wait()
+    for t in range(2):
+        total = gkv[t, 0].astype(F32)
         for p in range(1, n):
-            to = lax.rem(me + p, n)
-            copy = pltpu.make_async_remote_copy(
-                src_ref=src.at[pl.ds(pl.multiple_of(to * rows, rows), rows), :],
-                dst_ref=got.at[t, p],
-                send_sem=send.at[t, p],
-                recv_sem=recv.at[t, p],
-                device_id={"tp": to},
-                device_id_type=pl.DeviceIdType.MESH,
-            )
-            copy.start()
-            copies.append(copy)
-        own = pltpu.make_async_copy(src.at[pl.ds(pl.multiple_of(me * rows, rows), rows), :], got.at[t, 0], local.at[t])
-        own.start()
-        copies.append(own)
-    for copy in copies:
-        copy.wait()
-    for t in range(2):
-        total = got[t, 0].astype(F32)
-        for p in range(1, n):
-            total += got[t, p].astype(F32)
-        for e, part in enumerate(split3(total)):
-            parts[t, e] = part
-
-    def column(b, _):
-        at = pl.ds(pl.multiple_of(b * cols, cols), cols)
-        acc = None
+            total += gkv[t, p].astype(F32)
+        for e, piece in enumerate(split3(total)):
+            parts[t, e] = piece
+
+    k_cols, v_cols = pl.ds(0, head), pl.ds(head, head)
+    second = [
+        remote(sum1.at[3, :, k_cols], r1.at[0, 1], s1.at[0, 1], e1.at[0, 1], xn),
+        remote(sum1.at[3, :, v_cols], r1.at[1, 1], s1.at[1, 1], e1.at[1, 1], yn),
+        remote(sum1.at[1, :, k_cols], r1.at[0, 0], s1.at[0, 0], e1.at[0, 0], xn),
+        remote(sum1.at[2, :, v_cols], r1.at[1, 0], s1.at[1, 0], e1.at[1, 0], yn),
+    ]
+    for copy in second:
+        copy.start()
+    for p in order[early:]:
+        q_copy(p).start()
+
+    loads[1].wait()
+    loads[2].wait()
+
+    def kv_part(b, _):
+        cs = pl.ds(pl.multiple_of(b * cols, cols), cols)
+        total = None
         for t, w_ref in ((0, wk_ref), (1, wv_ref)):
-            w = w_ref[at, :]
+            w = w_ref[cs, :]
             for e in range(3):
                 d = dot(parts[t, e], w, NT)
-                acc = d if acc is None else acc + d
-        for p in range(n):
-            acc += dot(got[2, p], wq_ref[lax.rem(me + n - p, n), at, :], NT)
-        dx_ref[:, at] = acc.astype(BF16)
+                total = d if total is None else total + d
+        acc[:, cs] = total + dot(gq[0], wq_s[pl.ds(pl.multiple_of(me * model + b * cols, cols), cols), :], NT)
         return 0
 
-    lax.fori_loop(0, wk_ref.shape[0] // cols, column, 0)
-
-
-def grad_x(dq, dk, dv, wq_all, wk, wv, n, cols):
+    lax.fori_loop(0, model // cols, kv_part, 0)
+
+    def q_part(p):
+        owner = lax.rem(me + n - p, n)
+
+        def body(b, _):
+            cs = pl.ds(pl.multiple_of(b * cols, cols), cols)
+            acc[:, cs] += dot(gq[p], wq_s[pl.ds(pl.multiple_of(owner * model + b * cols, cols), cols), :], NT)
+            return 0
+
+        q_copy(p).wait_recv()
+        lax.fori_loop(0, model // cols, body, 0)
+
+    for p in order[:early]:
+        q_part(p)
+
+    second[0].wait_recv()
+    sum2[0] = sum1[2, :, :head] + r1[0, 1]
+    second[1].wait_recv()
+    sum2[1] = sum1[1, :, head:] + r1[1, 1]
+    for p in order[early:early + 1]:
+        q_part(p)
+    third = [
+        remote(sum2.at[0], r2.at[0], s2.at[0], e2.at[0], yn),
+        remote(sum2.at[1], r2.at[1], s2.at[1], e2.at[1], xn),
+    ]
+    for copy in third:
+        copy.start()
+    for p in order[early + 1:]:
+        q_part(p)
+    dx_ref[...] = acc[...].astype(BF16)
+    second[2].wait_recv()
+    second[3].wait_recv()
+    third[0].wait_recv()
+    third[1].wait_recv()
+    dwk_ref[...] = (sum1[0, :, :head] + r1[0, 0]) + r2[0]
+    dwv_ref[...] = (sum1[0, :, head:] + r1[1, 0]) + r2[1]
+    for copy in first + second + third:
+        copy.wait_send()
+    for p in range(1, n):
+        q_copy(p).wait_send()
+
+
+def grad_x(dq, got, wq_all, wk, wv, dwkv, n, cols):
     tokens, head = dq.shape
     model = wk.shape[0]
-    rows = tokens // n
+    rows, part = tokens // n, model // n
     hbm = pl.BlockSpec(memory_space=pl.ANY)
     vm = pl.BlockSpec(memory_space=pltpu.VMEM)
     return pl.pallas_call(
-        functools.partial(dx_body, n, rows, cols),
-        in_specs=[hbm] * 3 + [vm] * 3,
-        out_specs=vm,
-        out_shape=jax.ShapeDtypeStruct((rows, model), BF16),
+        functools.partial(dx_body, n, cols),
+        in_specs=[vm, hbm, hbm, vm, vm, vm],
+        out_specs=[vm] * 3,
+        out_shape=[jax.ShapeDtypeStruct((rows, model), BF16)] + [jax.ShapeDtypeStruct((part, head), F32)] * 2,
         scratch_shapes=[
-            pltpu.VMEM((3, n, rows, head), BF16),
+            pltpu.VMEM((n, rows, head), BF16),
+            pltpu.VMEM((2, n, rows, head), BF16),
+            pltpu.VMEM((n * model, head), BF16),
             pltpu.VMEM((2, 3, rows, head), BF16),
-            pltpu.SemaphoreType.DMA((3, n)),
-            pltpu.SemaphoreType.DMA((3, n)),
+            pltpu.VMEM((rows, model), F32),
+            pltpu.VMEM((4, part, 2 * head), F32),
+            pltpu.VMEM((2, 2, part, head), F32),
+            pltpu.VMEM((2, part, head), F32),
+            pltpu.VMEM((4, part, 2 * head), F32),
+            pltpu.VMEM((2, part, head), F32),
+            pltpu.SemaphoreType.DMA((n,)),
+            pltpu.SemaphoreType.DMA((n,)),
+            pltpu.SemaphoreType.DMA((4,)),
+            pltpu.SemaphoreType.DMA((4,)),
+            pltpu.SemaphoreType.DMA((2, 2)),
+            pltpu.SemaphoreType.DMA((2, 2)),
+            pltpu.SemaphoreType.DMA((2,)),
+            pltpu.SemaphoreType.DMA((2,)),
             pltpu.SemaphoreType.DMA((3,)),
         ],
         compiler_params=params(collective_id=0, has_side_effects=True),
-        cost_estimate=cost(60e9, 16e6),
+        cost_estimate=cost(8 * rows * n * model * head, 16e6),
         name="dx",
-    )(dq, dk, dv, wq_all, wk, wv)
+    )(dq, got, wq_all, wk, wv, dwkv)
 
 
 def solution(mesh):
@@ -499,13 +672,9 @@
         wo = wo_loc.reshape(head, model)
         x, q, qt, k, kt, v, vt = project_qkv(x_blk, wq, wk, wv, n)
         ot, m, rl, do, do_t, delta, dwo = attend_and_gather(dy_blk, wo, qt, k, vt, n, 512, c2)
-        wq_late, do = lax.optimization_barrier((wq, do))
-        wq_all = lax.all_gather(wq_late, "tp", axis=0, tiled=False)
-        dq, dqt, dk, dkt, dv, dvt = grad_attend(q, qt, k, kt, v, do, do_t, m, rl, delta, 512, c2, scale)
-        dwq, dwkv = grad_w(x, dqt, dkt, dvt, 512)
-        dwkv_blk = lax.psum_scatter(dwkv, "tp", scatter_dimension=0, tiled=True)
-        dx = grad_x(dq, dk, dv, wq_all, wk, wv, n, 512)
-        return (dx, dwq.reshape(model, 1, head), dwo.reshape(1, head, model), dwkv_blk[:, :head], dwkv_blk[:, head:])
+        dq, wq_all, got, dwq, dwkv = grad_attend(q, qt, k, kt, v, do, do_t, m, rl, delta, wq, x, n, c2, scale, 256)
+        dx, dwk, dwv = grad_x(dq, got, wq_all, wk, wv, dwkv, n, 512)
+        return dx, dwq, dwo.reshape(1, head, model), dwk, dwv
 
     tok_spec = P(("dp", "tp"))
     return jax.shard_map(

time: 427 us -> 315 us (0.74)
  waiting for transfers between devices: 80.9 us -> 0 us
  between operations: 14.1 us -> 0.68 us
  local copies, waits for them, and re-layouts: 17.2 us -> 8.39 us
  Pallas kernels: 314 us -> 306 us
    all_gather x1 -> x0, waiting for transfers between devices: 48.3 us -> none  [local_grads(): wq_all = lax.all_gather(wq_late, 'tp', axis=0, tiled=False)]
    reduce_scatter x1 -> x0, waiting for transfers between devices: 31.9 us -> none  [local_grads(): dwkv_blk = lax.psum_scatter(dwkv, 'tp', scatter_dimension=0, tiled=True)]
    pallas_call x3 -> x2, Pallas kernels: 148 us -> 140 us  [the longest x1 90.5 us: grad_attend(): pl.pallas_call(functools.partial(bwd_body, c2, scale, blk, n, cols), in_s...]
    unnamed x7 -> x13, local copies, waits for them, and re-layouts: 15.4 us -> 8.39 us
  transfers between devices with their start and end apart: 2 -> 0, of which waited for: 2 -> 0; matrix products, arithmetic and copies ran while one was open for 3% -> 0% of each run, Pallas kernels for 0% -> 0%
where the time goes in v3:
time: 315 us
  Pallas kernels  306 us (97%)
  local copies, waits for them, and re-layouts  8.39 us (3%)
    pallas_call x1, Pallas kernels, grad_attend(): pl.pallas_call(functools.partial(bwd_body, c2, scale, blk, n, cols), in_s...  90.5 us
    pallas_call x1, Pallas kernels, project_qkv(): pl.pallas_call(qkv_body, in_specs=[vm] * 4, out_specs=[hbm] + [vm] * 6, o...  85.2 us
    pallas_call x1, Pallas kernels, attend_and_gather(): pl.pallas_call(functools.partial(fwd_body, c2, blk), in_specs=[vm] * 5, o...  80.9 us
    pallas_call x1, Pallas kernels, grad_x(): pl.pallas_call(functools.partial(dx_body, n, cols), in_specs=[vm, hbm, hb...  49.3 us
    unnamed x13, local copies, waits for them, and re-layouts  8.39 us

profile of v3, /device:TPU:0, one launch (start us, length us, event | category | flops | bytes accessed | tf_op | source)
XLA Modules:
  0.0 314.9 jit_solution(14901146974514958806)
XLA Ops:
  0.6 85.2 %qkv.1 = (bf16[4096,2048]{1,0:T(8,128)(2,1)}, bf16[4096,256]{1,0:T(8,128)(2,1)}, bf16[256,4096]{1,0:T(8,128)(2,1)}, bf16[4096,256]{1,0:T(8,128)(2,1)}, bf16[256,...) custom-call(bf16[512,2048]{1,0:T(8,128)(2,1)} %x_ref.1, bf16[2048,256]{1,0:T(8,128)(2,1)} %bitcast.7, ...), custom_call_target="tpu_custom_call" | custom-call | flops 12884901888 | bytes 16777216 | tf_op jit(solution)/shard_map/qkv/pallas_call | solution.py:186
  85.9 80.9 %fwd.1 = (bf16[256,4096]{1,0:T(8,128)(2,1)}, f32[1,4096]{1,0:T(1,128)}, f32[1,4096]{1,0:T(1,128)}, bf16[4096,256]{1,0:T(8,128)(2,1)}, bf16[256,4096]{1,0:T(8,128...) custom-call(bf16[512,2048]{1,0:T(8,128)(2,1)} %dy_ref.1, bf16[256,2048]{1,0:T(8,128)(2,1)} %bitcast.6, ...), custom_call_target="tpu_custom_call" | custom-call | flops 17179869184 | bytes 8388608 | tf_op jit(solution)/shard_map/fwd/pallas_call | solution.py:289
  166.7 90.5 %bwd.1 = (bf16[4096,256]{1,0:T(8,128)(2,1)}, bf16[16384,256]{1,0:T(8,128)(2,1)}, bf16[2,8,512,256]{3,2,1,0:T(8,128)(2,1)}, f32[2048,1,256]{2,1,0:T(1,128)}, f32[2048,512]{1,0:T(8,128)}) custom-call(bf16[4096,256]{1,0:T(8,128)(2,1)} %get-tuple-element.26.q_ref, bf16[256,4096]{1,0:T(8,128)(2,1)} %get-tuple-element.27.qt_ref, ...), custom_call_target="tpu_custom_call" | custom-call | flops 21474836480 | bytes 16777216 | tf_op jit(solution)/shard_map/bwd/pallas_call | solution.py:466
  257.2 49.3 %dx.1 = (bf16[512,2048]{1,0:T(8,128)(2,1)}, f32[256,256]{1,0:T(8,128)}, f32[256,256]{1,0:T(8,128)}) custom-call(bf16[4096,256]{1,0:T(8,128)(2,1)} %get-tuple-element.38.dq_ref, bf16[2,8,512,256]{3,2,1,0:T(8,128)(2,1)} %get-tuple-element.39.got_hbm, bf16[16384,256]{1,0:T(8,128)(2,1)} %get-tuple-element.40.wq_hbm, bf16[2048,256]{1,0:T(8,128)(2,1)} %bitcast.10, ...), custom_call_target="tpu_custom_call" | custom-call | flops 17179869184 | bytes 16000000 | tf_op jit(solution)/shard_map/dx/pallas_call | solution.py:630
  306.5 0.0 copy-start.1
  306.5 3.3 %copy.16 = bf16[512,2048]{1,0:T(8,128)(2,1)} copy(bf16[512,2048]{1,0:T(8,128)(2,1)} %get-tuple-element.52) | data formatting | bytes 4194304
  309.8 0.0 copy-done.1
  309.8 0.0 copy-start
  309.8 1.3 copy.17
  311.2 1.0 copy-done
  312.2 0.0 copy-start.3
  312.2 0.0 copy-start.2
  312.2 1.3 copy.18
  313.5 0.0 copy-done.3
  313.5 0.7 copy.19
  314.2 0.0 copy-done.2
  314.2 0.7 copy.20
Async XLA Ops:
  306.5 3.3 %copy-start.1 = (f32[2048,1,256]{2,1,0:T(1,128)S(1)}, f32[2048,1,256]{2,1,0:T(1,128)}, u32[]{:S(2)}) copy-start(f32[2048,1,256]{2,1,0:T(1,128)} %get-tuple-element.53) | copy-start | bytes 6291460
  309.8 2.3 copy-start
  312.2 1.3 copy-start.3
  312.2 2.0 copy-start.2

commit v4 on v3

v4 whole, which is shorter than its diff:
```python
import functools

import jax
import jax.numpy as jnp
from jax import lax
from jax.experimental import pallas as pl
from jax.experimental.pallas import tpu as pltpu
from jax.sharding import PartitionSpec as P

F32 = jnp.float32
BF16 = jnp.bfloat16
LOG2E = 1.4426950408889634
VMEM_BYTES = 60 * 1024 * 1024
NN = (((1,), (0,)), ((), ()))
NT = (((1,), (1,)), ((), ()))


def dot(a, b, dims=NN):
    return lax.dot_general(a, b, dims, preferred_element_type=F32)


def cost(flops, bytes_accessed, trans=0):
    return pl.CostEstimate(flops=int(flops), bytes_accessed=int(bytes_accessed), transcendentals=int(trans))


def params(**kw):
    return pltpu.CompilerParams(vmem_limit_bytes=VMEM_BYTES, **kw)


def whole(shape):
    return pl.BlockSpec(shape, lambda *_: (0,) * len(shape))


class Gather:
    CHUNKS = 4
    X_ORDER = (0, 1, 2, 3)
    Y_ORDER = (2, 3, 0, 1)
    SEMS = [pltpu.SemaphoreType.DMA((7, CHUNKS)), pltpu.SemaphoreType.DMA((7, CHUNKS))]

    def __init__(self, own_ref, full_ref, send, recv):
        me = lax.axis_index("tp")
        c, x, y = me % 2, (me // 2) % 2, me // 4
        self.me = me
        self.xn = me + 2 - 4 * x
        self.yn = me + 4 - 8 * y
        self.dg = self.xn + 4 - 8 * y
        self.flip = 1 - 2 * c
        self.sib = me + self.flip
        self.own, self.full, self.send, self.recv = own_ref, full_ref, send, recv
        self.rows = own_ref.shape[0]
        self.piece = self.rows // self.CHUNKS
        self.sent = []

    def at(self, dev, q):
        return pl.ds(pl.multiple_of(dev * self.rows + q * self.piece, self.piece), self.piece)

    def copy(self, src, shard, q, slot, to):
        return pltpu.make_async_remote_copy(
            src_ref=src,
            dst_ref=self.full.at[self.at(shard, q), :],
            send_sem=self.send.at[slot, q],
            recv_sem=self.recv.at[slot, q],
            device_id={"tp": to},
            device_id_type=pl.DeviceIdType.MESH,
        )

    def push(self, src, shard, q, slot, to):
        self.copy(src, shard, q, slot, to).start()
        self.sent.append((slot, q))

    def start(self):
        for s in range(self.CHUNKS):
            for slot, to, q in ((0, self.xn, self.X_ORDER[s]), (1, self.yn, self.Y_ORDER[s]), (3, self.sib, s)):
                self.push(self.own.at[pl.ds(q * self.piece, self.piece), :], self.me, q, slot, to)

    def take(self, shard, q, slot):
        self.copy(self.full.at[self.at(shard, q), :], shard, q, slot, self.sib).wait_recv()

    def hand(self, shard, q, slot, to):
        self.push(self.full.at[self.at(shard, q), :], shard, q, slot, to)

    def step(self, s):
        q = self.X_ORDER[s]
        self.take(self.xn, q, 0)
        if s < 2:
            self.hand(self.xn, q, 2, self.yn)
        self.hand(self.xn, q, 4, self.sib)
        q = self.Y_ORDER[s]
        self.take(self.yn, q, 1)
        if s < 2:
            self.hand(self.yn, q, 2, self.xn)
        self.hand(self.yn, q, 5, self.sib)

    def last(self, s):
        for q in (self.Y_ORDER[s], self.X_ORDER[s]):
            self.take(self.dg, q, 2)
            self.hand(self.dg, q, 6, self.sib)

    def from_sib(self, slot, qs=range(CHUNKS)):
        shard = {3: self.me, 4: self.xn, 5: self.yn, 6: self.dg}[slot] + self.flip
        for q in qs:
            self.take(shard, q, slot)

    def near(self, k):
        return self.xn + (self.yn - self.xn) * (k // 2) + self.flip * (k % 2)

    def finish(self):
        for slot, q in self.sent:
            self.copy(self.full.at[self.at(self.me, q), :], self.me, q, slot, self.sib).wait_send()


def enter_all(n):
    me = lax.axis_index("tp")
    barrier = pltpu.get_barrier_semaphore()
    for p in range(1, n):
        pl.semaphore_signal(barrier, inc=1, device_id={"tp": lax.rem(me + p, n)}, device_id_type=pl.DeviceIdType.MESH)
    pl.semaphore_wait(barrier, n - 1)
    return me


def remote(src, dst, send, recv, to):
    return pltpu.make_async_remote_copy(
        src_ref=src, dst_ref=dst, send_sem=send, recv_sem=recv, device_id={"tp": to},
        device_id_type=pl.DeviceIdType.MESH,
    )


def main_body(c2, scale, blk, n, cols, x_ref, dy_ref, wq_ref, wk_ref, wv_ref, wo_ref,
              x_full, dy_full, wq_all, got, dwq_ref, dq_ref, dwo_ref, dwkv_ref,
              q_s, k_s, v_s, do_s, dot_s, ot_s, m_s, rl_s, delta_s, tra, stage, xs, big, acc_s, dk_acc, dv_acc, dwq_s,
              xsend, xrecv, ysend, yrecv, wsend, wrecv, send_kv, recv_kv, load, local):
    head = wq_ref.shape[1]
    model = wq_ref.shape[0]
    me = enter_all(n)
    gx = Gather(x_ref, x_full, xsend, xrecv)
    gy = Gather(dy_ref, dy_full, ysend, yrecv)
    gw = Gather(wq_ref, wq_all, wsend, wrecv)
    gx.start()

    def rows(j):
        return pl.ds(pl.multiple_of(j * blk, blk), blk)

    def into(src, slot):
        return pltpu.make_async_copy(src, stage.at[slot], load.at[slot])

    own_x = pltpu.make_async_copy(stage.at[0], x_full.at[rows(me), :], local.at[0])
    own_w = pltpu.make_async_copy(wq_ref, wq_all.at[pl.ds(pl.multiple_of(me * model, model), model), :], local.at[1])
    into(x_ref, 0).start()
    own_w.start()

    def project(slot, dev):
        x = stage[slot]
        for e, (w_ref, o_ref) in enumerate(((wq_ref, q_s), (wk_ref, k_s), (wv_ref, v_s))):
            acc = dot(x, w_ref[...])
            o_ref[rows(dev), :] = acc.astype(BF16)
            tra[pl.ds(e * head, head), rows(dev)] = acc.T.astype(BF16)

    into(x_ref, 0).wait()
    own_x.start()
    project(0, me)
    gx.from_sib(3)
    into(x_full.at[rows(gx.sib), :], 1).start()
    gx.step(0)
    into(x_full.at[rows(gx.sib), :], 1).wait()
    project(1, gx.sib)
    gx.step(1)
    gy.start()
    own_x.wait()
    gx.step(2)
    gx.step(3)
    gx.from_sib(4)
    gx.from_sib(5)

    def near_loop(full, work):
        def fetch(k):
            return into(full.at[rows(gx.near(k)), :], k % 2)

        fetch(0).start()

        def body(k, _):
            @pl.when(k < 3)
            def _():
                fetch(k + 1).start()

            fetch(k).wait()
            work(k % 2, gx.near(k))
            return 0

        lax.fori_loop(0, 4, body, 0)

    def far_pair(g, full, work):
        into(full.at[rows(g.dg), :], 0).start()
        g.from_sib(6)
        into(full.at[rows(g.dg + g.flip), :], 1).start()
        into(full.at[rows(g.dg), :], 0).wait()
        work(0, g.dg)
        into(full.at[rows(g.dg + g.flip), :], 1).wait()
        work(1, g.dg + g.flip)

    near_loop(x_full, project)
    gx.last(0)
    gx.last(1)
    far_pair(gx, x_full, project)

    def attend(i, _):
        qt = tra[pl.ds(0, head), rows(i)]

        def score(j, m):
            s = dot(k_s[rows(j), :], qt) * c2
            big[rows(j), :] = s
            return jnp.maximum(m, jnp.max(s, axis=0, keepdims=True))

        m = lax.fori_loop(0, i, score, jnp.full((1, blk), -jnp.inf, F32))
        s = dot(k_s[rows(i), :], qt) * c2
        key = lax.broadcasted_iota(jnp.int32, (blk, blk), 0)
        qry = lax.broadcasted_iota(jnp.int32, (blk, blk), 1)
        s = jnp.where(key <= qry, s, -jnp.inf)
        big[rows(i), :] = s
        m = jnp.maximum(m, jnp.max(s, axis=0, keepdims=True))

        def expo(j, l):
            p = jnp.exp2(big[rows(j), :] - m)
            big[rows(j), :] = p
            return l + jnp.sum(p, axis=0, keepdims=True)

        l = lax.fori_loop(0, i + 1, expo, jnp.zeros((1, blk), F32))
        rl = 1.0 / l
        acc_s[...] = jnp.zeros_like(acc_s)

        def out(j, _):
            acc_s[...] += dot(tra[pl.ds(2 * head, head), rows(j)], (big[rows(j), :] * rl).astype(BF16))
            return 0

        lax.fori_loop(0, i + 1, out, 0)
        ot_s[:, rows(i)] = acc_s[...].astype(BF16)
        m_s[:, rows(i)] = m
        rl_s[:, rows(i)] = rl
        return 0

    def grad_out(slot, dev):
        dy = stage[slot]
        at = rows(dev)
        d_out = dot(dy, wo_ref[...], NT).astype(BF16)
        do_s[at, :] = d_out
        d_out_t = d_out.astype(F32).T
        dot_s[:, at] = d_out_t.astype(BF16)
        ot = ot_s[:, at]
        delta_s[:, at] = jnp.sum(d_out_t * ot.astype(F32), axis=0, keepdims=True)
        dwo_ref[...] += dot(ot, dy)

    dwo_ref[...] = jnp.zeros_like(dwo_ref)
    lax.fori_loop(0, n // 2, attend, 0)
    gy.step(0)
    lax.fori_loop(n // 2, 3 * n // 4, attend, 0)
    gy.step(1)
    gw.start()
    into(dy_ref, 0).start()
    gy.from_sib(3)
    into(dy_full.at[rows(gy.sib), :], 1).start()
    lax.fori_loop(3 * n // 4, n, attend, 0)
    gy.step(2)
    into(dy_ref, 0).wait()
    grad_out(0, me)
    into(dy_full.at[rows(gy.sib), :], 1).wait()
    grad_out(1, gy.sib)
    gy.step(3)
    gy.from_sib(4)
    gy.from_sib(5)
    near_loop(dy_full, grad_out)
    gy.last(0)
    gy.last(1)
    far_pair(gy, dy_full, grad_out)

    def fetch_x(b):
        at = pl.ds(pl.multiple_of(b * cols, cols), cols)
        return pltpu.make_async_copy(x_full.at[:, at], xs.at[b % 2], load.at[b % 2])

    fetch_x(0).start()
    fetch_x(1).start()

    def dq_rows(i):
        return pl.ds(pl.multiple_of(i * head, head), head)

    big[pl.ds(0, n * head), :] = jnp.zeros((n * head, blk), F32)

    def pair(j, i, masked):
        at_k = rows(j)
        at_q = rows(i)
        s = dot(k_s[at_k, :], tra[pl.ds(0, head), at_q])
        p = jnp.exp2(s * c2 - m_s[:, at_q]) * rl_s[:, at_q]
        if masked:
            key = lax.broadcasted_iota(jnp.int32, (blk, blk), 0)
            qry = lax.broadcasted_iota(jnp.int32, (blk, blk), 1)
            p = jnp.where(key <= qry, p, 0.0)
        dp = dot(v_s[at_k, :], dot_s[:, at_q])
        ds = (p * (dp - delta_s[:, at_q])).astype(BF16)
        dv = dot(p.astype(BF16), do_s[at_q, :])
        dk = dot(ds, q_s[at_q, :])
        big[dq_rows(i), :] += dot(tra[pl.ds(head, head), at_k], ds)
        if masked:
            dv_acc[...] = dv
            dk_acc[...] = dk
        else:
            dv_acc[...] += dv
            dk_acc[...] += dk

    def kv_copy(t, p, to):
        src = (k_s, v_s)[t]
        return remote(src.at[rows(to), :], got.at[t, p], send_kv.at[t, p], recv_kv.at[t, p], to)

    def send_block(p):
        to = lax.rem(me + p, n)
        for t in range(2):
            kv_copy(t, p, to).start()

    def column(step, _):
        j = lax.rem(me + step, n)
        pair(j, j, True)

        def rest(i, _):
            pair(j, i, False)
            return 0

        lax.fori_loop(j + 1, n, rest, 0)
        for e, (ref, grad) in enumerate(((k_s, dk_acc[...] * scale), (v_s, dv_acc[...]))):
            ref[rows(j), :] = grad.astype(BF16)
            tra[pl.ds((e + 1) * head, head), rows(j)] = grad.T.astype(BF16)

        for s, when in ((0, 0), (1, 1), (2, 3), (3, 4)):
            @pl.when(step == when)
            def _(s=s):
                gw.step(s)

        @pl.when(step >= 2)
        def _():
            send_block(step - 1)

        return 0

    lax.fori_loop(0, n, column, 0)

    def finish(i, _):
        dq = big[dq_rows(i), :] * scale
        tra[pl.ds(0, head), rows(i)] = dq.astype(BF16)
        dq_ref[rows(i), :] = dq.T.astype(BF16)
        return 0

    lax.fori_loop(0, n, finish, 0)
    send_block(n - 1)
    own = [pltpu.make_async_copy(ref.at[rows(me), :], got.at[t, 0], local.at[2 + t])
           for t, ref in enumerate((k_s, v_s))]
    for copy in own:
        copy.start()
    gw.last(0)
    gw.last(1)

    def put(b):
        at = pl.ds(pl.multiple_of(b * cols, cols), cols)
        return pltpu.make_async_copy(dwq_s.at[b % 2], dwq_ref.at[at, 0, :], local.at[4 + b % 2])

    def weights(b, _):
        at = pl.ds(pl.multiple_of(b * cols, cols), cols)
        fetch_x(b).wait()
        grad = dot(tra[...], xs[b % 2]).T

        @pl.when(b + 2 < model // cols)
        def _():
            fetch_x(b + 2).start()

        @pl.when(b >= 2)
        def _():
            put(b - 2).wait()

        dwq_s[b % 2] = grad[:, :head]
        dwkv_ref[at, :] = grad[:, head:]
        put(b).start()
        return 0

    lax.fori_loop(0, model // cols, weights, 0)
    for b in (model // cols - 2, model // cols - 1):
        put(b).wait()
    for slot in (3, 4, 5, 6):
        gw.from_sib(slot)
    for g in (gx, gy, gw):
        g.finish()
    own_w.wait()
    for copy in own:
        copy.wait()
    for t in range(2):
        for p in range(1, n):
            copy = kv_copy(t, p, lax.rem(me + p, n))
            copy.wait_send()
            copy.wait_recv()


def main_part(x_blk, dy_blk, wq, wk, wv, wo, n, c2, scale, cols):
    blk, model = x_blk.shape
    tokens = blk * n
    head = wq.shape[1]
    vm = pl.BlockSpec(memory_space=pltpu.VMEM)
    hbm = pl.BlockSpec(memory_space=pl.ANY)
    sem = pltpu.SemaphoreType.DMA
    return pl.pallas_call(
        functools.partial(main_body, c2, scale, blk, n, cols),
        in_specs=[hbm] * 2 + [vm] * 4,
        out_specs=[hbm] * 5 + [vm] * 3,
        out_shape=[
            jax.ShapeDtypeStruct((tokens, model), BF16),
            jax.ShapeDtypeStruct((tokens, model), BF16),
            jax.ShapeDtypeStruct((n * model, head), BF16),
            jax.ShapeDtypeStruct((2, n, blk, head), BF16),
            jax.ShapeDtypeStruct((model, 1, head), F32),
            jax.ShapeDtypeStruct((tokens, head), BF16),
            jax.ShapeDtypeStruct((head, model), F32),
            jax.ShapeDtypeStruct((model, 2 * head), F32),
        ],
        scratch_shapes=[pltpu.VMEM((tokens, head), BF16)] * 4
        + [pltpu.VMEM((head, tokens), BF16)] * 2
        + [pltpu.VMEM((1, tokens), F32)] * 3
        + [
            pltpu.VMEM((3 * head, tokens), BF16),
            pltpu.VMEM((2, blk, model), BF16),
            pltpu.VMEM((2, tokens, cols), BF16),
            pltpu.VMEM((tokens, blk), F32),
            pltpu.VMEM((head, blk), F32),
            pltpu.VMEM((blk, head), F32),
            pltpu.VMEM((blk, head), F32),
            pltpu.VMEM((2, cols, head), F32),
        ]
        + Gather.SEMS * 3
        + [sem((2, n)), sem((2, n)), sem((2,)), sem((6,))],
        compiler_params=params(collective_id=1, has_side_effects=True),
        cost_estimate=cost(7 * tokens * tokens * head + 14 * tokens * model * head, 8 * tokens * model,
                           tokens * tokens),
        name="main",
    )(x_blk, dy_blk, wq, wk, wv, wo)


def split3(x):
    hi = x.astype(BF16)
    r = x - hi.astype(F32)
    mid = r.astype(BF16)
    lo = (r - mid.astype(F32)).astype(BF16)
    return hi, mid, lo


def dx_body(n, cols, dq_ref, got_hbm, wq_hbm, wk_ref, wv_ref, dwkv_ref, dx_ref, dwk_ref, dwv_ref,
            gq, gkv, wq_s, parts, acc, r0, r1, r2, sum1, sum2,
            send, recv, s0, e0, s1, e1, s2, e2, load):
    rows, head = gq.shape[1], gq.shape[2]
    model = wk_ref.shape[0]
    part = dwkv_ref.shape[0] // n
    me = enter_all(n)
    c, x, y = me % 2, (me // 2) % 2, me // 4
    xn = me + 2 - 4 * x
    yn = me + 4 - 8 * y
    dg = xn + 4 - 8 * y
    flip = 1 - 2 * c
    sib = me + flip
    chips = (me, xn, yn, dg)

    def at(dev, size):
        return pl.ds(pl.multiple_of(dev * size, size), size)

    first = [remote(dwkv_ref.at[at(d + flip, part), :], r0.at[i], s0.at[i], e0.at[i], sib)
             for i, d in enumerate(chips)]
    for copy in first:
        copy.start()

    def q_copy(p):
        to = lax.rem(me + p, n)
        return remote(dq_ref.at[at(to, rows), :], gq.at[p], send.at[p], recv.at[p], to)

    loads = [pltpu.make_async_copy(got_hbm, gkv, load.at[0]), pltpu.make_async_copy(wq_hbm, wq_s, load.at[1]),
             pltpu.make_async_copy(dq_ref.at[at(me, rows), :], gq.at[0], load.at[2])]
    for copy in loads:
        copy.start()
    order = (4, 2, 6, 1, 3, 5, 7)
    early = 3
    for p in order[:early]:
        q_copy(p).start()

    for copy in first:
        copy.wait_recv()
    for i, d in enumerate(chips):
        sum1[i] = dwkv_ref[at(d, part), :] + r0[i]

    loads[0].wait()
    for t in range(2):
        total = gkv[t, 0].astype(F32)
        for p in range(1, n):
            total += gkv[t, p].astype(F32)
        for e, piece in enumerate(split3(total)):
            parts[t, e] = piece

    k_cols, v_cols = pl.ds(0, head), pl.ds(head, head)
    second = [
        remote(sum1.at[3, :, k_cols], r1.at[0, 1], s1.at[0, 1], e1.at[0, 1], xn),
        remote(sum1.at[3, :, v_cols], r1.at[1, 1], s1.at[1, 1], e1.at[1, 1], yn),
        remote(sum1.at[1, :, k_cols], r1.at[0, 0], s1.at[0, 0], e1.at[0, 0], xn),
        remote(sum1.at[2, :, v_cols], r1.at[1, 0], s1.at[1, 0], e1.at[1, 0], yn),
    ]
    for copy in second:
        copy.start()
    for p in order[early:]:
        q_copy(p).start()

    loads[1].wait()
    loads[2].wait()

    def kv_part(b, _):
        cs = pl.ds(pl.multiple_of(b * cols, cols), cols)
        total = None
        for t, w_ref in ((0, wk_ref), (1, wv_ref)):
            w = w_ref[cs, :]
            for e in range(3):
                d = dot(parts[t, e], w, NT)
                total = d if total is None else total + d
        acc[:, cs] = total + dot(gq[0], wq_s[pl.ds(pl.multiple_of(me * model + b * cols, cols), cols), :], NT)
        return 0

    lax.fori_loop(0, model // cols, kv_part, 0)

    def q_part(p):
        owner = lax.rem(me + n - p, n)

        def body(b, _):
            cs = pl.ds(pl.multiple_of(b * cols, cols), cols)
            acc[:, cs] += dot(gq[p], wq_s[pl.ds(pl.multiple_of(owner * model + b * cols, cols), cols), :], NT)
            return 0

        q_copy(p).wait_recv()
        lax.fori_loop(0, model // cols, body, 0)

    for p in order[:early]:
        q_part(p)

    second[0].wait_recv()
    sum2[0] = sum1[2, :, :head] + r1[0, 1]
    second[1].wait_recv()
    sum2[1] = sum1[1, :, head:] + r1[1, 1]
    for p in order[early:early + 1]:
        q_part(p)
    third = [
        remote(sum2.at[0], r2.at[0], s2.at[0], e2.at[0], yn),
        remote(sum2.at[1], r2.at[1], s2.at[1], e2.at[1], xn),
    ]
    for copy in third:
        copy.start()
    for p in order[early + 1:]:
        q_part(p)
    dx_ref[...] = acc[...].astype(BF16)
    second[2].wait_recv()
    second[3].wait_recv()
    third[0].wait_recv()
    third[1].wait_recv()
    dwk_ref[...] = (sum1[0, :, :head] + r1[0, 0]) + r2[0]
    dwv_ref[...] = (sum1[0, :, head:] + r1[1, 0]) + r2[1]
    for copy in first + second + third:
        copy.wait_send()
    for p in range(1, n):
        q_copy(p).wait_send()


def grad_x(dq, got, wq_all, wk, wv, dwkv, n, cols):
    tokens, head = dq.shape
    model = wk.shape[0]
    rows, part = tokens // n, model // n
    hbm = pl.BlockSpec(memory_space=pl.ANY)
    vm = pl.BlockSpec(memory_space=pltpu.VMEM)
    return pl.pallas_call(
        functools.partial(dx_body, n, cols),
        in_specs=[vm, hbm, hbm, vm, vm, vm],
        out_specs=[vm] * 3,
        out_shape=[jax.ShapeDtypeStruct((rows, model), BF16)] + [jax.ShapeDtypeStruct((part, head), F32)] * 2,
        scratch_shapes=[
            pltpu.VMEM((n, rows, head), BF16),
            pltpu.VMEM((2, n, rows, head), BF16),
            pltpu.VMEM((n * model, head), BF16),
            pltpu.VMEM((2, 3, rows, head), BF16),
            pltpu.VMEM((rows, model), F32),
            pltpu.VMEM((4, part, 2 * head), F32),
            pltpu.VMEM((2, 2, part, head), F32),
            pltpu.VMEM((2, part, head), F32),
            pltpu.VMEM((4, part, 2 * head), F32),
            pltpu.VMEM((2, part, head), F32),
            pltpu.SemaphoreType.DMA((n,)),
            pltpu.SemaphoreType.DMA((n,)),
            pltpu.SemaphoreType.DMA((4,)),
            pltpu.SemaphoreType.DMA((4,)),
            pltpu.SemaphoreType.DMA((2, 2)),
            pltpu.SemaphoreType.DMA((2, 2)),
            pltpu.SemaphoreType.DMA((2,)),
            pltpu.SemaphoreType.DMA((2,)),
            pltpu.SemaphoreType.DMA((3,)),
        ],
        compiler_params=params(collective_id=0, has_side_effects=True),
        cost_estimate=cost(8 * rows * n * model * head, 16e6),
        name="dx",
    )(dq, got, wq_all, wk, wv, dwkv)


def solution(mesh):
    n = mesh.shape["tp"]

    def local_grads(x_blk, dy_blk, wq_loc, w_k, w_v, wo_loc):
        model, kv_heads, head = w_k.shape
        scale = head ** -0.5
        c2 = scale * LOG2E
        wq = wq_loc.reshape(model, head)
        wk = w_k.reshape(model, head)
        wv = w_v.reshape(model, head)
        wo = wo_loc.reshape(head, model)
        _, _, wq_all, got, dwq, dq, dwo, dwkv = main_part(x_blk, dy_blk, wq, wk, wv, wo, n, c2, scale, 256)
        dx, dwk, dwv = grad_x(dq, got, wq_all, wk, wv, dwkv, n, 512)
        return dx, dwq, dwo.reshape(1, head, model), dwk, dwv

    tok_spec = P(("dp", "tp"))
    return jax.shard_map(
        local_grads,
        mesh=mesh,
        in_specs=(tok_spec, tok_spec, P(None, "tp", None), P(), P(), P("tp")),
        out_specs=(tok_spec, P("dp", "tp", None), tok_spec, tok_spec, tok_spec),
        check_vma=False,
    )
```

time: 315 us -> 284 us (0.902)
  Pallas kernels: 306 us -> 275 us
    pallas_call x3 -> x1, Pallas kernels: 257 us -> 226 us  [main_part(): pl.pallas_call(functools.partial(main_body, c2, scale, blk, n, cols), in_...]
where the time goes in v4:
time: 284 us
  Pallas kernels  275 us (97%)
  local copies, waits for them, and re-layouts  8.39 us (3%)
    pallas_call x1, Pallas kernels, main_part(): pl.pallas_call(functools.partial(main_body, c2, scale, blk, n, cols), in_...  226 us
    pallas_call x1, Pallas kernels, grad_x(): pl.pallas_call(functools.partial(dx_body, n, cols), in_specs=[vm, hbm, hb...  49.2 us
    unnamed x13, local copies, waits for them, and re-layouts  8.39 us

profile of v4, /device:TPU:0, one launch (start us, length us, event | category | flops | bytes accessed | tf_op | source)
XLA Modules:
  0.0 283.9 jit_solution(17440600849192938669)
XLA Ops:
  0.6 225.7 %main.1 = (bf16[4096,2048]{1,0:T(8,128)(2,1)}, bf16[4096,2048]{1,0:T(8,128)(2,1)}, bf16[16384,256]{1,0:T(8,128)(2,1)}, bf16[2,8,512,256]{3,2,1,0:T(8,128)(2,1)},...) custom-call(bf16[512,2048]{1,0:T(8,128)(2,1)} %x_ref.1, ...), custom_call_target="tpu_custom_call" | custom-call | flops 60129542144 | bytes 67108864 | tf_op jit(solution)/shard_map/main/pallas_call | solution.py:403
  226.3 49.2 %dx.1 = (bf16[512,2048]{1,0:T(8,128)(2,1)}, f32[256,256]{1,0:T(8,128)}, f32[256,256]{1,0:T(8,128)}) custom-call(bf16[4096,256]{1,0:T(8,128)(2,1)} %get-tuple-element.14.dq_ref, bf16[2,8,512,256]{3,2,1,0:T(8,128)(2,1)} %get-tuple-element.15.got_hbm, bf16[16384,256]{1,0:T(8,128)(2,1)} %get-tuple-element.16.wq_hbm, bf16[2048,256]{1,0:T(8,128)(2,1)} %bitcast.9, ...), custom_call_target="tpu_custom_call" | custom-call | flops 17179869184 | bytes 16000000 | tf_op jit(solution)/shard_map/dx/pallas_call | solution.py:571
  275.5 0.0 copy-start.1
  275.5 3.3 %copy.16 = bf16[512,2048]{1,0:T(8,128)(2,1)} copy(bf16[512,2048]{1,0:T(8,128)(2,1)} %get-tuple-element.28) | data formatting | bytes 4194304
  278.8 0.0 copy-done.1
  278.8 0.0 copy-start
  278.9 1.3 copy.17
  280.2 1.0 copy-done
  281.2 0.0 copy-start.3
  281.2 0.0 copy-start.2
  281.2 1.3 copy.18
  282.5 0.0 copy-done.3
  282.5 0.7 copy.19
  283.2 0.0 copy-done.2
  283.2 0.7 copy.20
Async XLA Ops:
  275.5 3.3 %copy-start.1 = (f32[2048,1,256]{2,1,0:T(1,128)S(1)}, f32[2048,1,256]{2,1,0:T(1,128)}, u32[]{:S(2)}) copy-start(f32[2048,1,256]{2,1,0:T(1,128)} %get-tuple-element.29) | copy-start | bytes 6291460
  278.8 2.3 copy-start
  281.2 1.3 copy-start.3
  281.2 2.0 copy-start.2

commit v5 on v4

--- a/solution.py
+++ b/solution.py
@@ -10,7 +10,7 @@
 F32 = jnp.float32
 BF16 = jnp.bfloat16
 LOG2E = 1.4426950408889634
-VMEM_BYTES = 60 * 1024 * 1024
+VMEM_BYTES = 62 * 1024 * 1024
 NN = (((1,), (0,)), ((), ()))
 NT = (((1,), (1,)), ((), ()))
 
@@ -125,16 +125,25 @@
     )
 
 
+def split3(x):
+    hi = x.astype(BF16)
+    r = x - hi.astype(F32)
+    mid = r.astype(BF16)
+    lo = (r - mid.astype(F32)).astype(BF16)
+    return hi, mid, lo
+
+
 def main_body(c2, scale, blk, n, cols, x_ref, dy_ref, wq_ref, wk_ref, wv_ref, wo_ref,
-              x_full, dy_full, wq_all, got, dwq_ref, dq_ref, dwo_ref, dwkv_ref,
+              x_full, dy_full, wq_all, got, dwq_ref, dwo_ref, dx_ref, dwk_ref, dwv_ref,
               q_s, k_s, v_s, do_s, dot_s, ot_s, m_s, rl_s, delta_s, tra, stage, xs, big, acc_s, dk_acc, dv_acc, dwq_s,
-              xsend, xrecv, ysend, yrecv, wsend, wrecv, send_kv, recv_kv, load, local):
+              wqt, parts, r0, r1, r2,
+              xsend, xrecv, ysend, yrecv, wsend, wrecv, send_kv, recv_kv, load, local, s0, e0, s1, e1, s2, e2):
     head = wq_ref.shape[1]
     model = wq_ref.shape[0]
     me = enter_all(n)
     gx = Gather(x_ref, x_full, xsend, xrecv)
     gy = Gather(dy_ref, dy_full, ysend, yrecv)
-    gw = Gather(wq_ref, wq_all, wsend, wrecv)
+    gw = Gather(wqt, wq_all, wsend, wrecv)
     gx.start()
 
     def rows(j):
@@ -144,9 +153,8 @@
         return pltpu.make_async_copy(src, stage.at[slot], load.at[slot])
 
     own_x = pltpu.make_async_copy(stage.at[0], x_full.at[rows(me), :], local.at[0])
-    own_w = pltpu.make_async_copy(wq_ref, wq_all.at[pl.ds(pl.multiple_of(me * model, model), model), :], local.at[1])
     into(x_ref, 0).start()
-    own_w.start()
+    wqt[...] = wq_ref[...].T
 
     def project(slot, dev):
         x = stage[slot]
@@ -305,8 +313,8 @@
             dk_acc[...] += dk
 
     def kv_copy(t, p, to):
-        src = (k_s, v_s)[t]
-        return remote(src.at[rows(to), :], got.at[t, p], send_kv.at[t, p], recv_kv.at[t, p], to)
+        src = (k_s, v_s, q_s)[t]
+        return remote(src.at[rows(to), :], got.at[t, pl.ds(p * blk, blk), :], send_kv.at[t, p], recv_kv.at[t, p], to)
 
     def send_block(p):
         to = lax.rem(me + p, n)
@@ -342,12 +350,16 @@
     def finish(i, _):
         dq = big[dq_rows(i), :] * scale
         tra[pl.ds(0, head), rows(i)] = dq.astype(BF16)
-        dq_ref[rows(i), :] = dq.T.astype(BF16)
+        q_s[rows(i), :] = dq.T.astype(BF16)
         return 0
 
     lax.fori_loop(0, n, finish, 0)
     send_block(n - 1)
-    own = [pltpu.make_async_copy(ref.at[rows(me), :], got.at[t, 0], local.at[2 + t])
+    order = (4, 2, 6, 1, 3, 5, 7)
+    early = 3
+    for p in order[:early]:
+        kv_copy(2, p, lax.rem(me + p, n)).start()
+    own = [pltpu.make_async_copy(ref.at[rows(me), :], got.at[t, pl.ds(0, blk), :], local.at[2 + t])
            for t, ref in enumerate((k_s, v_s))]
     for copy in own:
         copy.start()
@@ -372,47 +384,169 @@
             put(b - 2).wait()
 
         dwq_s[b % 2] = grad[:, :head]
-        dwkv_ref[at, :] = grad[:, head:]
+        big[pl.ds(pl.multiple_of(n * head + b * cols, cols), cols), :] = grad[:, head:]
         put(b).start()
         return 0
 
     lax.fori_loop(0, model // cols, weights, 0)
     for b in (model // cols - 2, model // cols - 1):
         put(b).wait()
+
+    part = model // n
+    xn, yn, dg, flip, sib = gx.xn, gx.yn, gx.dg, gx.flip, gx.sib
+    chips = (me, xn, yn, dg)
+
+    def block(dev):
+        return big.at[pl.ds(pl.multiple_of(n * head + dev * part, part), part), :]
+
+    first = [remote(block(d + flip), r0.at[i], s0.at[i], e0.at[i], sib) for i, d in enumerate(chips)]
+    for copy in first:
+        copy.start()
+
+    wide = 2 * cols
+
+    def head_to_stage(k):
+        owner = lax.rem(me + n - order[k], n)
+        at = pl.ds(pl.multiple_of(owner * head, head), head)
+        return pltpu.make_async_copy(wq_all.at[at, :], stage.at[k % 2, pl.ds(0, head), :], load.at[k % 2])
+
+    def q_to_vmem(p):
+        return pltpu.make_async_copy(got.at[2, pl.ds(p * blk, blk), :], do_s.at[pl.ds(p * blk, blk), :], local.at[1])
+
+    def tile(b):
+        return big.at[pl.ds(pl.multiple_of(b * wide, wide), wide), :]
+
+    def across(work):
+        def body(b, _):
+            work(b, pl.ds(pl.multiple_of(b * wide, wide), wide))
+            return 0
+
+        lax.fori_loop(0, model // wide, body, 0)
+
+    def own_part(b, cs):
+        tile(b)[...] = dot(q_s[rows(me), :], wqt[:, cs])
+
+    across(own_part)
     for slot in (3, 4, 5, 6):
         gw.from_sib(slot)
+    for k in range(2):
+        head_to_stage(k).start()
+
+    for copy in first:
+        copy.wait_recv()
+    for i, d in enumerate(chips):
+        r0[i] += block(d)[...]
+
+    for p in range(1, n):
+        for t in range(2):
+            kv_copy(t, p, lax.rem(me + p, n)).wait_recv()
+    for copy in own:
+        copy.wait()
+    loads = [pltpu.make_async_copy(got.at[t], xs.at[t], local.at[6 + t]) for t in range(2)]
+    for copy in loads:
+        copy.start()
+
+    k_cols, v_cols = pl.ds(0, head), pl.ds(head, head)
+    second = [
+        remote(r0.at[3, :, k_cols], r1.at[0, 1], s1.at[0, 1], e1.at[0, 1], xn),
+        remote(r0.at[3, :, v_cols], r1.at[1, 1], s1.at[1, 1], e1.at[1, 1], yn),
+        remote(r0.at[1, :, k_cols], r1.at[0, 0], s1.at[0, 0], e1.at[0, 0], xn),
+        remote(r0.at[2, :, v_cols], r1.at[1, 0], s1.at[1, 0], e1.at[1, 0], yn),
+    ]
+    for copy in second:
+        copy.start()
+    for p in order[early:]:
+        kv_copy(2, p, lax.rem(me + p, n)).start()
+
+    for copy in loads:
+        copy.wait()
+    for t in range(2):
+        total = xs[t, pl.ds(0, blk), :].astype(F32)
+        for p in range(1, n):
+            total += xs[t, pl.ds(p * blk, blk), :].astype(F32)
+        for e, piece in enumerate(split3(total)):
+            parts[t, e] = piece
+
+    def kv_part(b, cs):
+        total = tile(b)[...]
+        for t, w_ref in ((0, wk_ref), (1, wv_ref)):
+            w = w_ref[cs, :]
+            for e in range(3):
+                total += dot(parts[t, e], w, NT)
+        tile(b)[...] = total
+
+    across(kv_part)
+
+    def q_part(k):
+        p = order[k]
+        kv_copy(2, p, lax.rem(me + p, n)).wait_recv()
+        q_to_vmem(p).start()
+        head_to_stage(k).wait()
+        q_to_vmem(p).wait()
+
+        def work(b, cs):
+            tile(b)[...] += dot(do_s[pl.ds(p * blk, blk), :], stage[k % 2, pl.ds(0, head), cs])
+
+        across(work)
+        if k + 2 < n - 1:
+            head_to_stage(k + 2).start()
+
+    for k in range(early):
+        q_part(k)
+
+    second[0].wait_recv()
+    r1[0, 1] += r0[2, :, :head]
+    second[1].wait_recv()
+    r1[1, 1] += r0[1, :, head:]
+    q_part(early)
+    third = [
+        remote(r1.at[0, 1], r2.at[0], s2.at[0], e2.at[0], yn),
+        remote(r1.at[1, 1], r2.at[1], s2.at[1], e2.at[1], xn),
+    ]
+    for copy in third:
+        copy.start()
+    for k in range(early + 1, n - 1):
+        q_part(k)
+
+    for b in range(model // wide):
+        dx_ref[:, pl.ds(b * wide, wide)] = big[pl.ds(b * wide, wide), :].astype(BF16)
+    second[2].wait_recv()
+    second[3].wait_recv()
+    third[0].wait_recv()
+    third[1].wait_recv()
+    dwk_ref[...] = (r0[0, :, :head] + r1[0, 0]) + r2[0]
+    dwv_ref[...] = (r0[0, :, head:] + r1[1, 0]) + r2[1]
+    for copy in first + second + third:
+        copy.wait_send()
     for g in (gx, gy, gw):
         g.finish()
-    own_w.wait()
-    for copy in own:
-        copy.wait()
-    for t in range(2):
+    for t in range(3):
         for p in range(1, n):
-            copy = kv_copy(t, p, lax.rem(me + p, n))
-            copy.wait_send()
-            copy.wait_recv()
+            kv_copy(t, p, lax.rem(me + p, n)).wait_send()
 
 
 def main_part(x_blk, dy_blk, wq, wk, wv, wo, n, c2, scale, cols):
     blk, model = x_blk.shape
     tokens = blk * n
     head = wq.shape[1]
+    part = model // n
     vm = pl.BlockSpec(memory_space=pltpu.VMEM)
     hbm = pl.BlockSpec(memory_space=pl.ANY)
     sem = pltpu.SemaphoreType.DMA
     return pl.pallas_call(
         functools.partial(main_body, c2, scale, blk, n, cols),
         in_specs=[hbm] * 2 + [vm] * 4,
-        out_specs=[hbm] * 5 + [vm] * 3,
+        out_specs=[hbm] * 5 + [vm] * 4,
         out_shape=[
             jax.ShapeDtypeStruct((tokens, model), BF16),
             jax.ShapeDtypeStruct((tokens, model), BF16),
-            jax.ShapeDtypeStruct((n * model, head), BF16),
-            jax.ShapeDtypeStruct((2, n, blk, head), BF16),
+            jax.ShapeDtypeStruct((n * head, model), BF16),
+            jax.ShapeDtypeStruct((3, tokens, head), BF16),
             jax.ShapeDtypeStruct((model, 1, head), F32),
-            jax.ShapeDtypeStruct((tokens, head), BF16),
             jax.ShapeDtypeStruct((head, model), F32),
-            jax.ShapeDtypeStruct((model, 2 * head), F32),
+            jax.ShapeDtypeStruct((blk, model), BF16),
+            jax.ShapeDtypeStruct((part, head), F32),
+            jax.ShapeDtypeStruct((part, head), F32),
         ],
         scratch_shapes=[pltpu.VMEM((tokens, head), BF16)] * 4
         + [pltpu.VMEM((head, tokens), BF16)] * 2
@@ -426,178 +560,20 @@
             pltpu.VMEM((blk, head), F32),
             pltpu.VMEM((blk, head), F32),
             pltpu.VMEM((2, cols, head), F32),
+            pltpu.VMEM((head, model), BF16),
+            pltpu.VMEM((2, 3, blk, head), BF16),
+            pltpu.VMEM((4, part, 2 * head), F32),
+            pltpu.VMEM((2, 2, part, head), F32),
+            pltpu.VMEM((2, part, head), F32),
         ]
         + Gather.SEMS * 3
-        + [sem((2, n)), sem((2, n)), sem((2,)), sem((6,))],
+        + [sem((3, n)), sem((3, n)), sem((2,)), sem((8,)), sem((4,)), sem((4,)), sem((2, 2)), sem((2, 2)), sem((2,)),
+           sem((2,))],
         compiler_params=params(collective_id=1, has_side_effects=True),
         cost_estimate=cost(7 * tokens * tokens * head + 14 * tokens * model * head, 8 * tokens * model,
                            tokens * tokens),
         name="main",
     )(x_blk, dy_blk, wq, wk, wv, wo)
-
-
-def split3(x):
-    hi = x.astype(BF16)
-    r = x - hi.astype(F32)
-    mid = r.astype(BF16)
-    lo = (r - mid.astype(F32)).astype(BF16)
-    return hi, mid, lo
-
-
-def dx_body(n, cols, dq_ref, got_hbm, wq_hbm, wk_ref, wv_ref, dwkv_ref, dx_ref, dwk_ref, dwv_ref,
-            gq, gkv, wq_s, parts, acc, r0, r1, r2, sum1, sum2,
-            send, recv, s0, e0, s1, e1, s2, e2, load):
-    rows, head = gq.shape[1], gq.shape[2]
-    model = wk_ref.shape[0]
-    part = dwkv_ref.shape[0] // n
-    me = enter_all(n)
-    c, x, y = me % 2, (me // 2) % 2, me // 4
-    xn = me + 2 - 4 * x
-    yn = me + 4 - 8 * y
-    dg = xn + 4 - 8 * y
-    flip = 1 - 2 * c
-    sib = me + flip
-    chips = (me, xn, yn, dg)
-
-    def at(dev, size):
-        return pl.ds(pl.multiple_of(dev * size, size), size)
-
-    first = [remote(dwkv_ref.at[at(d + flip, part), :], r0.at[i], s0.at[i], e0.at[i], sib)
-             for i, d in enumerate(chips)]
-    for copy in first:
-        copy.start()
-
-    def q_copy(p):
-        to = lax.rem(me + p, n)
-        return remote(dq_ref.at[at(to, rows), :], gq.at[p], send.at[p], recv.at[p], to)
-
-    loads = [pltpu.make_async_copy(got_hbm, gkv, load.at[0]), pltpu.make_async_copy(wq_hbm, wq_s, load.at[1]),
-             pltpu.make_async_copy(dq_ref.at[at(me, rows), :], gq.at[0], load.at[2])]
-    for copy in loads:
-        copy.start()
-    order = (4, 2, 6, 1, 3, 5, 7)
-    early = 3
-    for p in order[:early]:
-        q_copy(p).start()
-
-    for copy in first:
-        copy.wait_recv()
-    for i, d in enumerate(chips):
-        sum1[i] = dwkv_ref[at(d, part), :] + r0[i]
-
-    loads[0].wait()
-    for t in range(2):
-        total = gkv[t, 0].astype(F32)
-        for p in range(1, n):
-            total += gkv[t, p].astype(F32)
-        for e, piece in enumerate(split3(total)):
-            parts[t, e] = piece
-
-    k_cols, v_cols = pl.ds(0, head), pl.ds(head, head)
-    second = [
-        remote(sum1.at[3, :, k_cols], r1.at[0, 1], s1.at[0, 1], e1.at[0, 1], xn),
-        remote(sum1.at[3, :, v_cols], r1.at[1, 1], s1.at[1, 1], e1.at[1, 1], yn),
-        remote(sum1.at[1, :, k_cols], r1.at[0, 0], s1.at[0, 0], e1.at[0, 0], xn),
-        remote(sum1.at[2, :, v_cols], r1.at[1, 0], s1.at[1, 0], e1.at[1, 0], yn),
-    ]
-    for copy in second:
-        copy.start()
-    for p in order[early:]:
-        q_copy(p).start()
-
-    loads[1].wait()
-    loads[2].wait()
-
-    def kv_part(b, _):
-        cs = pl.ds(pl.multiple_of(b * cols, cols), cols)
-        total = None
-        for t, w_ref in ((0, wk_ref), (1, wv_ref)):
-            w = w_ref[cs, :]
-            for e in range(3):
-                d = dot(parts[t, e], w, NT)
-                total = d if total is None else total + d
-        acc[:, cs] = total + dot(gq[0], wq_s[pl.ds(pl.multiple_of(me * model + b * cols, cols), cols), :], NT)
-        return 0
-
-    lax.fori_loop(0, model // cols, kv_part, 0)
-
-    def q_part(p):
-        owner = lax.rem(me + n - p, n)
-
-        def body(b, _):
-            cs = pl.ds(pl.multiple_of(b * cols, cols), cols)
-            acc[:, cs] += dot(gq[p], wq_s[pl.ds(pl.multiple_of(owner * model + b * cols, cols), cols), :], NT)
-            return 0
-
-        q_copy(p).wait_recv()
-        lax.fori_loop(0, model // cols, body, 0)
-
-    for p in order[:early]:
-        q_part(p)
-
-    second[0].wait_recv()
-    sum2[0] = sum1[2, :, :head] + r1[0, 1]
-    second[1].wait_recv()
-    sum2[1] = sum1[1, :, head:] + r1[1, 1]
-    for p in order[early:early + 1]:
-        q_part(p)
-    third = [
-        remote(sum2.at[0], r2.at[0], s2.at[0], e2.at[0], yn),
-        remote(sum2.at[1], r2.at[1], s2.at[1], e2.at[1], xn),
-    ]
-    for copy in third:
-        copy.start()
-    for p in order[early + 1:]:
-        q_part(p)
-    dx_ref[...] = acc[...].astype(BF16)
-    second[2].wait_recv()
-    second[3].wait_recv()
-    third[0].wait_recv()
-    third[1].wait_recv()
-    dwk_ref[...] = (sum1[0, :, :head] + r1[0, 0]) + r2[0]
-    dwv_ref[...] = (sum1[0, :, head:] + r1[1, 0]) + r2[1]
-    for copy in first + second + third:
-        copy.wait_send()
-    for p in range(1, n):
-        q_copy(p).wait_send()
-
-
-def grad_x(dq, got, wq_all, wk, wv, dwkv, n, cols):
-    tokens, head = dq.shape
-    model = wk.shape[0]
-    rows, part = tokens // n, model // n
-    hbm = pl.BlockSpec(memory_space=pl.ANY)
-    vm = pl.BlockSpec(memory_space=pltpu.VMEM)
-    return pl.pallas_call(
-        functools.partial(dx_body, n, cols),
-        in_specs=[vm, hbm, hbm, vm, vm, vm],
-        out_specs=[vm] * 3,
-        out_shape=[jax.ShapeDtypeStruct((rows, model), BF16)] + [jax.ShapeDtypeStruct((part, head), F32)] * 2,
-        scratch_shapes=[
-            pltpu.VMEM((n, rows, head), BF16),
-            pltpu.VMEM((2, n, rows, head), BF16),
-            pltpu.VMEM((n * model, head), BF16),
-            pltpu.VMEM((2, 3, rows, head), BF16),
-            pltpu.VMEM((rows, model), F32),
-            pltpu.VMEM((4, part, 2 * head), F32),
-            pltpu.VMEM((2, 2, part, head), F32),
-            pltpu.VMEM((2, part, head), F32),
-            pltpu.VMEM((4, part, 2 * head), F32),
-            pltpu.VMEM((2, part, head), F32),
-            pltpu.SemaphoreType.DMA((n,)),
-            pltpu.SemaphoreType.DMA((n,)),
-            pltpu.SemaphoreType.DMA((4,)),
-            pltpu.SemaphoreType.DMA((4,)),
-            pltpu.SemaphoreType.DMA((2, 2)),
-            pltpu.SemaphoreType.DMA((2, 2)),
-            pltpu.SemaphoreType.DMA((2,)),
-            pltpu.SemaphoreType.DMA((2,)),
-            pltpu.SemaphoreType.DMA((3,)),
-        ],
-        compiler_params=params(collective_id=0, has_side_effects=True),
-        cost_estimate=cost(8 * rows * n * model * head, 16e6),
-        name="dx",
-    )(dq, got, wq_all, wk, wv, dwkv)
 
 
 def solution(mesh):
@@ -611,8 +587,7 @@
         wk = w_k.reshape(model, head)
         wv = w_v.reshape(model, head)
         wo = wo_loc.reshape(head, model)
-        _, _, wq_all, got, dwq, dq, dwo, dwkv = main_part(x_blk, dy_blk, wq, wk, wv, wo, n, c2, scale, 256)
-        dx, dwk, dwv = grad_x(dq, got, wq_all, wk, wv, dwkv, n, 512)
+        *_, dwq, dwo, dx, dwk, dwv = main_part(x_blk, dy_blk, wq, wk, wv, wo, n, c2, scale, 256)
         return dx, dwq, dwo.reshape(1, head, model), dwk, dwv
 
     tok_spec = P(("dp", "tp"))

time: 284 us -> 275 us (0.968)
  Pallas kernels: 275 us -> 266 us
    pallas_call x1 -> x0, Pallas kernels: 49.2 us -> none  [grad_x(): pl.pallas_call(functools.partial(dx_body, n, cols), in_specs=[vm, hbm, hb...]
    pallas_call x1, Pallas kernels: 226 us -> 266 us  [main_part(): pl.pallas_call(functools.partial(main_body, c2, scale, blk, n, cols), in_...]
where the time goes in v5:
time: 275 us
  Pallas kernels  266 us (97%)
  local copies, waits for them, and re-layouts  8.39 us (3%)
    pallas_call x1, Pallas kernels, main_part(): pl.pallas_call(functools.partial(main_body, c2, scale, blk, n, cols), in_...  266 us
    unnamed x13, local copies, waits for them, and re-layouts  8.39 us

profile of v5, /device:TPU:0, one launch (start us, length us, event | category | flops | bytes accessed | tf_op | source)
XLA Modules:
  0.0 275.0 jit_solution(11748839625076176679)
XLA Ops:
  0.6 266.0 %main.1 = (bf16[4096,2048]{1,0:T(8,128)(2,1)}, bf16[4096,2048]{1,0:T(8,128)(2,1)}, bf16[2048,2048]{1,0:T(8,128)(2,1)}, bf16[3,4096,256]{2,1,0:T(8,128)(2,1)}, f3...) custom-call(bf16[512,2048]{1,0:T(8,128)(2,1)} %x_ref.1, ...), custom_call_target="tpu_custom_call" | custom-call | flops 60129542144 | bytes 67108864 | tf_op jit(solution)/shard_map/main/pallas_call | solution.py:536
  266.6 0.0 copy-start.1
  266.6 3.3 %copy.16 = bf16[512,2048]{1,0:T(8,128)(2,1)} copy(bf16[512,2048]{1,0:T(8,128)(2,1)} %get-tuple-element.20) | data formatting | bytes 4194304
  269.9 0.0 copy-done.1
  269.9 0.0 copy-start
  269.9 1.3 copy.17
  271.3 1.0 copy-done
  272.3 0.0 copy-start.3
  272.3 0.0 copy-start.2
  272.3 1.3 copy.18
  273.6 0.0 copy-done.3
  273.6 0.7 copy.19
  274.3 0.0 copy-done.2
  274.3 0.7 copy.20
Async XLA Ops:
  266.6 3.3 %copy-start.1 = (f32[2048,1,256]{2,1,0:T(1,128)S(1)}, f32[2048,1,256]{2,1,0:T(1,128)}, u32[]{:S(2)}) copy-start(f32[2048,1,256]{2,1,0:T(1,128)} %get-tuple-element.21) | copy-start | bytes 6291460
  269.9 2.3 copy-start
  272.3 1.3 copy-start.3
  272.3 2.0 copy-start.2

commit v6 on v5

--- a/solution.py
+++ b/solution.py
@@ -136,8 +136,9 @@
 def main_body(c2, scale, blk, n, cols, x_ref, dy_ref, wq_ref, wk_ref, wv_ref, wo_ref,
               x_full, dy_full, wq_all, got, dwq_ref, dwo_ref, dx_ref, dwk_ref, dwv_ref,
               q_s, k_s, v_s, do_s, dot_s, ot_s, m_s, rl_s, delta_s, tra, stage, xs, big, acc_s, dk_acc, dv_acc, dwq_s,
-              wqt, parts, r0, r1, r2,
-              xsend, xrecv, ysend, yrecv, wsend, wrecv, send_kv, recv_kv, load, local, s0, e0, s1, e1, s2, e2):
+              wqt, rel, near_kv, far_kv, r0, r1, r2,
+              xsend, xrecv, ysend, yrecv, wsend, wrecv, send_q, recv_q, send_kv, send_sib, send_far, recv_rel, recv_near,
+              recv_far, load, local, s0, e0, s1, e1, s2, e2):
     head = wq_ref.shape[1]
     model = wq_ref.shape[0]
     me = enter_all(n)
@@ -312,17 +313,58 @@
             dv_acc[...] += dv
             dk_acc[...] += dk
 
-    def kv_copy(t, p, to):
-        src = (k_s, v_s, q_s)[t]
-        return remote(src.at[rows(to), :], got.at[t, pl.ds(p * blk, blk), :], send_kv.at[t, p], recv_kv.at[t, p], to)
-
-    def send_block(p):
+    core = me % 2
+    ways = (gx.dg, gx.xn, gx.yn, me)
+    refs = (k_s, v_s)
+
+    def block_of(step):
+        k = step // 2
+        way = jnp.where(k == 0, gx.dg, jnp.where(k == 1, gx.xn, jnp.where(k == 2, gx.yn, me)))
+        return way - core + step % 2
+
+    def to_relay(t, s):
+        e = s % 2
+        to = (gx.yn, gx.xn)[t] - core + e
+        return remote(refs[t].at[rows(gx.dg - core + e), :], rel.at[t, 1 + core], send_kv.at[t, s],
+                      recv_rel.at[t, 1 + core], to)
+
+    def to_owner(t, s):
+        to = ways[s // 2] - core + s % 2
+        return remote(refs[t].at[rows(to), :], near_kv.at[t, core], send_kv.at[t, s], recv_near.at[t, core], to)
+
+    def to_sib_relay(t):
+        return remote(refs[t].at[rows(ways[1 + t] + gx.flip), :], rel.at[t, 0], send_sib.at[t, 0], recv_rel.at[t, 0],
+                      gx.sib)
+
+    def to_sib(t):
+        return remote(refs[t].at[rows(gx.sib), :], near_kv.at[t, 2], send_sib.at[t, 1], recv_near.at[t, 2], gx.sib)
+
+    def from_relay(t):
+        return remote((dk_acc, dv_acc)[t], far_kv.at[t], send_far.at[t], recv_far.at[t], ways[1 + t])
+
+    def send_block(s):
+        k, e = s // 2, s % 2
+        if k == 0:
+            to_relay(0, s).start()
+            to_relay(1, s).start()
+        elif k < 3:
+            to_owner(2 - k, s).start()
+
+            @pl.when(core != e)
+            def _():
+                to_sib_relay(k - 1).start()
+        else:
+            @pl.when(core != e)
+            def _():
+                to_sib(0).start()
+                to_sib(1).start()
+
+    def q_copy(p):
         to = lax.rem(me + p, n)
-        for t in range(2):
-            kv_copy(t, p, to).start()
+        return remote(q_s.at[rows(to), :], got.at[pl.ds(p * blk, blk), :], send_q.at[p], recv_q.at[p], to)
 
     def column(step, _):
-        j = lax.rem(me + step, n)
+        j = block_of(step)
         pair(j, j, True)
 
         def rest(i, _):
@@ -339,13 +381,19 @@
             def _(s=s):
                 gw.step(s)
 
-        @pl.when(step >= 2)
-        def _():
-            send_block(step - 1)
+        for s in range(n - 1):
+            @pl.when(step == s + 1)
+            def _(s=s):
+                send_block(s)
 
         return 0
 
     lax.fori_loop(0, n, column, 0)
+    for t, acc in enumerate((dk_acc, dv_acc)):
+        for i in range(3):
+            remote(rel.at[t, i], rel.at[t, i], send_far.at[t], recv_rel.at[t, i], gx.sib).wait_recv()
+        total = refs[t][rows(ways[1 + t]), :].astype(F32) + rel[t, 0].astype(F32)
+        acc[...] = total + (rel[t, 1].astype(F32) + rel[t, 2].astype(F32))
 
     def finish(i, _):
         dq = big[dq_rows(i), :] * scale
@@ -355,14 +403,12 @@
 
     lax.fori_loop(0, n, finish, 0)
     send_block(n - 1)
+    from_relay(0).start()
+    from_relay(1).start()
     order = (4, 2, 6, 1, 3, 5, 7)
     early = 3
     for p in order[:early]:
-        kv_copy(2, p, lax.rem(me + p, n)).start()
-    own = [pltpu.make_async_copy(ref.at[rows(me), :], got.at[t, pl.ds(0, blk), :], local.at[2 + t])
-           for t, ref in enumerate((k_s, v_s))]
-    for copy in own:
-        copy.start()
+        q_copy(p).start()
     gw.last(0)
     gw.last(1)
 
@@ -411,7 +457,7 @@
         return pltpu.make_async_copy(wq_all.at[at, :], stage.at[k % 2, pl.ds(0, head), :], load.at[k % 2])
 
     def q_to_vmem(p):
-        return pltpu.make_async_copy(got.at[2, pl.ds(p * blk, blk), :], do_s.at[pl.ds(p * blk, blk), :], local.at[1])
+        return pltpu.make_async_copy(got.at[pl.ds(p * blk, blk), :], do_s.at[pl.ds(p * blk, blk), :], local.at[1])
 
     def tile(b):
         return big.at[pl.ds(pl.multiple_of(b * wide, wide), wide), :]
@@ -436,15 +482,6 @@
         copy.wait_recv()
     for i, d in enumerate(chips):
         r0[i] += block(d)[...]
-
-    for p in range(1, n):
-        for t in range(2):
-            kv_copy(t, p, lax.rem(me + p, n)).wait_recv()
-    for copy in own:
-        copy.wait()
-    loads = [pltpu.make_async_copy(got.at[t], xs.at[t], local.at[6 + t]) for t in range(2)]
-    for copy in loads:
-        copy.start()
 
     k_cols, v_cols = pl.ds(0, head), pl.ds(head, head)
     second = [
@@ -456,30 +493,31 @@
     for copy in second:
         copy.start()
     for p in order[early:]:
-        kv_copy(2, p, lax.rem(me + p, n)).start()
-
-    for copy in loads:
-        copy.wait()
+        q_copy(p).start()
+
     for t in range(2):
-        total = xs[t, pl.ds(0, blk), :].astype(F32)
-        for p in range(1, n):
-            total += xs[t, pl.ds(p * blk, blk), :].astype(F32)
+        for i in range(3):
+            remote(near_kv.at[t, i], near_kv.at[t, i], send_far.at[t], recv_near.at[t, i], sib).wait_recv()
+        from_relay(t).wait_recv()
+        total = refs[t][rows(me), :].astype(F32) + near_kv[t, 2].astype(F32)
+        total += near_kv[t, 0].astype(F32) + near_kv[t, 1].astype(F32)
+        total += far_kv[t]
         for e, piece in enumerate(split3(total)):
-            parts[t, e] = piece
+            xs[t, pl.ds(e * blk, blk), :] = piece
 
     def kv_part(b, cs):
         total = tile(b)[...]
         for t, w_ref in ((0, wk_ref), (1, wv_ref)):
             w = w_ref[cs, :]
             for e in range(3):
-                total += dot(parts[t, e], w, NT)
+                total += dot(xs[t, pl.ds(e * blk, blk), :], w, NT)
         tile(b)[...] = total
 
     across(kv_part)
 
     def q_part(k):
         p = order[k]
-        kv_copy(2, p, lax.rem(me + p, n)).wait_recv()
+        q_copy(p).wait_recv()
         q_to_vmem(p).start()
         head_to_stage(k).wait()
         q_to_vmem(p).wait()
@@ -520,9 +558,16 @@
         copy.wait_send()
     for g in (gx, gy, gw):
         g.finish()
-    for t in range(3):
-        for p in range(1, n):
-            kv_copy(t, p, lax.rem(me + p, n)).wait_send()
+    for p in range(1, n):
+        q_copy(p).wait_send()
+    for t in range(2):
+        for s in (0, 1):
+            to_relay(t, s).wait_send()
+        for s in (4 - 2 * t, 5 - 2 * t):
+            to_owner(t, s).wait_send()
+        to_sib_relay(t).wait_send()
+        to_sib(t).wait_send()
+        from_relay(t).wait_send()
 
 
 def main_part(x_blk, dy_blk, wq, wk, wv, wo, n, c2, scale, cols):
@@ -541,7 +586,7 @@
             jax.ShapeDtypeStruct((tokens, model), BF16),
             jax.ShapeDtypeStruct((tokens, model), BF16),
             jax.ShapeDtypeStruct((n * head, model), BF16),
-            jax.ShapeDtypeStruct((3, tokens, head), BF16),
+            jax.ShapeDtypeStruct((tokens, head), BF16),
             jax.ShapeDtypeStruct((model, 1, head), F32),
             jax.ShapeDtypeStruct((head, model), F32),
             jax.ShapeDtypeStruct((blk, model), BF16),
@@ -562,12 +607,14 @@
             pltpu.VMEM((2, cols, head), F32),
             pltpu.VMEM((head, model), BF16),
             pltpu.VMEM((2, 3, blk, head), BF16),
+            pltpu.VMEM((2, 3, blk, head), BF16),
+            pltpu.VMEM((2, blk, head), F32),
             pltpu.VMEM((4, part, 2 * head), F32),
             pltpu.VMEM((2, 2, part, head), F32),
             pltpu.VMEM((2, part, head), F32),
         ]
         + Gather.SEMS * 3
-        + [sem((3, n)), sem((3, n)), sem((2,)), sem((8,)), sem((4,)), sem((4,)), sem((2, 2)), sem((2, 2)), sem((2,)),
+        + [sem((n,)), sem((n,)), sem((2, n)), sem((2, 2)), sem((2,)), sem((2, 3)), sem((2, 3)), sem((2,)), sem((2,)), sem((8,)), sem((4,)), sem((4,)), sem((2, 2)), sem((2, 2)), sem((2,)),
            sem((2,))],
         compiler_params=params(collective_id=1, has_side_effects=True),
         cost_estimate=cost(7 * tokens * tokens * head + 14 * tokens * model * head, 8 * tokens * model,

time: 275 us -> 264 us (0.960)
  Pallas kernels: 266 us -> 255 us
    pallas_call x1, Pallas kernels: 266 us -> 255 us  [main_part(): pl.pallas_call(functools.partial(main_body, c2, scale, blk, n, cols), in_...]
where the time goes in v6:
time: 264 us
  Pallas kernels  255 us (97%)
  local copies, waits for them, and re-layouts  8.39 us (3%)
    pallas_call x1, Pallas kernels, main_part(): pl.pallas_call(functools.partial(main_body, c2, scale, blk, n, cols), in_...  255 us
    unnamed x13, local copies, waits for them, and re-layouts  8.39 us

profile of v6, /device:TPU:0, one launch (start us, length us, event | category | flops | bytes accessed | tf_op | source)
XLA Modules:
  0.0 263.8 jit_solution(12600348346384805534)
XLA Ops:
  0.6 254.8 %main.1 = (bf16[4096,2048]{1,0:T(8,128)(2,1)}, bf16[4096,2048]{1,0:T(8,128)(2,1)}, bf16[2048,2048]{1,0:T(8,128)(2,1)}, bf16[4096,256]{1,0:T(8,128)(2,1)}, f32[20...) custom-call(bf16[512,2048]{1,0:T(8,128)(2,1)} %x_ref.1, ...), custom_call_target="tpu_custom_call" | custom-call | flops 60129542144 | bytes 67108864 | tf_op jit(solution)/shard_map/main/pallas_call | solution.py:581
  255.4 0.0 copy-start.1
  255.4 3.3 %copy.16 = bf16[512,2048]{1,0:T(8,128)(2,1)} copy(bf16[512,2048]{1,0:T(8,128)(2,1)} %get-tuple-element.20) | data formatting | bytes 4194304
  258.7 0.0 copy-done.1
  258.7 0.0 copy-start
  258.7 1.3 copy.17
  260.0 1.0 copy-done
  261.1 0.0 copy-start.3
  261.1 0.0 copy-start.2
  261.1 1.3 copy.18
  262.4 0.0 copy-done.3
  262.4 0.7 copy.19
  263.1 0.0 copy-done.2
  263.1 0.7 copy.20
Async XLA Ops:
  255.4 3.3 %copy-start.1 = (f32[2048,1,256]{2,1,0:T(1,128)S(1)}, f32[2048,1,256]{2,1,0:T(1,128)}, u32[]{:S(2)}) copy-start(f32[2048,1,256]{2,1,0:T(1,128)} %get-tuple-element.21) | copy-start | bytes 6291460
  258.7 2.3 copy-start
  261.1 1.3 copy-start.3
  261.1 2.0 copy-start.2

commit v7 on v6

--- a/solution.py
+++ b/solution.py
@@ -109,13 +109,11 @@
             self.copy(self.full.at[self.at(self.me, q), :], self.me, q, slot, self.sib).wait_send()
 
 
-def enter_all(n):
-    me = lax.axis_index("tp")
+def enter(devices):
     barrier = pltpu.get_barrier_semaphore()
-    for p in range(1, n):
-        pl.semaphore_signal(barrier, inc=1, device_id={"tp": lax.rem(me + p, n)}, device_id_type=pl.DeviceIdType.MESH)
-    pl.semaphore_wait(barrier, n - 1)
-    return me
+    for dev in devices:
+        pl.semaphore_signal(barrier, inc=1, device_id={"tp": dev}, device_id_type=pl.DeviceIdType.MESH)
+    pl.semaphore_wait(barrier, len(devices))
 
 
 def remote(src, dst, send, recv, to):
@@ -133,18 +131,19 @@
     return hi, mid, lo
 
 
-def main_body(c2, scale, blk, n, cols, x_ref, dy_ref, wq_ref, wk_ref, wv_ref, wo_ref,
-              x_full, dy_full, wq_all, got, dwq_ref, dwo_ref, dx_ref, dwk_ref, dwv_ref,
+def main_body(c2, scale, blk, n, cols, x_ref, dy_ref, wq_hbm, wk_hbm, wv_hbm, wo_hbm,
+              x_full, dy_full, wq_all, got, dwq_ref, dwo_ref, dx_ref, keep_k, keep_v, pass_k, pass_v,
               q_s, k_s, v_s, do_s, dot_s, ot_s, m_s, rl_s, delta_s, tra, stage, xs, big, acc_s, dk_acc, dv_acc, dwq_s,
-              wqt, rel, near_kv, far_kv, r0, r1, r2,
+              wq_ref, wk_ref, wv_ref, wo_ref, wqt, rel, near_kv, far_kv, r0, r1,
               xsend, xrecv, ysend, yrecv, wsend, wrecv, send_q, recv_q, send_kv, send_sib, send_far, recv_rel, recv_near,
-              recv_far, load, local, s0, e0, s1, e1, s2, e2):
+              recv_far, load, local, s0, e0, s1, e1, wload):
     head = wq_ref.shape[1]
     model = wq_ref.shape[0]
-    me = enter_all(n)
+    me = lax.axis_index("tp")
     gx = Gather(x_ref, x_full, xsend, xrecv)
     gy = Gather(dy_ref, dy_full, ysend, yrecv)
     gw = Gather(wqt, wq_all, wsend, wrecv)
+    enter((gx.xn, gx.yn, gx.sib))
     gx.start()
 
     def rows(j):
@@ -155,7 +154,10 @@
 
     own_x = pltpu.make_async_copy(stage.at[0], x_full.at[rows(me), :], local.at[0])
     into(x_ref, 0).start()
-    wqt[...] = wq_ref[...].T
+    weights_in = [pltpu.make_async_copy(src, dst, wload.at[i]) for i, (src, dst) in enumerate(
+        ((wq_hbm, wq_ref), (wk_hbm, wk_ref), (wv_hbm, wv_ref), (wo_hbm, wo_ref)))]
+    for copy in weights_in:
+        copy.start()
 
     def project(slot, dev):
         x = stage[slot]
@@ -166,6 +168,9 @@
 
     into(x_ref, 0).wait()
     own_x.start()
+    for copy in weights_in:
+        copy.wait()
+    wqt[...] = wq_ref[...].T
     project(0, me)
     gx.from_sib(3)
     into(x_full.at[rows(gx.sib), :], 1).start()
@@ -359,8 +364,11 @@
                 to_sib(0).start()
                 to_sib(1).start()
 
+    def partner(p):
+        return (me, gx.xn, gx.yn, gx.dg)[p // 2] + (p % 2) * gx.flip
+
     def q_copy(p):
-        to = lax.rem(me + p, n)
+        to = partner(p)
         return remote(q_s.at[rows(to), :], got.at[pl.ds(p * blk, blk), :], send_q.at[p], recv_q.at[p], to)
 
     def column(step, _):
@@ -371,12 +379,19 @@
             pair(j, i, False)
             return 0
 
-        lax.fori_loop(j + 1, n, rest, 0)
+        half = (j + 1 + n) // 2
+        lax.fori_loop(j + 1, half, rest, 0)
+
+        @pl.when(step == 0)
+        def _():
+            gw.step(1)
+
+        lax.fori_loop(half, n, rest, 0)
         for e, (ref, grad) in enumerate(((k_s, dk_acc[...] * scale), (v_s, dv_acc[...]))):
             ref[rows(j), :] = grad.astype(BF16)
             tra[pl.ds((e + 1) * head, head), rows(j)] = grad.T.astype(BF16)
 
-        for s, when in ((0, 0), (1, 1), (2, 3), (3, 4)):
+        for s, when in ((2, 3), (3, 4)):
             @pl.when(step == when)
             def _(s=s):
                 gw.step(s)
@@ -388,6 +403,7 @@
 
         return 0
 
+    gw.step(0)
     lax.fori_loop(0, n, column, 0)
     for t, acc in enumerate((dk_acc, dv_acc)):
         for i in range(3):
@@ -405,16 +421,15 @@
     send_block(n - 1)
     from_relay(0).start()
     from_relay(1).start()
-    order = (4, 2, 6, 1, 3, 5, 7)
-    early = 3
-    for p in order[:early]:
+    order = (6, 2, 4, 7, 3, 5, 1)
+    for p in order:
         q_copy(p).start()
     gw.last(0)
     gw.last(1)
 
     def put(b):
         at = pl.ds(pl.multiple_of(b * cols, cols), cols)
-        return pltpu.make_async_copy(dwq_s.at[b % 2], dwq_ref.at[at, 0, :], local.at[4 + b % 2])
+        return pltpu.make_async_copy(dwq_s.at[b % 2], dwq_ref.at[at, :], local.at[4 + b % 2])
 
     def weights(b, _):
         at = pl.ds(pl.multiple_of(b * cols, cols), cols)
@@ -452,8 +467,7 @@
     wide = 2 * cols
 
     def head_to_stage(k):
-        owner = lax.rem(me + n - order[k], n)
-        at = pl.ds(pl.multiple_of(owner * head, head), head)
+        at = pl.ds(pl.multiple_of(partner(order[k]) * head, head), head)
         return pltpu.make_async_copy(wq_all.at[at, :], stage.at[k % 2, pl.ds(0, head), :], load.at[k % 2])
 
     def q_to_vmem(p):
@@ -492,9 +506,6 @@
     ]
     for copy in second:
         copy.start()
-    for p in order[early:]:
-        q_copy(p).start()
-
     for t in range(2):
         for i in range(3):
             remote(near_kv.at[t, i], near_kv.at[t, i], send_far.at[t], recv_near.at[t, i], sib).wait_recv()
@@ -526,39 +537,25 @@
             tile(b)[...] += dot(do_s[pl.ds(p * blk, blk), :], stage[k % 2, pl.ds(0, head), cs])
 
         across(work)
-        if k + 2 < n - 1:
+        if k + 2 < len(order):
             head_to_stage(k + 2).start()
 
-    for k in range(early):
+    for k in range(len(order)):
         q_part(k)
-
-    second[0].wait_recv()
-    r1[0, 1] += r0[2, :, :head]
-    second[1].wait_recv()
-    r1[1, 1] += r0[1, :, head:]
-    q_part(early)
-    third = [
-        remote(r1.at[0, 1], r2.at[0], s2.at[0], e2.at[0], yn),
-        remote(r1.at[1, 1], r2.at[1], s2.at[1], e2.at[1], xn),
-    ]
-    for copy in third:
-        copy.start()
-    for k in range(early + 1, n - 1):
-        q_part(k)
-
     for b in range(model // wide):
         dx_ref[:, pl.ds(b * wide, wide)] = big[pl.ds(b * wide, wide), :].astype(BF16)
-    second[2].wait_recv()
-    second[3].wait_recv()
-    third[0].wait_recv()
-    third[1].wait_recv()
-    dwk_ref[...] = (r0[0, :, :head] + r1[0, 0]) + r2[0]
-    dwv_ref[...] = (r0[0, :, head:] + r1[1, 0]) + r2[1]
-    for copy in first + second + third:
+
+    for copy in second:
+        copy.wait_recv()
+    pass_k[...] = r0[2, :, :head] + r1[0, 1]
+    pass_v[...] = r0[1, :, head:] + r1[1, 1]
+    keep_k[...] = r0[0, :, :head] + r1[0, 0]
+    keep_v[...] = r0[0, :, head:] + r1[1, 0]
+    for copy in first + second:
         copy.wait_send()
     for g in (gx, gy, gw):
         g.finish()
-    for p in range(1, n):
+    for p in order:
         q_copy(p).wait_send()
     for t in range(2):
         for s in (0, 1):
@@ -580,19 +577,17 @@
     sem = pltpu.SemaphoreType.DMA
     return pl.pallas_call(
         functools.partial(main_body, c2, scale, blk, n, cols),
-        in_specs=[hbm] * 2 + [vm] * 4,
-        out_specs=[hbm] * 5 + [vm] * 4,
+        in_specs=[hbm] * 6,
+        out_specs=[hbm] * 5 + [vm] * 6,
         out_shape=[
             jax.ShapeDtypeStruct((tokens, model), BF16),
             jax.ShapeDtypeStruct((tokens, model), BF16),
             jax.ShapeDtypeStruct((n * head, model), BF16),
             jax.ShapeDtypeStruct((tokens, head), BF16),
-            jax.ShapeDtypeStruct((model, 1, head), F32),
+            jax.ShapeDtypeStruct((model, head), F32),
             jax.ShapeDtypeStruct((head, model), F32),
             jax.ShapeDtypeStruct((blk, model), BF16),
-            jax.ShapeDtypeStruct((part, head), F32),
-            jax.ShapeDtypeStruct((part, head), F32),
-        ],
+        ] + [jax.ShapeDtypeStruct((part, head), F32)] * 4,
         scratch_shapes=[pltpu.VMEM((tokens, head), BF16)] * 4
         + [pltpu.VMEM((head, tokens), BF16)] * 2
         + [pltpu.VMEM((1, tokens), F32)] * 3
@@ -605,22 +600,62 @@
             pltpu.VMEM((blk, head), F32),
             pltpu.VMEM((blk, head), F32),
             pltpu.VMEM((2, cols, head), F32),
+            pltpu.VMEM((model, head), BF16),
+            pltpu.VMEM((model, head), BF16),
+            pltpu.VMEM((model, head), BF16),
+            pltpu.VMEM((head, model), BF16),
             pltpu.VMEM((head, model), BF16),
             pltpu.VMEM((2, 3, blk, head), BF16),
             pltpu.VMEM((2, 3, blk, head), BF16),
             pltpu.VMEM((2, blk, head), F32),
             pltpu.VMEM((4, part, 2 * head), F32),
             pltpu.VMEM((2, 2, part, head), F32),
-            pltpu.VMEM((2, part, head), F32),
         ]
         + Gather.SEMS * 3
-        + [sem((n,)), sem((n,)), sem((2, n)), sem((2, 2)), sem((2,)), sem((2, 3)), sem((2, 3)), sem((2,)), sem((2,)), sem((8,)), sem((4,)), sem((4,)), sem((2, 2)), sem((2, 2)), sem((2,)),
-           sem((2,))],
+        + [sem((n,)), sem((n,)), sem((2, n)), sem((2, 2)), sem((2,)), sem((2, 3)), sem((2, 3)), sem((2,)), sem((2,)), sem((8,)), sem((4,)), sem((4,)), sem((2, 2)), sem((2, 2)),
+           sem((4,))],
         compiler_params=params(collective_id=1, has_side_effects=True),
         cost_estimate=cost(7 * tokens * tokens * head + 14 * tokens * model * head, 8 * tokens * model,
                            tokens * tokens),
         name="main",
     )(x_blk, dy_blk, wq, wk, wv, wo)
+
+
+def out_body(pieces, dx_in, dwq_in, dwo_in, dx_out, dwq_out, dwo_out, dx_buf, dwq_buf, dwo_buf, sem_in, sem_out):
+    trips = []
+    for i, (src, buf, dst) in enumerate(((dx_in, dx_buf, dx_out), (dwo_in, dwo_buf, dwo_out),
+                                         (dwq_in, dwq_buf, dwq_out))):
+        size = src.shape[0] // pieces
+        for p in range(pieces):
+            at = pl.ds(p * size, size)
+            there = dst.at[at, 0, :] if dst is dwq_out else dst.at[at, :]
+            trips.append((pltpu.make_async_copy(src.at[at, :], buf.at[at, :], sem_in.at[i, p]),
+                          pltpu.make_async_copy(buf.at[at, :], there, sem_out.at[i, p])))
+    for there, _ in trips:
+        there.start()
+    for there, back in trips:
+        there.wait()
+        back.start()
+    for _, back in trips:
+        back.wait()
+
+
+def write_out(dx, dwq, dwo, pieces=4):
+    hbm = pl.BlockSpec(memory_space=pl.ANY)
+    model, head = dwq.shape
+    arrays = (dx, dwq, dwo)
+    return pl.pallas_call(
+        functools.partial(out_body, pieces),
+        in_specs=[hbm] * 3,
+        out_specs=[hbm] * 3,
+        out_shape=[jax.ShapeDtypeStruct(dx.shape, dx.dtype), jax.ShapeDtypeStruct((model, 1, head), F32),
+                   jax.ShapeDtypeStruct(dwo.shape, F32)],
+        scratch_shapes=[pltpu.VMEM(a.shape, a.dtype) for a in arrays]
+        + [pltpu.SemaphoreType.DMA((3, pieces)), pltpu.SemaphoreType.DMA((3, pieces))],
+        compiler_params=params(),
+        cost_estimate=cost(10e9, 14e6),
+        name="out",
+    )(*arrays)
 
 
 def solution(mesh):
@@ -634,7 +669,12 @@
         wk = w_k.reshape(model, head)
         wv = w_v.reshape(model, head)
         wo = wo_loc.reshape(head, model)
-        *_, dwq, dwo, dx, dwk, dwv = main_part(x_blk, dy_blk, wq, wk, wv, wo, n, c2, scale, 256)
+        *_, dwq, dwo, dx, keep_k, keep_v, pass_k, pass_v = main_part(x_blk, dy_blk, wq, wk, wv, wo, n, c2, scale, 256)
+        over_y = [(i, i + 4 - 8 * (i // 4)) for i in range(n)]
+        over_x = [(i, i + 2 - 4 * ((i // 2) % 2)) for i in range(n)]
+        dx, dwq, dwo = write_out(dx, dwq, dwo)
+        dwk = keep_k + lax.ppermute(pass_k, "tp", over_y)
+        dwv = keep_v + lax.ppermute(pass_v, "tp", over_x)
         return dx, dwq, dwo.reshape(1, head, model), dwk, dwv
 
     tok_spec = P(("dp", "tp"))

time: 264 us -> 256 us (0.970)
  local copies, waits for them, and re-layouts: 8.39 us -> 0.01 us
  Pallas kernels: 255 us -> 252 us
    pallas_call x1, Pallas kernels: 255 us -> 246 us  [main_part(): pl.pallas_call(functools.partial(main_body, c2, scale, blk, n, cols), in_...]
    unnamed x13 -> x4, local copies, waits for them, and re-layouts: 8.39 us -> 0.01 us
    pallas_call x0 -> x1, Pallas kernels: none -> 5.51 us  [write_out(): pl.pallas_call(functools.partial(out_body, pieces), in_specs=[hbm] * 3, o...]
  transfers between devices with their start and end apart: 0 -> 2, of which waited for: 0 -> 0; matrix products, arithmetic and copies ran while one was open for 0% -> 0% of each run, Pallas kernels for 0% -> 2%
where the time goes in v7:
time: 256 us
  Pallas kernels  252 us (98%)
    pallas_call x1, Pallas kernels, main_part(): pl.pallas_call(functools.partial(main_body, c2, scale, blk, n, cols), in_...  246 us
    pallas_call x1, Pallas kernels, write_out(): pl.pallas_call(functools.partial(out_body, pieces), in_specs=[hbm] * 3, o...  5.51 us
  transfers between devices with their start and end apart: 2, of which 0 were waited for; matrix products, arithmetic and copies ran while one was open for 0% of the time, Pallas kernels for 2%

profile of v7, /device:TPU:0, one launch (start us, length us, event | category | flops | bytes accessed | tf_op | source)
XLA Modules:
  0.0 255.8 jit_solution(7644004863442996908)
XLA Ops:
  0.6 246.1 %main.1 = (bf16[4096,2048]{1,0:T(8,128)(2,1)}, bf16[4096,2048]{1,0:T(8,128)(2,1)}, bf16[2048,2048]{1,0:T(8,128)(2,1)}, bf16[4096,256]{1,0:T(8,128)(2,1)}, f32[20...) custom-call(bf16[512,2048]{1,0:T(8,128)(2,1)} %x_ref.1, ...), custom_call_target="tpu_custom_call" | custom-call | flops 60129542144 | bytes 67108864 | tf_op jit(solution)/shard_map/main/pallas_call | solution.py:578
  246.8 1.0 collective-permute-start
  247.8 1.1 collective-permute-start.1
  248.8 0.0 copy-start.1
  248.8 0.0 copy-start
  248.8 5.5 %out.1 = (bf16[512,2048]{1,0:T(8,128)(2,1)}, f32[2048,1,256]{2,1,0:T(1,128)}, f32[256,2048]{1,0:T(8,128)}) custom-call(bf16[512,2048]{1,0:T(8,128)(2,1)} %get-tuple-element.15.dx_in, f32[2048,256]{1,0:T(8,128)} %get-tuple-element.16.dwq_in, f32[256,2048]{1,0:T(8,128)} %get-tuple-element.17.dwo_in), custom_call_target="tpu_custom_call" | custom-call | flops 10000000000 | bytes 14000000 | tf_op jit(solution)/shard_map/out/pallas_call | solution.py:647
  254.3 0.0 collective-permute-done
  254.3 0.0 copy-done.1
  254.4 0.7 add.6
  255.1 0.0 collective-permute-done.1
  255.1 0.0 copy-done
  255.1 0.7 add.7
Async XLA Ops:
  246.8 7.6 %collective-permute-start = (f32[256,256]{1,0:T(8,128)}, f32[256,256]{1,0:T(8,128)S(1)}, u32[]{:S(2)}, u32[]{:S(2)}) collective-permute-start(f32[256,256]{1,0:T(8,128)} %get-tuple-element.22), channel_id=1, source_target_pairs={{0,4},{1,5},{2,6},{3,7},{4,0},{5,1},{6,2},{7,3}} | collective-permute-start | bytes 786440 | tf_op jit(solution)/shard_map/ppermute | solution.py:676
  247.8 7.3 %collective-permute-start.1 = (f32[256,256]{1,0:T(8,128)}, f32[256,256]{1,0:T(8,128)S(1)}, u32[]{:S(2)}, u32[]{:S(2)}) collective-permute-start(f32[256,256]{1,0:T(8,128)} %get-tuple-element.24), channel_id=1, source_target_pairs={{0,2},{1,3},{2,0},{3,1},{4,6},{5,7},{6,4},{7,5}} | collective-permute-start | bytes 786440 | tf_op jit(solution)/shard_map/ppermute | solution.py:677
  248.8 5.5 %copy-start.1 = (f32[256,256]{1,0:T(8,128)S(1)}, f32[256,256]{1,0:T(8,128)}, u32[]{:S(2)}) copy-start(f32[256,256]{1,0:T(8,128)} %get-tuple-element.21) | copy-start | bytes 786436
  248.8 6.3 %copy-start = (f32[256,256]{1,0:T(8,128)S(1)}, f32[256,256]{1,0:T(8,128)}, u32[]{:S(2)}) copy-start(f32[256,256]{1,0:T(8,128)} %get-tuple-element.23) | copy-start | bytes 786436

commit v8 on v7

--- a/solution.py
+++ b/solution.py
@@ -132,11 +132,11 @@
 
 
 def main_body(c2, scale, blk, n, cols, x_ref, dy_ref, wq_hbm, wk_hbm, wv_hbm, wo_hbm,
-              x_full, dy_full, wq_all, got, dwq_ref, dwo_ref, dx_ref, keep_k, keep_v, pass_k, pass_v,
+              x_full, dy_full, wq_all, got, dwq_ref, dwo_hbm, dx_hbm, keep_k, keep_v, pass_k, pass_v,
               q_s, k_s, v_s, do_s, dot_s, ot_s, m_s, rl_s, delta_s, tra, stage, xs, big, acc_s, dk_acc, dv_acc, dwq_s,
-              wq_ref, wk_ref, wv_ref, wo_ref, wqt, rel, near_kv, far_kv, r0, r1,
+              wq_ref, wk_ref, wv_ref, wo_ref, wqt, dwo_s, dx_s, rel, near_kv, far_kv, r0, r1,
               xsend, xrecv, ysend, yrecv, wsend, wrecv, send_q, recv_q, send_kv, send_sib, send_far, recv_rel, recv_near,
-              recv_far, load, local, s0, e0, s1, e1, wload):
+              recv_far, load, local, s0, e0, s1, e1, wload, results):
     head = wq_ref.shape[1]
     model = wq_ref.shape[0]
     me = lax.axis_index("tp")
@@ -260,9 +260,9 @@
         dot_s[:, at] = d_out_t.astype(BF16)
         ot = ot_s[:, at]
         delta_s[:, at] = jnp.sum(d_out_t * ot.astype(F32), axis=0, keepdims=True)
-        dwo_ref[...] += dot(ot, dy)
-
-    dwo_ref[...] = jnp.zeros_like(dwo_ref)
+        dwo_s[...] += dot(ot, dy)
+
+    dwo_s[...] = jnp.zeros_like(dwo_s)
     lax.fori_loop(0, n // 2, attend, 0)
     gy.step(0)
     lax.fori_loop(n // 2, 3 * n // 4, attend, 0)
@@ -284,6 +284,8 @@
     gy.last(0)
     gy.last(1)
     far_pair(gy, dy_full, grad_out)
+    out_wo = pltpu.make_async_copy(dwo_s, dwo_hbm, results.at[0])
+    out_wo.start()
 
     def fetch_x(b):
         at = pl.ds(pl.multiple_of(b * cols, cols), cols)
@@ -543,14 +545,10 @@
     for k in range(len(order)):
         q_part(k)
     for b in range(model // wide):
-        dx_ref[:, pl.ds(b * wide, wide)] = big[pl.ds(b * wide, wide), :].astype(BF16)
-
-    for copy in second:
-        copy.wait_recv()
-    pass_k[...] = r0[2, :, :head] + r1[0, 1]
-    pass_v[...] = r0[1, :, head:] + r1[1, 1]
-    keep_k[...] = r0[0, :, :head] + r1[0, 0]
-    keep_v[...] = r0[0, :, head:] + r1[1, 0]
+        dx_s[:, pl.ds(b * wide, wide)] = big[pl.ds(b * wide, wide), :].astype(BF16)
+    out_x = pltpu.make_async_copy(dx_s, dx_hbm, results.at[1])
+    out_x.start()
+
     for copy in first + second:
         copy.wait_send()
     for g in (gx, gy, gw):
@@ -565,6 +563,14 @@
         to_sib_relay(t).wait_send()
         to_sib(t).wait_send()
         from_relay(t).wait_send()
+    out_wo.wait()
+    out_x.wait()
+    for copy in second:
+        copy.wait_recv()
+    pass_k[...] = r0[2, :, :head] + r1[0, 1]
+    pass_v[...] = r0[1, :, head:] + r1[1, 1]
+    keep_k[...] = r0[0, :, :head] + r1[0, 0]
+    keep_v[...] = r0[0, :, head:] + r1[1, 0]
 
 
 def main_part(x_blk, dy_blk, wq, wk, wv, wo, n, c2, scale, cols):
@@ -578,7 +584,7 @@
     return pl.pallas_call(
         functools.partial(main_body, c2, scale, blk, n, cols),
         in_specs=[hbm] * 6,
-        out_specs=[hbm] * 5 + [vm] * 6,
+        out_specs=[hbm] * 7 + [vm] * 4,
         out_shape=[
             jax.ShapeDtypeStruct((tokens, model), BF16),
             jax.ShapeDtypeStruct((tokens, model), BF16),
@@ -605,6 +611,8 @@
             pltpu.VMEM((model, head), BF16),
             pltpu.VMEM((head, model), BF16),
             pltpu.VMEM((head, model), BF16),
+            pltpu.VMEM((head, model), F32),
+            pltpu.VMEM((blk, model), BF16),
             pltpu.VMEM((2, 3, blk, head), BF16),
             pltpu.VMEM((2, 3, blk, head), BF16),
             pltpu.VMEM((2, blk, head), F32),
@@ -613,7 +621,7 @@
         ]
         + Gather.SEMS * 3
         + [sem((n,)), sem((n,)), sem((2, n)), sem((2, 2)), sem((2,)), sem((2, 3)), sem((2, 3)), sem((2,)), sem((2,)), sem((8,)), sem((4,)), sem((4,)), sem((2, 2)), sem((2, 2)),
-           sem((4,))],
+           sem((4,)), sem((2,))],
         compiler_params=params(collective_id=1, has_side_effects=True),
         cost_estimate=cost(7 * tokens * tokens * head + 14 * tokens * model * head, 8 * tokens * model,
                            tokens * tokens),

time: 256 us -> 255 us (level)
  no operation moved by 1% of the time
where the time goes in v8:
time: 255 us; the launch traced here: 254 us
  Pallas kernels  250 us (98%)
    pallas_call x1, Pallas kernels, main_part(): pl.pallas_call(functools.partial(main_body, c2, scale, blk, n, cols), in_...  245 us
    pallas_call x1, Pallas kernels, write_out(): pl.pallas_call(functools.partial(out_body, pieces), in_specs=[hbm] * 3, o...  5.51 us
  transfers between devices with their start and end apart: 2, of which 0 were waited for; matrix products, arithmetic and copies ran while one was open for 0% of the time, Pallas kernels for 2%

profile of v8, /device:TPU:0, one launch (start us, length us, event | category | flops | bytes accessed | tf_op | source)
XLA Modules:
  0.0 254.2 jit_solution(12296750369621570166)
XLA Ops:
  0.6 244.5 %main.1 = (bf16[4096,2048]{1,0:T(8,128)(2,1)}, bf16[4096,2048]{1,0:T(8,128)(2,1)}, bf16[2048,2048]{1,0:T(8,128)(2,1)}, bf16[4096,256]{1,0:T(8,128)(2,1)}, f32[20...) custom-call(bf16[512,2048]{1,0:T(8,128)(2,1)} %x_ref.1, ...), custom_call_target="tpu_custom_call" | custom-call | flops 60129542144 | bytes 67108864 | tf_op jit(solution)/shard_map/main/pallas_call | solution.py:584
  245.2 1.0 collective-permute-start
  246.1 1.1 collective-permute-start.1
  247.2 0.0 copy-start.1
  247.2 0.0 copy-start
  247.2 5.5 %out.1 = (bf16[512,2048]{1,0:T(8,128)(2,1)}, f32[2048,1,256]{2,1,0:T(1,128)}, f32[256,2048]{1,0:T(8,128)}) custom-call(bf16[512,2048]{1,0:T(8,128)(2,1)} %get-tuple-element.15.dx_in, f32[2048,256]{1,0:T(8,128)} %get-tuple-element.16.dwq_in, f32[256,2048]{1,0:T(8,128)} %get-tuple-element.17.dwo_in), custom_call_target="tpu_custom_call" | custom-call | flops 10000000000 | bytes 14000000 | tf_op jit(solution)/shard_map/out/pallas_call | solution.py:655
  252.7 0.0 collective-permute-done
  252.7 0.0 copy-done.1
  252.7 0.7 add.6
  253.5 0.0 collective-permute-done.1
  253.5 0.0 copy-done
  253.5 0.7 add.7
Async XLA Ops:
  245.2 7.6 %collective-permute-start = (f32[256,256]{1,0:T(8,128)}, f32[256,256]{1,0:T(8,128)S(1)}, u32[]{:S(2)}, u32[]{:S(2)}) collective-permute-start(f32[256,256]{1,0:T(8,128)} %get-tuple-element.22), channel_id=1, source_target_pairs={{0,4},{1,5},{2,6},{3,7},{4,0},{5,1},{6,2},{7,3}} | collective-permute-start | bytes 786440 | tf_op jit(solution)/shard_map/ppermute | solution.py:684
  246.1 7.3 %collective-permute-start.1 = (f32[256,256]{1,0:T(8,128)}, f32[256,256]{1,0:T(8,128)S(1)}, u32[]{:S(2)}, u32[]{:S(2)}) collective-permute-start(f32[256,256]{1,0:T(8,128)} %get-tuple-element.24), channel_id=1, source_target_pairs={{0,2},{1,3},{2,0},{3,1},{4,6},{5,7},{6,4},{7,5}} | collective-permute-start | bytes 786440 | tf_op jit(solution)/shard_map/ppermute | solution.py:685
  247.2 5.5 %copy-start.1 = (f32[256,256]{1,0:T(8,128)S(1)}, f32[256,256]{1,0:T(8,128)}, u32[]{:S(2)}) copy-start(f32[256,256]{1,0:T(8,128)} %get-tuple-element.21) | copy-start | bytes 786436
  247.2 6.3 %copy-start = (f32[256,256]{1,0:T(8,128)S(1)}, f32[256,256]{1,0:T(8,128)}, u32[]{:S(2)}) copy-start(f32[256,256]{1,0:T(8,128)} %get-tuple-element.23) | copy-start | bytes 786436

commit v9 on v8

--- a/solution.py
+++ b/solution.py
@@ -220,12 +220,12 @@
         qt = tra[pl.ds(0, head), rows(i)]
 
         def score(j, m):
-            s = dot(k_s[rows(j), :], qt) * c2
+            s = dot(k_s[rows(j), :], qt)
             big[rows(j), :] = s
             return jnp.maximum(m, jnp.max(s, axis=0, keepdims=True))
 
         m = lax.fori_loop(0, i, score, jnp.full((1, blk), -jnp.inf, F32))
-        s = dot(k_s[rows(i), :], qt) * c2
+        s = dot(k_s[rows(i), :], qt)
         key = lax.broadcasted_iota(jnp.int32, (blk, blk), 0)
         qry = lax.broadcasted_iota(jnp.int32, (blk, blk), 1)
         s = jnp.where(key <= qry, s, -jnp.inf)
@@ -233,7 +233,7 @@
         m = jnp.maximum(m, jnp.max(s, axis=0, keepdims=True))
 
         def expo(j, l):
-            p = jnp.exp2(big[rows(j), :] - m)
+            p = jnp.exp2((big[rows(j), :] - m) * c2)
             big[rows(j), :] = p
             return l + jnp.sum(p, axis=0, keepdims=True)
 
@@ -303,7 +303,7 @@
         at_k = rows(j)
         at_q = rows(i)
         s = dot(k_s[at_k, :], tra[pl.ds(0, head), at_q])
-        p = jnp.exp2(s * c2 - m_s[:, at_q]) * rl_s[:, at_q]
+        p = jnp.exp2((s - m_s[:, at_q]) * c2) * rl_s[:, at_q]
         if masked:
             key = lax.broadcasted_iota(jnp.int32, (blk, blk), 0)
             qry = lax.broadcasted_iota(jnp.int32, (blk, blk), 1)

time: 255 us -> 255 us (level)
  no operation moved by 1% of the time
where the time goes in v9:
time: 255 us; the launch traced here: 254 us
  Pallas kernels  250 us (98%)
    pallas_call x1, Pallas kernels, main_part(): pl.pallas_call(functools.partial(main_body, c2, scale, blk, n, cols), in_...  245 us
    pallas_call x1, Pallas kernels, write_out(): pl.pallas_call(functools.partial(out_body, pieces), in_specs=[hbm] * 3, o...  5.51 us
  transfers between devices with their start and end apart: 2, of which 0 were waited for; matrix products, arithmetic and copies ran while one was open for 0% of the time, Pallas kernels for 2%

profile of v9, /device:TPU:0, one launch (start us, length us, event | category | flops | bytes accessed | tf_op | source)
XLA Modules:
  0.0 254.2 jit_solution(4451504098482898107)
XLA Ops:
  0.6 244.5 %main.1 = (bf16[4096,2048]{1,0:T(8,128)(2,1)}, bf16[4096,2048]{1,0:T(8,128)(2,1)}, bf16[2048,2048]{1,0:T(8,128)(2,1)}, bf16[4096,256]{1,0:T(8,128)(2,1)}, f32[20...) custom-call(bf16[512,2048]{1,0:T(8,128)(2,1)} %x_ref.1, ...), custom_call_target="tpu_custom_call" | custom-call | flops 60129542144 | bytes 67108864 | tf_op jit(solution)/shard_map/main/pallas_call | solution.py:584
  245.2 1.0 collective-permute-start
  246.1 1.1 collective-permute-start.1
  247.2 0.0 copy-start.1
  247.2 0.0 copy-start
  247.2 5.5 %out.1 = (bf16[512,2048]{1,0:T(8,128)(2,1)}, f32[2048,1,256]{2,1,0:T(1,128)}, f32[256,2048]{1,0:T(8,128)}) custom-call(bf16[512,2048]{1,0:T(8,128)(2,1)} %get-tuple-element.15.dx_in, f32[2048,256]{1,0:T(8,128)} %get-tuple-element.16.dwq_in, f32[256,2048]{1,0:T(8,128)} %get-tuple-element.17.dwo_in), custom_call_target="tpu_custom_call" | custom-call | flops 10000000000 | bytes 14000000 | tf_op jit(solution)/shard_map/out/pallas_call | solution.py:655
  252.7 0.0 collective-permute-done
  252.7 0.0 copy-done.1
  252.7 0.7 add.6
  253.5 0.0 collective-permute-done.1
  253.5 0.0 copy-done
  253.5 0.7 add.7
Async XLA Ops:
  245.2 7.6 %collective-permute-start = (f32[256,256]{1,0:T(8,128)}, f32[256,256]{1,0:T(8,128)S(1)}, u32[]{:S(2)}, u32[]{:S(2)}) collective-permute-start(f32[256,256]{1,0:T(8,128)} %get-tuple-element.22), channel_id=1, source_target_pairs={{0,4},{1,5},{2,6},{3,7},{4,0},{5,1},{6,2},{7,3}} | collective-permute-start | bytes 786440 | tf_op jit(solution)/shard_map/ppermute | solution.py:684
  246.1 7.3 %collective-permute-start.1 = (f32[256,256]{1,0:T(8,128)}, f32[256,256]{1,0:T(8,128)S(1)}, u32[]{:S(2)}, u32[]{:S(2)}) collective-permute-start(f32[256,256]{1,0:T(8,128)} %get-tuple-element.24), channel_id=1, source_target_pairs={{0,2},{1,3},{2,0},{3,1},{4,6},{5,7},{6,4},{7,5}} | collective-permute-start | bytes 786440 | tf_op jit(solution)/shard_map/ppermute | solution.py:685
  247.2 5.5 %copy-start.1 = (f32[256,256]{1,0:T(8,128)S(1)}, f32[256,256]{1,0:T(8,128)}, u32[]{:S(2)}) copy-start(f32[256,256]{1,0:T(8,128)} %get-tuple-element.21) | copy-start | bytes 786436
  247.2 6.3 %copy-start = (f32[256,256]{1,0:T(8,128)S(1)}, f32[256,256]{1,0:T(8,128)}, u32[]{:S(2)}) copy-start(f32[256,256]{1,0:T(8,128)} %get-tuple-element.23) | copy-start | bytes 786436

commit v10 on v9

--- a/solution.py
+++ b/solution.py
@@ -424,10 +424,10 @@
     from_relay(0).start()
     from_relay(1).start()
     order = (6, 2, 4, 7, 3, 5, 1)
+    gw.last(0)
+    gw.last(1)
     for p in order:
         q_copy(p).start()
-    gw.last(0)
-    gw.last(1)
 
     def put(b):
         at = pl.ds(pl.multiple_of(b * cols, cols), cols)
@@ -506,8 +506,6 @@
         remote(r0.at[1, :, k_cols], r1.at[0, 0], s1.at[0, 0], e1.at[0, 0], xn),
         remote(r0.at[2, :, v_cols], r1.at[1, 0], s1.at[1, 0], e1.at[1, 0], yn),
     ]
-    for copy in second:
-        copy.start()
     for t in range(2):
         for i in range(3):
             remote(near_kv.at[t, i], near_kv.at[t, i], send_far.at[t], recv_near.at[t, i], sib).wait_recv()
@@ -517,6 +515,8 @@
         total += far_kv[t]
         for e, piece in enumerate(split3(total)):
             xs[t, pl.ds(e * blk, blk), :] = piece
+    for copy in second:
+        copy.start()
 
     def kv_part(b, cs):
         total = tile(b)[...]

time: 255 us -> 255 us (level)
  no operation moved by 1% of the time
where the time goes in v10:
time: 255 us; the launch traced here: 254 us
  Pallas kernels  250 us (98%)
    pallas_call x1, Pallas kernels, main_part(): pl.pallas_call(functools.partial(main_body, c2, scale, blk, n, cols), in_...  245 us
    pallas_call x1, Pallas kernels, write_out(): pl.pallas_call(functools.partial(out_body, pieces), in_specs=[hbm] * 3, o...  5.51 us
  transfers between devices with their start and end apart: 2, of which 0 were waited for; matrix products, arithmetic and copies ran while one was open for 0% of the time, Pallas kernels for 2%

profile of v10, /device:TPU:0, one launch (start us, length us, event | category | flops | bytes accessed | tf_op | source)
XLA Modules:
  0.0 254.2 jit_solution(352424748861162828)
XLA Ops:
  0.6 244.5 %main.1 = (bf16[4096,2048]{1,0:T(8,128)(2,1)}, bf16[4096,2048]{1,0:T(8,128)(2,1)}, bf16[2048,2048]{1,0:T(8,128)(2,1)}, bf16[4096,256]{1,0:T(8,128)(2,1)}, f32[20...) custom-call(bf16[512,2048]{1,0:T(8,128)(2,1)} %x_ref.1, ...), custom_call_target="tpu_custom_call" | custom-call | flops 60129542144 | bytes 67108864 | tf_op jit(solution)/shard_map/main/pallas_call | solution.py:584
  245.2 1.0 collective-permute-start
  246.1 1.1 collective-permute-start.1
  247.2 0.0 copy-start.1
  247.2 0.0 copy-start
  247.2 5.5 %out.1 = (bf16[512,2048]{1,0:T(8,128)(2,1)}, f32[2048,1,256]{2,1,0:T(1,128)}, f32[256,2048]{1,0:T(8,128)}) custom-call(bf16[512,2048]{1,0:T(8,128)(2,1)} %get-tuple-element.15.dx_in, f32[2048,256]{1,0:T(8,128)} %get-tuple-element.16.dwq_in, f32[256,2048]{1,0:T(8,128)} %get-tuple-element.17.dwo_in), custom_call_target="tpu_custom_call" | custom-call | flops 10000000000 | bytes 14000000 | tf_op jit(solution)/shard_map/out/pallas_call | solution.py:655
  252.7 0.0 collective-permute-done
  252.7 0.0 copy-done.1
  252.7 0.7 add.6
  253.5 0.0 collective-permute-done.1
  253.5 0.0 copy-done
  253.5 0.7 add.7
Async XLA Ops:
  245.2 7.6 %collective-permute-start = (f32[256,256]{1,0:T(8,128)}, f32[256,256]{1,0:T(8,128)S(1)}, u32[]{:S(2)}, u32[]{:S(2)}) collective-permute-start(f32[256,256]{1,0:T(8,128)} %get-tuple-element.22), channel_id=1, source_target_pairs={{0,4},{1,5},{2,6},{3,7},{4,0},{5,1},{6,2},{7,3}} | collective-permute-start | bytes 786440 | tf_op jit(solution)/shard_map/ppermute | solution.py:684
  246.1 7.3 %collective-permute-start.1 = (f32[256,256]{1,0:T(8,128)}, f32[256,256]{1,0:T(8,128)S(1)}, u32[]{:S(2)}, u32[]{:S(2)}) collective-permute-start(f32[256,256]{1,0:T(8,128)} %get-tuple-element.24), channel_id=1, source_target_pairs={{0,2},{1,3},{2,0},{3,1},{4,6},{5,7},{6,4},{7,5}} | collective-permute-start | bytes 786440 | tf_op jit(solution)/shard_map/ppermute | solution.py:685
  247.2 5.5 %copy-start.1 = (f32[256,256]{1,0:T(8,128)S(1)}, f32[256,256]{1,0:T(8,128)}, u32[]{:S(2)}) copy-start(f32[256,256]{1,0:T(8,128)} %get-tuple-element.21) | copy-start | bytes 786436
  247.2 6.3 %copy-start = (f32[256,256]{1,0:T(8,128)S(1)}, f32[256,256]{1,0:T(8,128)}, u32[]{:S(2)}) copy-start(f32[256,256]{1,0:T(8,128)} %get-tuple-element.23) | copy-start | bytes 786436

commit v11 on v10

--- a/solution.py
+++ b/solution.py
@@ -136,7 +136,7 @@
               q_s, k_s, v_s, do_s, dot_s, ot_s, m_s, rl_s, delta_s, tra, stage, xs, big, acc_s, dk_acc, dv_acc, dwq_s,
               wq_ref, wk_ref, wv_ref, wo_ref, wqt, dwo_s, dx_s, rel, near_kv, far_kv, r0, r1,
               xsend, xrecv, ysend, yrecv, wsend, wrecv, send_q, recv_q, send_kv, send_sib, send_far, recv_rel, recv_near,
-              recv_far, load, local, s0, e0, s1, e1, wload, results):
+              recv_far, load, local, s0, e0, s1, e1, wload, results, passing):
     head = wq_ref.shape[1]
     model = wq_ref.shape[0]
     me = lax.axis_index("tp")
@@ -549,7 +549,16 @@
     out_x = pltpu.make_async_copy(dx_s, dx_hbm, results.at[1])
     out_x.start()
 
-    for copy in first + second:
+    second[0].wait_recv()
+    r1[0, 1] += r0[2, :, :head]
+    second[1].wait_recv()
+    r1[1, 1] += r0[1, :, head:]
+    for copy in first:
+        copy.wait_send()
+    passed = [pltpu.make_async_copy(r1.at[t, 1], ref, passing.at[t]) for t, ref in enumerate((pass_k, pass_v))]
+    for copy in passed:
+        copy.start()
+    for copy in second:
         copy.wait_send()
     for g in (gx, gy, gw):
         g.finish()
@@ -565,12 +574,12 @@
         from_relay(t).wait_send()
     out_wo.wait()
     out_x.wait()
-    for copy in second:
-        copy.wait_recv()
-    pass_k[...] = r0[2, :, :head] + r1[0, 1]
-    pass_v[...] = r0[1, :, head:] + r1[1, 1]
+    second[2].wait_recv()
     keep_k[...] = r0[0, :, :head] + r1[0, 0]
+    second[3].wait_recv()
     keep_v[...] = r0[0, :, head:] + r1[1, 0]
+    for copy in passed:
+        copy.wait()
 
 
 def main_part(x_blk, dy_blk, wq, wk, wv, wo, n, c2, scale, cols):
@@ -584,7 +593,7 @@
     return pl.pallas_call(
         functools.partial(main_body, c2, scale, blk, n, cols),
         in_specs=[hbm] * 6,
-        out_specs=[hbm] * 7 + [vm] * 4,
+        out_specs=[hbm] * 7 + [vm] * 2 + [hbm] * 2,
         out_shape=[
             jax.ShapeDtypeStruct((tokens, model), BF16),
             jax.ShapeDtypeStruct((tokens, model), BF16),
@@ -621,7 +630,7 @@
         ]
         + Gather.SEMS * 3
         + [sem((n,)), sem((n,)), sem((2, n)), sem((2, 2)), sem((2,)), sem((2, 3)), sem((2, 3)), sem((2,)), sem((2,)), sem((8,)), sem((4,)), sem((4,)), sem((2, 2)), sem((2, 2)),
-           sem((4,)), sem((2,))],
+           sem((4,)), sem((2,)), sem((2,))],
         compiler_params=params(collective_id=1, has_side_effects=True),
         cost_estimate=cost(7 * tokens * tokens * head + 14 * tokens * model * head, 8 * tokens * model,
                            tokens * tokens),

time: 255 us -> 254 us (level)
  no operation moved by 1% of the time
where the time goes in v11:
time: 254 us
  Pallas kernels  250 us (98%)
    pallas_call x1, Pallas kernels, main_part(): pl.pallas_call(functools.partial(main_body, c2, scale, blk, n, cols), in_...  244 us
    pallas_call x1, Pallas kernels, write_out(): pl.pallas_call(functools.partial(out_body, pieces), in_specs=[hbm] * 3, o...  5.51 us
  transfers between devices with their start and end apart: 2, of which 0 were waited for; matrix products, arithmetic and copies ran while one was open for 0% of the time, Pallas kernels for 2%

profile of v11, /device:TPU:0, one launch (start us, length us, event | category | flops | bytes accessed | tf_op | source)
XLA Modules:
  0.0 254.1 jit_solution(10429201671443986403)
XLA Ops:
  0.6 244.4 %main.1 = (bf16[4096,2048]{1,0:T(8,128)(2,1)}, bf16[4096,2048]{1,0:T(8,128)(2,1)}, bf16[2048,2048]{1,0:T(8,128)(2,1)}, bf16[4096,256]{1,0:T(8,128)(2,1)}, f32[20...) custom-call(bf16[512,2048]{1,0:T(8,128)(2,1)} %x_ref.1, ...), custom_call_target="tpu_custom_call" | custom-call | flops 60129542144 | bytes 67108864 | tf_op jit(solution)/shard_map/main/pallas_call | solution.py:593
  245.0 1.0 collective-permute-start
  246.0 1.1 collective-permute-start.1
  247.1 0.0 copy-start.1
  247.1 0.0 copy-start
  247.1 5.5 %out.1 = (bf16[512,2048]{1,0:T(8,128)(2,1)}, f32[2048,1,256]{2,1,0:T(1,128)}, f32[256,2048]{1,0:T(8,128)}) custom-call(bf16[512,2048]{1,0:T(8,128)(2,1)} %get-tuple-element.15.dx_in, f32[2048,256]{1,0:T(8,128)} %get-tuple-element.16.dwq_in, f32[256,2048]{1,0:T(8,128)} %get-tuple-element.17.dwo_in), custom_call_target="tpu_custom_call" | custom-call | flops 10000000000 | bytes 14000000 | tf_op jit(solution)/shard_map/out/pallas_call | solution.py:664
  252.6 0.0 collective-permute-done
  252.6 0.0 copy-done.1
  252.6 0.7 add.6
  253.4 0.0 collective-permute-done.1
  253.4 0.0 copy-done
  253.4 0.7 add.7
Async XLA Ops:
  245.0 7.6 %collective-permute-start = (f32[256,256]{1,0:T(8,128)}, f32[256,256]{1,0:T(8,128)S(1)}, u32[]{:S(2)}, u32[]{:S(2)}) collective-permute-start(f32[256,256]{1,0:T(8,128)} %get-tuple-element.22), channel_id=1, source_target_pairs={{0,4},{1,5},{2,6},{3,7},{4,0},{5,1},{6,2},{7,3}} | collective-permute-start | bytes 786440 | tf_op jit(solution)/shard_map/ppermute | solution.py:693
  246.0 7.3 %collective-permute-start.1 = (f32[256,256]{1,0:T(8,128)}, f32[256,256]{1,0:T(8,128)S(1)}, u32[]{:S(2)}, u32[]{:S(2)}) collective-permute-start(f32[256,256]{1,0:T(8,128)} %get-tuple-element.24), channel_id=1, source_target_pairs={{0,2},{1,3},{2,0},{3,1},{4,6},{5,7},{6,4},{7,5}} | collective-permute-start | bytes 786440 | tf_op jit(solution)/shard_map/ppermute | solution.py:694
  247.1 5.5 %copy-start.1 = (f32[256,256]{1,0:T(8,128)S(1)}, f32[256,256]{1,0:T(8,128)}, u32[]{:S(2)}) copy-start(f32[256,256]{1,0:T(8,128)} %get-tuple-element.21) | copy-start | bytes 786436
  247.1 6.3 %copy-start = (f32[256,256]{1,0:T(8,128)S(1)}, f32[256,256]{1,0:T(8,128)}, u32[]{:S(2)}) copy-start(f32[256,256]{1,0:T(8,128)} %get-tuple-element.23) | copy-start | bytes 786436

commit v12 on v11

--- a/solution.py
+++ b/solution.py
@@ -574,11 +574,12 @@
         from_relay(t).wait_send()
     out_wo.wait()
     out_x.wait()
-    second[2].wait_recv()
-    keep_k[...] = r0[0, :, :head] + r1[0, 0]
-    second[3].wait_recv()
-    keep_v[...] = r0[0, :, head:] + r1[1, 0]
-    for copy in passed:
+    kept = [pltpu.make_async_copy(r1.at[t, 0], ref, passing.at[2 + t]) for t, ref in enumerate((keep_k, keep_v))]
+    for t, cols_t in enumerate((k_cols, v_cols)):
+        second[2 + t].wait_recv()
+        r1[t, 0] += r0[0, :, cols_t]
+        kept[t].start()
+    for copy in passed + kept:
         copy.wait()
 
 
@@ -593,7 +594,7 @@
     return pl.pallas_call(
         functools.partial(main_body, c2, scale, blk, n, cols),
         in_specs=[hbm] * 6,
-        out_specs=[hbm] * 7 + [vm] * 2 + [hbm] * 2,
+        out_specs=[hbm] * 11,
         out_shape=[
             jax.ShapeDtypeStruct((tokens, model), BF16),
             jax.ShapeDtypeStruct((tokens, model), BF16),
@@ -630,7 +631,7 @@
         ]
         + Gather.SEMS * 3
         + [sem((n,)), sem((n,)), sem((2, n)), sem((2, 2)), sem((2,)), sem((2, 3)), sem((2, 3)), sem((2,)), sem((2,)), sem((8,)), sem((4,)), sem((4,)), sem((2, 2)), sem((2, 2)),
-           sem((4,)), sem((2,)), sem((2,))],
+           sem((4,)), sem((2,)), sem((4,))],
         compiler_params=params(collective_id=1, has_side_effects=True),
         cost_estimate=cost(7 * tokens * tokens * head + 14 * tokens * model * head, 8 * tokens * model,
                            tokens * tokens),

time: 254 us -> 254 us (level)
  no operation moved by 1% of the time
where the time goes in v12:
time: 254 us
  Pallas kernels  250 us (98%)
    pallas_call x1, Pallas kernels, main_part(): pl.pallas_call(functools.partial(main_body, c2, scale, blk, n, cols), in_...  244 us
    pallas_call x1, Pallas kernels, write_out(): pl.pallas_call(functools.partial(out_body, pieces), in_specs=[hbm] * 3, o...  5.51 us
  transfers between devices with their start and end apart: 2, of which 0 were waited for; matrix products, arithmetic and copies ran while one was open for 0% of the time, Pallas kernels for 2%

profile of v12, /device:TPU:0, one launch (start us, length us, event | category | flops | bytes accessed | tf_op | source)
XLA Modules:
  0.0 254.1 jit_solution(4975003682007376748)
XLA Ops:
  0.6 244.4 %main.1 = (bf16[4096,2048]{1,0:T(8,128)(2,1)}, bf16[4096,2048]{1,0:T(8,128)(2,1)}, bf16[2048,2048]{1,0:T(8,128)(2,1)}, bf16[4096,256]{1,0:T(8,128)(2,1)}, f32[20...) custom-call(bf16[512,2048]{1,0:T(8,128)(2,1)} %x_ref.1, ...), custom_call_target="tpu_custom_call" | custom-call | flops 60129542144 | bytes 67108864 | tf_op jit(solution)/shard_map/main/pallas_call | solution.py:594
  245.0 1.0 collective-permute-start
  246.0 1.1 collective-permute-start.1
  247.1 0.0 copy-start.1
  247.1 0.0 copy-start
  247.1 5.5 %out.1 = (bf16[512,2048]{1,0:T(8,128)(2,1)}, f32[2048,1,256]{2,1,0:T(1,128)}, f32[256,2048]{1,0:T(8,128)}) custom-call(bf16[512,2048]{1,0:T(8,128)(2,1)} %get-tuple-element.15.dx_in, f32[2048,256]{1,0:T(8,128)} %get-tuple-element.16.dwq_in, f32[256,2048]{1,0:T(8,128)} %get-tuple-element.17.dwo_in), custom_call_target="tpu_custom_call" | custom-call | flops 10000000000 | bytes 14000000 | tf_op jit(solution)/shard_map/out/pallas_call | solution.py:665
  252.6 0.0 collective-permute-done
  252.6 0.0 copy-done.1
  252.6 0.7 add.6
  253.4 0.0 collective-permute-done.1
  253.4 0.0 copy-done
  253.4 0.7 add.7
Async XLA Ops:
  245.0 7.6 %collective-permute-start = (f32[256,256]{1,0:T(8,128)}, f32[256,256]{1,0:T(8,128)S(1)}, u32[]{:S(2)}, u32[]{:S(2)}) collective-permute-start(f32[256,256]{1,0:T(8,128)} %get-tuple-element.22), channel_id=1, source_target_pairs={{0,4},{1,5},{2,6},{3,7},{4,0},{5,1},{6,2},{7,3}} | collective-permute-start | bytes 786440 | tf_op jit(solution)/shard_map/ppermute | solution.py:694
  246.0 7.3 %collective-permute-start.1 = (f32[256,256]{1,0:T(8,128)}, f32[256,256]{1,0:T(8,128)S(1)}, u32[]{:S(2)}, u32[]{:S(2)}) collective-permute-start(f32[256,256]{1,0:T(8,128)} %get-tuple-element.24), channel_id=1, source_target_pairs={{0,2},{1,3},{2,0},{3,1},{4,6},{5,7},{6,4},{7,5}} | collective-permute-start | bytes 786440 | tf_op jit(solution)/shard_map/ppermute | solution.py:695
  247.1 5.5 %copy-start.1 = (f32[256,256]{1,0:T(8,128)S(1)}, f32[256,256]{1,0:T(8,128)}, u32[]{:S(2)}) copy-start(f32[256,256]{1,0:T(8,128)} %get-tuple-element.21) | copy-start | bytes 786436
  247.1 6.3 %copy-start = (f32[256,256]{1,0:T(8,128)S(1)}, f32[256,256]{1,0:T(8,128)}, u32[]{:S(2)}) copy-start(f32[256,256]{1,0:T(8,128)} %get-tuple-element.23) | copy-start | bytes 786436
